TPU v7x, 256 devices: a whole 4x4x8 slice. The times are simulated.
256 devices in a mesh: tm: 32 (over z_hi, x, core), space: 8 (over y, z_lo).
Axes of the slice: x: 4, y: 4, z: 8 (z_hi: 4, z_lo: 2; z = z_hi * 2 + z_lo), core: 2. Of those that a mesh axis runs over, the one named last changes fastest.
Arguments:
- fine_nodes: float32 [32, 3, 3, 128, 4096], P('tm', None, None, 'space'), may hold values from -6 to 6
- init_state: float32 [3, 128, 4096], P(None, 'space'), may hold values from -6 to 6
- mean_depth: float32 [128, 4096], P('space'), may hold values from 0.5 to 2
Outputs:
- new_nodes: float32 [32, 3, 3, 128, 4096], P('tm', None, None, 'space')
All inputs are finite; a program needn't handle non-finite values.
Results may differ from a plain program's by a relative error of at most 0.00002.
Values sent between devices are 32-bit elements; how exact they have to be, the bound alone decides.
A program may use at most 64 MiB of HBM per device.

v0:
```python
import jax
import jax.numpy as jnp
from jax import lax
from jax.sharding import PartitionSpec as P

step_size = 0.3
viscosity = 1.0 / 3.0
coriolis = 0.5
quad_near = 5.0 / 24.0
quad_mid = 1.0 / 3.0
quad_far = -1.0 / 24.0


def from_behind(value, axis, by):
    peers = lax.axis_size(axis)
    pairs = [(i, i + by) for i in range(peers) if 0 <= i + by < peers]
    return lax.ppermute(value, axis, pairs)


def extended(cells, sides, width):
    for axis, dim in sides:
        count = lax.axis_size(axis)
        head = lax.slice_in_dim(cells, 0, width, axis=dim)
        tail = lax.slice_in_dim(cells, cells.shape[dim] - width, cells.shape[dim], axis=dim)
        cells = jnp.concatenate(
            [
                lax.ppermute(tail, axis, [(i, (i + 1) % count) for i in range(count)]),
                cells,
                lax.ppermute(head, axis, [((i + 1) % count, i) for i in range(count)]),
            ],
            axis=dim,
        )
    return cells


def column_slope(values):
    return (jnp.roll(values, -1, -1) - jnp.roll(values, 1, -1)) * 0.5


def row_slope(values):
    return (values[..., 2:, :] - values[..., :-2, :]) * 0.5


def diffuse(values, centre):
    return (
        values[..., 2:, :]
        + values[..., :-2, :]
        + jnp.roll(centre, -1, -1)
        + jnp.roll(centre, 1, -1)
        - 4.0 * centre
    )


def tendency(padded, depth_rows):
    height = padded[..., 0, :, :]
    east_flow = padded[..., 1, :, :]
    north_flow = padded[..., 2, :, :]
    centre = padded[..., 1:-1, :]
    height_c = centre[..., 0, :, :]
    east_c = centre[..., 1, :, :]
    north_c = centre[..., 2, :, :]
    depth_c = depth_rows[1:-1]
    height_rate = (
        -column_slope(depth_c * east_c)
        - row_slope(depth_rows * north_flow)
        + viscosity * diffuse(height, height_c)
    )
    east_rate = (
        -column_slope(height_c) + coriolis * north_c + viscosity * diffuse(east_flow, east_c)
    )
    north_rate = -row_slope(height) - coriolis * east_c + viscosity * diffuse(north_flow, north_c)
    return jnp.stack([height_rate, east_rate, north_rate], axis=-3)


def per_device(fine_nodes, init_state, mean_depth):
    points = fine_nodes[0]
    row_count = points.shape[-2]
    col_count = points.shape[-1]
    half_step = step_size * 0.5
    is_first = lax.axis_index("tm") == 0
    previous = from_behind(points[2], "tm", 1)
    section_zero = jnp.where(is_first, init_state, previous)
    stacked = jnp.concatenate([points.reshape(9, row_count, col_count), mean_depth[None]], axis=0)
    widened_old = extended(stacked, (("space", 1),), 1)
    depth_rows = widened_old[9]
    old_rates = tendency(widened_old[:9].reshape(3, 3, row_count + 2, col_count), depth_rows)

    def fresh_rate(values):
        return tendency(extended(values, (("space", 1),), 1), depth_rows)

    rate_zero = fresh_rate(section_zero)
    section_one = (
        section_zero
        + half_step * (rate_zero - old_rates[0])
        + step_size * (quad_near * old_rates[0] + quad_mid * old_rates[1] + quad_far * old_rates[2])
    )
    rate_one = fresh_rate(section_one)
    section_two = (
        section_one
        + half_step * (rate_one - old_rates[1])
        + step_size * (quad_far * old_rates[0] + quad_mid * old_rates[1] + quad_near * old_rates[2])
    )
    rate_two = fresh_rate(section_two)
    fas_term = -(step_size / 3.0) * (rate_zero - 2.0 * rate_one + rate_two)
    drift_total = half_step * (rate_two - rate_zero) + fas_term
    boosted = drift_total + jnp.where(is_first, section_zero + step_size * rate_zero, 0.0)
    coarse_end = boosted
    offset = 1
    while offset < lax.axis_size("tm"):

        def one_layer(turn_index, values):
            padded = extended(values, (("space", 1),), 1)
            return values + step_size * tendency(padded, depth_rows)

        powered = lax.fori_loop(0, offset, one_layer, coarse_end)
        coarse_end = coarse_end + from_behind(powered, "tm", offset)
        offset = offset * 2
    previous_end = from_behind(coarse_end, "tm", 1)
    coarse_begin = jnp.where(is_first, init_state, previous_end)
    middle = section_one + 0.5 * (coarse_begin - section_zero + (coarse_end - section_two))
    return jnp.stack([coarse_begin, middle, coarse_end], axis=0)[None]


def solution(mesh):
    placed = (P("tm", None, None, "space", None), P(None, "space", None), P("space", None))
    return jax.shard_map(
        per_device,
        mesh=mesh,
        in_specs=placed,
        out_specs=P("tm", None, None, "space", None),
        check_vma=False,
    )
```

profile of v0, /device:TPU:192, one launch (start us, length us, event | category | flops | bytes accessed | tf_op | source)
XLA Modules:
  0.0 758.0 jit_solution(1756218878752198605)
XLA Ops:
  19.6 14.8 %collective-permute-done.8 = f32[3,16,4096]{2,1,0:T(8,128)S(1)} collective-permute-done((f32[3,16,4096]{2,1,0:T(8,128)}, f32[3,16,4096]{2,1,0:T(8,128)S(1)}, u32[]{:S(2)}, u32[]{:S(2)}) %collective-permute-start.8) | collective-permute-done | bytes 786464 | tf_op jit(solution)/shard_map/ppermute | solution.py:17
  54.8 4.2 collective-permute-start.16
  63.2 4.3 collective-permute-start.18
  73.8 23.3 %collective-permute-done.19 = f32[3,16,4096]{2,1,0:T(8,128)} collective-permute-done((f32[3,16,4096]{2,1,0:T(8,128)}, f32[3,16,4096]{2,1,0:T(8,128)}, u32[]{:S(2)}, u32[]{:S(2)}) %collective-permute-start.19) | collective-permute-done | bytes 786464 | tf_op jit(solution)/shard_map/ppermute | solution.py:17
  100.1 33.2 %while.44 = (s32[]{:T(128)}, f32[3,16,4096]{2,1,0:T(8,128)S(1)}, f32[18,4096]{1,0:T(8,128)S(1)}, s32[]{:T(128)}, s32[]{}, /*index=5*/s32[]{}) while((s32[]{:T(128)}, f32[3,16,4096]{2,1,0:T(8,128)S(1)}, f32[18,4096]{1,0:T(8,128)S(1)}, s32[]{:T(128)}, s32[]{}, /*index=5*/s32[]{}) %tuple.299), condition=%wide.region_1.2_spmd, body=%wide.region_0.1_spmd.sunk | while | flops 4415490 | bytes 29294428 | solution.py:115
  100.8 4.1 collective-permute-start.1
  117.4 4.1 collective-permute-start.1
  135.5 28.9 %collective-permute-done.20 = f32[3,16,4096]{2,1,0:T(8,128)} collective-permute-done((f32[3,16,4096]{2,1,0:T(8,128)S(1)}, f32[3,16,4096]{2,1,0:T(8,128)}, u32[]{:S(2)}, u32[]{:S(2)}) %collective-permute-start.20) | collective-permute-done | bytes 786464 | tf_op jit(solution)/shard_map/ppermute | solution.py:17
  166.8 66.4 %while.45 = (s32[]{:T(128)}, f32[3,16,4096]{2,1,0:T(8,128)S(1)}, f32[18,4096]{1,0:T(8,128)S(1)}, s32[]{:T(128)}, s32[]{}, /*index=5*/s32[]{}) while((s32[]{:T(128)}, f32[3,16,4096]{2,1,0:T(8,128)S(1)}, f32[18,4096]{1,0:T(8,128)S(1)}, s32[]{:T(128)}, s32[]{}, /*index=5*/s32[]{}) %tuple.311), condition=%wide.region_3.4_spmd, body=%wide.region_2.3_spmd.sunk | while | flops 4415490 | bytes 29294428 | solution.py:115
  200.7 4.1 collective-permute-start.3
  217.3 4.1 collective-permute-start.3
  235.1 20.7 %collective-permute-done.21 = f32[3,16,4096]{2,1,0:T(8,128)} collective-permute-done((f32[3,16,4096]{2,1,0:T(8,128)S(1)}, f32[3,16,4096]{2,1,0:T(8,128)}, u32[]{:S(2)}, u32[]{:S(2)}) %collective-permute-start.21) | collective-permute-done | bytes 786464 | tf_op jit(solution)/shard_map/ppermute | solution.py:17
  258.2 140.9 %while.46 = (s32[]{:T(128)}, f32[3,16,4096]{2,1,0:T(8,128)S(1)}, f32[18,4096]{1,0:T(8,128)S(1)}, s32[]{:T(128)}, s32[]{}, /*index=5*/s32[]{}) while((s32[]{:T(128)}, f32[3,16,4096]{2,1,0:T(8,128)S(1)}, f32[18,4096]{1,0:T(8,128)S(1)}, s32[]{:T(128)}, s32[]{}, /*index=5*/s32[]{}) %tuple.312), condition=%wide.region_5.6_spmd, body=%wide.region_4.5_spmd.sunk | while | flops 4415490 | bytes 29294428 | solution.py:115
  259.0 10.5 %collective-permute-start.4 = (f32[3,1,4096]{2,1,0:T(1,128)}, f32[3,1,4096]{2,1,0:T(1,128)}, u32[]{:S(2)}, u32[]{:S(2)}) collective-permute-start(f32[3,1,4096]{2,1,0:T(1,128)} %get-tuple-element.625), channel_id=1, source_target_pairs={{0,1},{1,2},{2,3},{3,4},{4,5},{5,6},{6,7},{7,0},{8,9},{9,10},{10,1... | collective-permute-start | bytes 147464 | tf_op jit(solution)/shard_map/while/body/eval_jaxpr/ppermute | solution.py:27
  300.2 4.1 collective-permute-start.5
  316.9 4.1 collective-permute-start.5
  333.5 4.1 collective-permute-start.5
  350.1 4.1 collective-permute-start.5
  366.7 4.1 collective-permute-start.5
  400.5 20.7 %collective-permute-done.22 = f32[3,16,4096]{2,1,0:T(8,128)S(1)} collective-permute-done((f32[3,16,4096]{2,1,0:T(8,128)S(1)}, f32[3,16,4096]{2,1,0:T(8,128)S(1)}, u32[]{:S(2)}, u32[]{:S(2)}) %collective-permute-start.22) | collective-permute-done | bytes 786464 | tf_op jit(solution)/shard_map/ppermute | solution.py:17
  423.3 273.3 %while.47 = (s32[]{:T(128)}, f32[3,16,4096]{2,1,0:T(8,128)S(1)}, f32[18,4096]{1,0:T(8,128)S(1)}, s32[]{:T(128)}, s32[]{}, /*index=5*/s32[]{}) while((s32[]{:T(128)}, f32[3,16,4096]{2,1,0:T(8,128)S(1)}, f32[18,4096]{1,0:T(8,128)S(1)}, s32[]{:T(128)}, s32[]{}, /*index=5*/s32[]{}) %tuple.313), condition=%wide.region_7.8_spmd, body=%wide.region_6.7_spmd.sunk | while | flops 4415490 | bytes 29294428 | solution.py:115
  424.1 10.6 %collective-permute-start.6 = (f32[3,1,4096]{2,1,0:T(1,128)}, f32[3,1,4096]{2,1,0:T(1,128)}, u32[]{:S(2)}, u32[]{:S(2)}) collective-permute-start(f32[3,1,4096]{2,1,0:T(1,128)} %get-tuple-element.654), channel_id=1, source_target_pairs={{0,1},{1,2},{2,3},{3,4},{4,5},{5,6},{6,7},{7,0},{8,9},{9,10},{10,1... | collective-permute-start | bytes 147464 | tf_op jit(solution)/shard_map/while/body/eval_jaxpr/ppermute | solution.py:27
  464.8 4.1 collective-permute-start.7
  481.5 4.1 collective-permute-start.7
  514.7 4.1 collective-permute-start.7
  564.5 4.1 collective-permute-start.7
  597.7 4.1 collective-permute-start.7
  614.3 4.1 collective-permute-start.7
  647.6 4.1 collective-permute-start.7
  664.2 4.1 collective-permute-start.7
  698.1 32.1 %collective-permute-done.23 = f32[3,16,4096]{2,1,0:T(8,128)S(1)} collective-permute-done((f32[3,16,4096]{2,1,0:T(8,128)S(1)}, f32[3,16,4096]{2,1,0:T(8,128)S(1)}, u32[]{:S(2)}, u32[]{:S(2)}) %collective-permute-start.23) | collective-permute-done | bytes 786464 | tf_op jit(solution)/shard_map/ppermute | solution.py:17
  733.3 22.8 %collective-permute-done.24 = f32[3,16,4096]{2,1,0:T(8,128)S(1)} collective-permute-done((f32[3,16,4096]{2,1,0:T(8,128)S(1)}, f32[3,16,4096]{2,1,0:T(8,128)S(1)}, u32[]{:S(2)}, u32[]{:S(2)}) %collective-permute-start.24) | collective-permute-done | bytes 786464 | tf_op jit(solution)/shard_map/ppermute | solution.py:17
  (1146 shorter events, 491.2 us)
Async XLA Ops:
  7.7 26.7 %collective-permute-start.8 = (f32[3,16,4096]{2,1,0:T(8,128)}, f32[3,16,4096]{2,1,0:T(8,128)S(1)}, u32[]{:S(2)}, u32[]{:S(2)}) collective-permute-start(f32[3,16,4096]{2,1,0:T(8,128)} %slice_bitcast_fusion.68), channel_id=1, source_target_pairs={{0,8},{8,16},{16,24},{24,32},{32,40},{40,48},{48,56},{56,64},{64,7... | collective-permute-start | bytes 2359304 | tf_op jit(solution)/shard_map/ppermute | solution.py:17
  71.9 25.2 %collective-permute-start.19 = (f32[3,16,4096]{2,1,0:T(8,128)}, f32[3,16,4096]{2,1,0:T(8,128)}, u32[]{:S(2)}, u32[]{:S(2)}) collective-permute-start(f32[3,16,4096]{2,1,0:T(8,128)} %fusion.122), channel_id=1, source_target_pairs={{0,8},{8,16},{16,24},{24,32},{32,40},{40,48},{48,56},{56,64},{64,7... | collective-permute-start | bytes 2359304 | tf_op jit(solution)/shard_map/ppermute | solution.py:17
  100.8 10.5 %collective-permute-start = (f32[3,1,4096]{2,1,0:T(1,128)}, f32[3,1,4096]{2,1,0:T(1,128)}, u32[]{:S(2)}, u32[]{:S(2)}) collective-permute-start(f32[3,1,4096]{2,1,0:T(1,128)} %get-tuple-element.567), channel_id=1, source_target_pairs={{0,1},{1,2},{2,3},{3,4},{4,5},{5,6},{6,7},{7,0},{8,9},{9,10},{10,1... | collective-permute-start | bytes 147464 | tf_op jit(solution)/shard_map/while/body/eval_jaxpr/ppermute | solution.py:27
  117.4 10.5 %collective-permute-start = (f32[3,1,4096]{2,1,0:T(1,128)}, f32[3,1,4096]{2,1,0:T(1,128)}, u32[]{:S(2)}, u32[]{:S(2)}) collective-permute-start(f32[3,1,4096]{2,1,0:T(1,128)} %get-tuple-element.567), channel_id=1, source_target_pairs={{0,1},{1,2},{2,3},{3,4},{4,5},{5,6},{6,7},{7,0},{8,9},{9,10},{10,1... | collective-permute-start | bytes 147464 | tf_op jit(solution)/shard_map/while/body/eval_jaxpr/ppermute | solution.py:27
  133.3 31.0 %collective-permute-start.20 = (f32[3,16,4096]{2,1,0:T(8,128)S(1)}, f32[3,16,4096]{2,1,0:T(8,128)}, u32[]{:S(2)}, u32[]{:S(2)}) collective-permute-start(f32[3,16,4096]{2,1,0:T(8,128)S(1)} %get-tuple-element.82), channel_id=1, source_target_pairs={{0,16},{8,24},{16,32},{24,40},{32,48},{40,56},{48,64},{56,72},{64,... | collective-permute-start | bytes 2359304 | tf_op jit(solution)/shard_map/ppermute | solution.py:17
  167.5 10.5 %collective-permute-start.2 = (f32[3,1,4096]{2,1,0:T(1,128)}, f32[3,1,4096]{2,1,0:T(1,128)}, u32[]{:S(2)}, u32[]{:S(2)}) collective-permute-start(f32[3,1,4096]{2,1,0:T(1,128)} %get-tuple-element.596), channel_id=1, source_target_pairs={{0,1},{1,2},{2,3},{3,4},{4,5},{5,6},{6,7},{7,0},{8,9},{9,10},{10,1... | collective-permute-start | bytes 147464 | tf_op jit(solution)/shard_map/while/body/eval_jaxpr/ppermute | solution.py:27
  184.1 10.5 %collective-permute-start.2 = (f32[3,1,4096]{2,1,0:T(1,128)}, f32[3,1,4096]{2,1,0:T(1,128)}, u32[]{:S(2)}, u32[]{:S(2)}) collective-permute-start(f32[3,1,4096]{2,1,0:T(1,128)} %get-tuple-element.596), channel_id=1, source_target_pairs={{0,1},{1,2},{2,3},{3,4},{4,5},{5,6},{6,7},{7,0},{8,9},{9,10},{10,1... | collective-permute-start | bytes 147464 | tf_op jit(solution)/shard_map/while/body/eval_jaxpr/ppermute | solution.py:27
  200.7 10.5 %collective-permute-start.2 = (f32[3,1,4096]{2,1,0:T(1,128)}, f32[3,1,4096]{2,1,0:T(1,128)}, u32[]{:S(2)}, u32[]{:S(2)}) collective-permute-start(f32[3,1,4096]{2,1,0:T(1,128)} %get-tuple-element.596), channel_id=1, source_target_pairs={{0,1},{1,2},{2,3},{3,4},{4,5},{5,6},{6,7},{7,0},{8,9},{9,10},{10,1... | collective-permute-start | bytes 147464 | tf_op jit(solution)/shard_map/while/body/eval_jaxpr/ppermute | solution.py:27
  217.3 10.5 %collective-permute-start.2 = (f32[3,1,4096]{2,1,0:T(1,128)}, f32[3,1,4096]{2,1,0:T(1,128)}, u32[]{:S(2)}, u32[]{:S(2)}) collective-permute-start(f32[3,1,4096]{2,1,0:T(1,128)} %get-tuple-element.596), channel_id=1, source_target_pairs={{0,1},{1,2},{2,3},{3,4},{4,5},{5,6},{6,7},{7,0},{8,9},{9,10},{10,1... | collective-permute-start | bytes 147464 | tf_op jit(solution)/shard_map/while/body/eval_jaxpr/ppermute | solution.py:27
  233.2 22.6 %collective-permute-start.21 = (f32[3,16,4096]{2,1,0:T(8,128)S(1)}, f32[3,16,4096]{2,1,0:T(8,128)}, u32[]{:S(2)}, u32[]{:S(2)}) collective-permute-start(f32[3,16,4096]{2,1,0:T(8,128)S(1)} %get-tuple-element.83), channel_id=1, source_target_pairs={{0,32},{8,40},{16,48},{24,56},{32,64},{40,72},{48,80},{56,88},{64,... | collective-permute-start | bytes 2359304 | tf_op jit(solution)/shard_map/ppermute | solution.py:17
  259.0 18.6 %collective-permute-start.4 = (f32[3,1,4096]{2,1,0:T(1,128)}, f32[3,1,4096]{2,1,0:T(1,128)}, u32[]{:S(2)}, u32[]{:S(2)}) collective-permute-start(f32[3,1,4096]{2,1,0:T(1,128)} %get-tuple-element.625), channel_id=1, source_target_pairs={{0,1},{1,2},{2,3},{3,4},{4,5},{5,6},{6,7},{7,0},{8,9},{9,10},{10,1... | collective-permute-start | bytes 147464 | tf_op jit(solution)/shard_map/while/body/eval_jaxpr/ppermute | solution.py:27
  283.6 10.5 %collective-permute-start.4 = (f32[3,1,4096]{2,1,0:T(1,128)}, f32[3,1,4096]{2,1,0:T(1,128)}, u32[]{:S(2)}, u32[]{:S(2)}) collective-permute-start(f32[3,1,4096]{2,1,0:T(1,128)} %get-tuple-element.625), channel_id=1, source_target_pairs={{0,1},{1,2},{2,3},{3,4},{4,5},{5,6},{6,7},{7,0},{8,9},{9,10},{10,1... | collective-permute-start | bytes 147464 | tf_op jit(solution)/shard_map/while/body/eval_jaxpr/ppermute | solution.py:27
  300.2 10.5 %collective-permute-start.4 = (f32[3,1,4096]{2,1,0:T(1,128)}, f32[3,1,4096]{2,1,0:T(1,128)}, u32[]{:S(2)}, u32[]{:S(2)}) collective-permute-start(f32[3,1,4096]{2,1,0:T(1,128)} %get-tuple-element.625), channel_id=1, source_target_pairs={{0,1},{1,2},{2,3},{3,4},{4,5},{5,6},{6,7},{7,0},{8,9},{9,10},{10,1... | collective-permute-start | bytes 147464 | tf_op jit(solution)/shard_map/while/body/eval_jaxpr/ppermute | solution.py:27
  316.8 10.5 %collective-permute-start.4 = (f32[3,1,4096]{2,1,0:T(1,128)}, f32[3,1,4096]{2,1,0:T(1,128)}, u32[]{:S(2)}, u32[]{:S(2)}) collective-permute-start(f32[3,1,4096]{2,1,0:T(1,128)} %get-tuple-element.625), channel_id=1, source_target_pairs={{0,1},{1,2},{2,3},{3,4},{4,5},{5,6},{6,7},{7,0},{8,9},{9,10},{10,1... | collective-permute-start | bytes 147464 | tf_op jit(solution)/shard_map/while/body/eval_jaxpr/ppermute | solution.py:27
  333.5 10.5 %collective-permute-start.4 = (f32[3,1,4096]{2,1,0:T(1,128)}, f32[3,1,4096]{2,1,0:T(1,128)}, u32[]{:S(2)}, u32[]{:S(2)}) collective-permute-start(f32[3,1,4096]{2,1,0:T(1,128)} %get-tuple-element.625), channel_id=1, source_target_pairs={{0,1},{1,2},{2,3},{3,4},{4,5},{5,6},{6,7},{7,0},{8,9},{9,10},{10,1... | collective-permute-start | bytes 147464 | tf_op jit(solution)/shard_map/while/body/eval_jaxpr/ppermute | solution.py:27
  350.1 10.5 %collective-permute-start.4 = (f32[3,1,4096]{2,1,0:T(1,128)}, f32[3,1,4096]{2,1,0:T(1,128)}, u32[]{:S(2)}, u32[]{:S(2)}) collective-permute-start(f32[3,1,4096]{2,1,0:T(1,128)} %get-tuple-element.625), channel_id=1, source_target_pairs={{0,1},{1,2},{2,3},{3,4},{4,5},{5,6},{6,7},{7,0},{8,9},{9,10},{10,1... | collective-permute-start | bytes 147464 | tf_op jit(solution)/shard_map/while/body/eval_jaxpr/ppermute | solution.py:27
  366.7 10.5 %collective-permute-start.4 = (f32[3,1,4096]{2,1,0:T(1,128)}, f32[3,1,4096]{2,1,0:T(1,128)}, u32[]{:S(2)}, u32[]{:S(2)}) collective-permute-start(f32[3,1,4096]{2,1,0:T(1,128)} %get-tuple-element.625), channel_id=1, source_target_pairs={{0,1},{1,2},{2,3},{3,4},{4,5},{5,6},{6,7},{7,0},{8,9},{9,10},{10,1... | collective-permute-start | bytes 147464 | tf_op jit(solution)/shard_map/while/body/eval_jaxpr/ppermute | solution.py:27
  383.3 10.5 %collective-permute-start.4 = (f32[3,1,4096]{2,1,0:T(1,128)}, f32[3,1,4096]{2,1,0:T(1,128)}, u32[]{:S(2)}, u32[]{:S(2)}) collective-permute-start(f32[3,1,4096]{2,1,0:T(1,128)} %get-tuple-element.625), channel_id=1, source_target_pairs={{0,1},{1,2},{2,3},{3,4},{4,5},{5,6},{6,7},{7,0},{8,9},{9,10},{10,1... | collective-permute-start | bytes 147464 | tf_op jit(solution)/shard_map/while/body/eval_jaxpr/ppermute | solution.py:27
  399.2 22.0 %collective-permute-start.22 = (f32[3,16,4096]{2,1,0:T(8,128)S(1)}, f32[3,16,4096]{2,1,0:T(8,128)S(1)}, u32[]{:S(2)}, u32[]{:S(2)}) collective-permute-start(f32[3,16,4096]{2,1,0:T(8,128)S(1)} %get-tuple-element.84), channel_id=1, source_target_pairs={{0,64},{8,72},{16,80},{24,88},{32,96},{40,104},{48,112},{56,120},{... | collective-permute-start | bytes 2359304 | tf_op jit(solution)/shard_map/ppermute | solution.py:17
  424.1 18.1 %collective-permute-start.6 = (f32[3,1,4096]{2,1,0:T(1,128)}, f32[3,1,4096]{2,1,0:T(1,128)}, u32[]{:S(2)}, u32[]{:S(2)}) collective-permute-start(f32[3,1,4096]{2,1,0:T(1,128)} %get-tuple-element.654), channel_id=1, source_target_pairs={{0,1},{1,2},{2,3},{3,4},{4,5},{5,6},{6,7},{7,0},{8,9},{9,10},{10,1... | collective-permute-start | bytes 147464 | tf_op jit(solution)/shard_map/while/body/eval_jaxpr/ppermute | solution.py:27
  448.2 10.5 %collective-permute-start.6 = (f32[3,1,4096]{2,1,0:T(1,128)}, f32[3,1,4096]{2,1,0:T(1,128)}, u32[]{:S(2)}, u32[]{:S(2)}) collective-permute-start(f32[3,1,4096]{2,1,0:T(1,128)} %get-tuple-element.654), channel_id=1, source_target_pairs={{0,1},{1,2},{2,3},{3,4},{4,5},{5,6},{6,7},{7,0},{8,9},{9,10},{10,1... | collective-permute-start | bytes 147464 | tf_op jit(solution)/shard_map/while/body/eval_jaxpr/ppermute | solution.py:27
  464.8 10.5 %collective-permute-start.6 = (f32[3,1,4096]{2,1,0:T(1,128)}, f32[3,1,4096]{2,1,0:T(1,128)}, u32[]{:S(2)}, u32[]{:S(2)}) collective-permute-start(f32[3,1,4096]{2,1,0:T(1,128)} %get-tuple-element.654), channel_id=1, source_target_pairs={{0,1},{1,2},{2,3},{3,4},{4,5},{5,6},{6,7},{7,0},{8,9},{9,10},{10,1... | collective-permute-start | bytes 147464 | tf_op jit(solution)/shard_map/while/body/eval_jaxpr/ppermute | solution.py:27
  481.4 10.5 %collective-permute-start.6 = (f32[3,1,4096]{2,1,0:T(1,128)}, f32[3,1,4096]{2,1,0:T(1,128)}, u32[]{:S(2)}, u32[]{:S(2)}) collective-permute-start(f32[3,1,4096]{2,1,0:T(1,128)} %get-tuple-element.654), channel_id=1, source_target_pairs={{0,1},{1,2},{2,3},{3,4},{4,5},{5,6},{6,7},{7,0},{8,9},{9,10},{10,1... | collective-permute-start | bytes 147464 | tf_op jit(solution)/shard_map/while/body/eval_jaxpr/ppermute | solution.py:27
  498.1 10.5 %collective-permute-start.6 = (f32[3,1,4096]{2,1,0:T(1,128)}, f32[3,1,4096]{2,1,0:T(1,128)}, u32[]{:S(2)}, u32[]{:S(2)}) collective-permute-start(f32[3,1,4096]{2,1,0:T(1,128)} %get-tuple-element.654), channel_id=1, source_target_pairs={{0,1},{1,2},{2,3},{3,4},{4,5},{5,6},{6,7},{7,0},{8,9},{9,10},{10,1... | collective-permute-start | bytes 147464 | tf_op jit(solution)/shard_map/while/body/eval_jaxpr/ppermute | solution.py:27
  514.7 10.5 %collective-permute-start.6 = (f32[3,1,4096]{2,1,0:T(1,128)}, f32[3,1,4096]{2,1,0:T(1,128)}, u32[]{:S(2)}, u32[]{:S(2)}) collective-permute-start(f32[3,1,4096]{2,1,0:T(1,128)} %get-tuple-element.654), channel_id=1, source_target_pairs={{0,1},{1,2},{2,3},{3,4},{4,5},{5,6},{6,7},{7,0},{8,9},{9,10},{10,1... | collective-permute-start | bytes 147464 | tf_op jit(solution)/shard_map/while/body/eval_jaxpr/ppermute | solution.py:27
  531.3 10.5 %collective-permute-start.6 = (f32[3,1,4096]{2,1,0:T(1,128)}, f32[3,1,4096]{2,1,0:T(1,128)}, u32[]{:S(2)}, u32[]{:S(2)}) collective-permute-start(f32[3,1,4096]{2,1,0:T(1,128)} %get-tuple-element.654), channel_id=1, source_target_pairs={{0,1},{1,2},{2,3},{3,4},{4,5},{5,6},{6,7},{7,0},{8,9},{9,10},{10,1... | collective-permute-start | bytes 147464 | tf_op jit(solution)/shard_map/while/body/eval_jaxpr/ppermute | solution.py:27
  564.5 10.5 %collective-permute-start.6 = (f32[3,1,4096]{2,1,0:T(1,128)}, f32[3,1,4096]{2,1,0:T(1,128)}, u32[]{:S(2)}, u32[]{:S(2)}) collective-permute-start(f32[3,1,4096]{2,1,0:T(1,128)} %get-tuple-element.654), channel_id=1, source_target_pairs={{0,1},{1,2},{2,3},{3,4},{4,5},{5,6},{6,7},{7,0},{8,9},{9,10},{10,1... | collective-permute-start | bytes 147464 | tf_op jit(solution)/shard_map/while/body/eval_jaxpr/ppermute | solution.py:27
  581.1 10.5 %collective-permute-start.6 = (f32[3,1,4096]{2,1,0:T(1,128)}, f32[3,1,4096]{2,1,0:T(1,128)}, u32[]{:S(2)}, u32[]{:S(2)}) collective-permute-start(f32[3,1,4096]{2,1,0:T(1,128)} %get-tuple-element.654), channel_id=1, source_target_pairs={{0,1},{1,2},{2,3},{3,4},{4,5},{5,6},{6,7},{7,0},{8,9},{9,10},{10,1... | collective-permute-start | bytes 147464 | tf_op jit(solution)/shard_map/while/body/eval_jaxpr/ppermute | solution.py:27
  614.3 10.5 %collective-permute-start.6 = (f32[3,1,4096]{2,1,0:T(1,128)}, f32[3,1,4096]{2,1,0:T(1,128)}, u32[]{:S(2)}, u32[]{:S(2)}) collective-permute-start(f32[3,1,4096]{2,1,0:T(1,128)} %get-tuple-element.654), channel_id=1, source_target_pairs={{0,1},{1,2},{2,3},{3,4},{4,5},{5,6},{6,7},{7,0},{8,9},{9,10},{10,1... | collective-permute-start | bytes 147464 | tf_op jit(solution)/shard_map/while/body/eval_jaxpr/ppermute | solution.py:27
  630.9 10.5 %collective-permute-start.6 = (f32[3,1,4096]{2,1,0:T(1,128)}, f32[3,1,4096]{2,1,0:T(1,128)}, u32[]{:S(2)}, u32[]{:S(2)}) collective-permute-start(f32[3,1,4096]{2,1,0:T(1,128)} %get-tuple-element.654), channel_id=1, source_target_pairs={{0,1},{1,2},{2,3},{3,4},{4,5},{5,6},{6,7},{7,0},{8,9},{9,10},{10,1... | collective-permute-start | bytes 147464 | tf_op jit(solution)/shard_map/while/body/eval_jaxpr/ppermute | solution.py:27
  696.7 33.5 %collective-permute-start.23 = (f32[3,16,4096]{2,1,0:T(8,128)S(1)}, f32[3,16,4096]{2,1,0:T(8,128)S(1)}, u32[]{:S(2)}, u32[]{:S(2)}) collective-permute-start(f32[3,16,4096]{2,1,0:T(8,128)S(1)} %get-tuple-element.85), channel_id=1, source_target_pairs={{0,128},{8,136},{16,144},{24,152},{32,160},{40,168},{48,176},{56,1... | collective-permute-start | bytes 2359304 | tf_op jit(solution)/shard_map/ppermute | solution.py:17
  731.4 24.7 %collective-permute-start.24 = (f32[3,16,4096]{2,1,0:T(8,128)S(1)}, f32[3,16,4096]{2,1,0:T(8,128)S(1)}, u32[]{:S(2)}, u32[]{:S(2)}) collective-permute-start(f32[3,16,4096]{2,1,0:T(8,128)S(1)} %add.633), channel_id=1, source_target_pairs={{0,8},{8,16},{16,24},{24,32},{32,40},{40,48},{48,56},{56,64},{64,7... | collective-permute-start | bytes 2359304 | tf_op jit(solution)/shard_map/ppermute | solution.py:17
  (270 other events, 809.2 us)
where the time goes:
time: 767 us; the launch traced here: 758 us
  local copies, waits for them, and re-layouts  243 us (32%)
  waiting for transfers between devices  178 us (23%)
  starting transfers between devices  171 us (22%)
  other arithmetic  163 us (21%)
    ppermute x7, waiting for transfers between devices, from_behind(): return lax.ppermute(value, axis, pairs)  163 us
    ppermute x35, starting transfers between devices, extended(): lax.ppermute(head, axis, [((i + 1) % count, i) for i in range(count)])  132 us
    slice x70, local copies, waits for them, and re-layouts, diffuse(): jnp.roll(centre, 1, -1)  61.1 us
    concatenate x30, local copies, waits for them, and re-layouts, extended(): jnp.concatenate([lax.ppermute(tail, axis, [(i, (i + 1) % count) for i in...  54.9 us
    concatenate x136, local copies, waits for them, and re-layouts, diffuse(): jnp.roll(centre, 1, -1)  54.3 us
    add x34, other arithmetic, tendency(): -column_slope(height_c) + coriolis * north_c  48.9 us
    while x450, local copies, waits for them, and re-layouts  41.2 us
    add x34, other arithmetic, tendency(): -row_slope(height) - coriolis * east_c  31.9 us
  transfers between devices with their start and end apart: 77, of which 14 were waited for; matrix products, arithmetic and copies ran while one was open for 26% of the time, Pallas kernels for 0%

commit v1 on v0

v1 whole, which is shorter than its diff:
```python
import functools

import jax
import jax.numpy as jnp
from jax import lax
from jax.experimental import pallas as pl
from jax.experimental.pallas import tpu as pltpu
from jax.sharding import PartitionSpec as P

MESH = pl.DeviceIdType.MESH
F32 = jnp.float32

step_size = 0.3
viscosity = 1.0 / 3.0
coriolis = 0.5
quad_near = 5.0 / 24.0
quad_mid = 1.0 / 3.0
quad_far = -1.0 / 24.0
half_step = 0.5 * step_size

ROWS = 16
COLS = 4096
SPACE = 8
CHIPS = 16
PART = 256
OWN = 16
HALO = 32
WIDE = OWN + 2 * HALO


def rates(h, u, v, de, dn, left, right, up, down, centre):
    nh, nu, nv = viscosity * h, viscosity * u, viscosity * v
    he, hn, hh = 0.5 * de, 0.5 * dn, 0.5 * h
    nhc, nuc, nvc = centre(nh), centre(nu), centre(nv)
    hr = right(nh - he) + left(nh + he) + down(centre(nh - hn)) + up(centre(nh + hn)) - 4.0 * nhc
    ur = right(nu - hh) + left(nu + hh) + down(nuc) + up(nuc) - 4.0 * nuc + coriolis * centre(v)
    vr = right(nv) + left(nv) + down(centre(nv - hh)) + up(centre(nv + hh)) - 4.0 * nvc - coriolis * centre(u)
    return hr, ur, vr


CHUNK = 512


def fine_kernel(fine, fine_halo, start, start_halo, depth, depth_halo, item, boosted, partial, g1, g2, s1, acc, bst):
    slot = lax.axis_index("tm")
    first = jnp.where(slot == 0, 1.0, 0.0).astype(F32)
    even = jnp.where(lax.rem(slot, 2) == 0, step_size, 0.0).astype(F32)

    def ring(main, halo, idx, cols):
        return jnp.concatenate([main[idx + (slice(None), cols)], halo[idx + (slice(None), cols)]], axis=0)

    def edges(base):
        lo = pl.multiple_of(lax.rem(base + COLS - 128, COLS), 128)
        hi = pl.multiple_of(lax.rem(base + CHUNK, COLS), 128)
        return pl.ds(lo, 128), pl.ds(base, CHUNK), pl.ds(hi, 128)

    def wide(get, base):
        return jnp.concatenate([get(c) for c in edges(base)], axis=1)

    n = CHUNK + 256

    def right(x):
        return pltpu.roll(x, n - 1, 1)[:, 128 : 128 + CHUNK]

    def left(x):
        return pltpu.roll(x, 1, 1)[:, 128 : 128 + CHUNK]

    def down(x):
        return pltpu.roll(x, 23, 0)

    def up(x):
        return pltpu.roll(x, 1, 0)

    def centre(x):
        return x[:, 128 : 128 + CHUNK]

    def rate(get, base):
        h, u, v = (wide(functools.partial(get, f), base) for f in range(3))
        d = wide(lambda c: ring(depth, depth_halo, (), c), base)
        return rates(h, u, v, d * u, d * v, left, right, up, down, centre)

    def loop(body):
        @pl.loop(0, COLS // CHUNK)
        def _(i):
            body(pl.multiple_of(i * CHUNK, CHUNK))

    def old(base):
        cols = pl.ds(base, CHUNK)
        r = [rate(lambda f, c, m=m: ring(fine, fine_halo, (3 * m + f,), c), base) for m in range(3)]
        for f in range(3):
            near, mid, far = r[0][f], r[1][f], r[2][f]
            g1[f, :, cols] = step_size * (quad_near * near + quad_mid * mid + quad_far * far) - half_step * near
            g2[f, :, cols] = step_size * (quad_far * near + quad_mid * mid + quad_near * far) - half_step * mid

    loop(old)

    def zero(base):
        cols = pl.ds(base, CHUNK)
        r = rate(lambda f, c: ring(start, start_halo, (f,), c), base)
        for f in range(3):
            sz = ring(start, start_halo, (f,), cols)
            s1[f, :, cols] = sz + half_step * r[f] + g1[f, :, cols]
            acc[f, :, cols] = first * (sz + step_size * r[f]) - (half_step + step_size / 3.0) * r[f]

    loop(zero)

    def one(base):
        cols = pl.ds(base, CHUNK)
        r = rate(lambda f, c: s1[f, :, c], base)
        for f in range(3):
            g2[f, :, cols] = s1[f, :, cols] + half_step * r[f] + g2[f, :, cols]
            acc[f, :, cols] += (2.0 * step_size / 3.0) * r[f]

    loop(one)

    def two(base):
        cols = pl.ds(base, CHUNK)
        r = rate(lambda f, c: g2[f, :, c], base)
        for f in range(3):
            b = acc[f, :, cols] + (half_step - step_size / 3.0) * r[f]
            bst[f, :, cols] = b
            boosted[f, :, cols] = b[:ROWS]
            partial[f, :, cols] = s1[f, :ROWS, cols] - 0.5 * (start[f, :, cols] + g2[f, :ROWS, cols])

    loop(two)

    def push(base):
        cols = pl.ds(base, CHUNK)
        r = rate(lambda f, c: bst[f, :, c], base)
        for f in range(3):
            item[f, :, cols] = boosted[f, :, cols] + even * r[f][:ROWS]

    loop(push)


def ring_place(k, chip):
    z, x = chip // 4, lax.rem(chip, 4)
    r = z * 4 + jnp.where(lax.rem(z, 2) == 0, x, 3 - x)
    return jnp.where(k == 0, r, CHIPS - 1 - r)


def ring_chip(k, r):
    r = jnp.where(k == 0, r, CHIPS - 1 - r)
    z, x = r // 4, lax.rem(r, 4)
    return z * 4 + jnp.where(lax.rem(z, 2) == 0, x, 3 - x)


def coarse_kernel(
    item, boosted, depth, esum, other, vout, ritem, rt, et, dr, dt, ex, vx, vt, vr,
    pair_s, pair_r, one_s, one_r, dep_s, dep_r, two_s, two_r, halo_s, halo_r,
    ret_s, ret_r, row_s, row_r, fin_s, fin_r,
):
    tm = lax.axis_index("tm")
    s = lax.axis_index("space")
    chip, k = tm // 2, lax.rem(tm, 2)
    place = ring_place(k, chip)
    q = (s * 2 + k) * CHIPS + place
    partner = {"tm": chip * 2 + 1 - k, "space": s}

    def at(c, sp):
        return {"tm": c * 2 + k, "space": sp}

    def near(step):
        p = lax.rem(q + step + 256, 256)
        kk = lax.rem(p // CHIPS, 2)
        return {"tm": ring_chip(kk, lax.rem(p, CHIPS)) * 2 + kk, "space": p // 32}

    rows_of = [at(chip, lax.rem(s + d, SPACE)) for d in range(1, SPACE)]
    chips_of = [at(lax.rem(chip + d, CHIPS), s) for d in range(1, CHIPS)]
    rings = [near(1), near(-1), near(2), near(-2)]
    vt[...] = jnp.zeros_like(vt)
    barrier = pltpu.get_barrier_semaphore()
    peers = [partner] + rows_of + chips_of + rings
    for p in peers:
        pl.semaphore_signal(barrier, inc=1, device_id=p, device_id_type=MESH)
    pl.semaphore_wait(barrier, len(peers))

    def copy(src, dst, ss, rs, dev):
        return pltpu.make_async_remote_copy(src_ref=src, dst_ref=dst, send_sem=ss, recv_sem=rs, device_id=dev, device_id_type=MESH)

    def block(sp, kk=None):
        return pl.ds(pl.multiple_of(512 * sp + 256 * (k if kk is None else kk), PART), PART)

    def rows(sp, n=ROWS):
        return pl.ds(pl.multiple_of(sp, 8), n)

    pair = [copy(item, ritem, pair_s.at[0], pair_r.at[0], partner), copy(boosted, other, pair_s.at[1], pair_r.at[1], partner)]
    for c in pair:
        c.start()

    def depth_parts(sp):
        base = 512 * sp + 256 * k
        return (
            (pl.ds(pl.multiple_of(base, 128), PART), pl.ds(128, PART)),
            (pl.ds(pl.multiple_of(lax.rem(base + COLS - 128, COLS), 128), 128), pl.ds(0, 128)),
            (pl.ds(pl.multiple_of(lax.rem(base + PART, COLS), 128), 128), pl.ds(384, 128)),
        )

    def depth_copy(d, n, send):
        sp = lax.rem(s + d, SPACE) if send else lax.rem(s + SPACE - d, SPACE)
        src, dst = depth_parts(sp if send else s)[n]
        return copy(depth.at[:, src], dr.at[rows(ROWS * (s if send else sp)), dst], dep_s.at[n, d], dep_r.at[n, d], at(chip, sp))

    for d in range(1, SPACE):
        for n in range(3):
            depth_copy(d, n, True).start()
    for src, dst in depth_parts(s):
        dr[rows(ROWS * s), dst] = depth[:, src]

    pair[0].wait_recv()
    for f in range(3):
        esum[f] = item[f] + ritem[f]

    def one_copy(d, send):
        sp = lax.rem(s + d, SPACE) if send else lax.rem(s + SPACE - d, SPACE)
        return copy(
            esum.at[:, :, block(sp if send else s)], rt.at[:, rows(ROWS * (s if send else sp)), :], one_s.at[d], one_r.at[d], at(chip, sp)
        )

    for d in range(1, SPACE):
        one_copy(d, True).start()
    rt[:, rows(ROWS * s), :] = esum[:, :, block(s)]

    for d in range(1, SPACE):
        for n in range(3):
            depth_copy(d, n, False).wait_recv()
    for t in range(4):
        dt[128 * t : 128 * t + 128, :] = dr[:, 128 * t : 128 * t + 128].T

    for d in range(1, SPACE):
        one_copy(d, False).wait_recv()
    for f in range(3):
        for t in range(2):
            et[f, 128 * t : 128 * t + 128, :] = rt[f, :, 128 * t : 128 * t + 128].T

    def two_copy(d, send):
        c = lax.rem(chip + d, CHIPS) if send else lax.rem(chip + CHIPS - d, CHIPS)
        src = et.at[:, rows(OWN * (ring_place(k, c) if send else place), OWN), :]
        return copy(src, ex.at[chip if send else c, :, pl.ds(HALO, OWN), :], two_s.at[d], two_r.at[d], at(c, s))

    for d in range(1, CHIPS):
        two_copy(d, True).start()
    ex[chip, :, HALO : HALO + OWN, :] = et[:, rows(OWN * place, OWN), :]
    for d in range(1, CHIPS):
        two_copy(d, False).wait_recv()

    halos = []
    for hop, lo, hi, width in ((1, 0, 10, 16), (1, 10, 14, 8), (2, 0, 2, 16), (2, 2, 6, 8)):
        far = OWN * (hop - 1)
        halos.append((lo, hi, HALO + OWN - width, HALO - far - width, width, hop))
        halos.append((lo, hi, HALO, HALO + OWN + far, width, -hop))

    def halo_copy(i):
        lo, hi, src, dst, width, hop = halos[i]
        to = rings[{1: 0, -1: 1, 2: 2, -2: 3}[hop]]
        return copy(ex.at[lo:hi, :, pl.ds(src, width), :], ex.at[lo:hi, :, pl.ds(dst, width), :], halo_s.at[i], halo_r.at[i], to)

    for i in range(len(halos)):
        halo_copy(i).start()
    for i in range(len(halos)):
        halo_copy(i).wait_recv()

    d_own = dt[rows(96 + OWN * place, WIDE), :]

    def same(x):
        return x

    def stepped(state):
        h, u, v = state
        r = rates(
            h, u, v, d_own * u, d_own * v,
            lambda x: pltpu.roll(x, 1, 0), lambda x: pltpu.roll(x, WIDE - 1, 0),
            lambda x: pltpu.roll(x, 1, 1), lambda x: pltpu.roll(x, 127, 1), same,
        )
        return tuple(x + step_size * y for x, y in zip(state, r))

    def ret_copy(j):
        return copy(vx.at[j], vt.at[:, rows(OWN * place, OWN), :], ret_s.at[j], ret_r.at[chip], at(j, s))

    def body(j, state):
        state = stepped(stepped(state))
        state = tuple(x + ex[j, f] for f, x in enumerate(state))
        for f in range(3):
            vx[j + 1, f] = state[f][HALO : HALO + OWN]

        @pl.when(chip != j + 1)
        def _():
            ret_copy(j + 1).start()

        return state

    empty = jnp.zeros((WIDE, 128), F32)
    lax.fori_loop(0, CHIPS - 1, body, (empty, empty, empty))

    @pl.when(chip > 0)
    def _():
        vt[:, rows(OWN * place, OWN), :] = vx[chip]
        for d in range(1, CHIPS):
            c = lax.rem(chip + CHIPS - d, CHIPS)
            dst = vt.at[:, rows(OWN * ring_place(k, c), OWN), :]
            copy(vx.at[0], dst, ret_s.at[0], ret_r.at[c], at(c, s)).wait_recv()

    for f in range(3):
        for t in range(2):
            vr[f, :, 128 * t : 128 * t + 128] = vt[f, 128 * t : 128 * t + 128, :].T

    def row_parts(sp):
        return (
            (rows(ROWS * sp), pl.ds(0, 16)),
            (rows(lax.rem(ROWS * sp + 16, 128), 8), pl.ds(16, 8)),
            (rows(lax.rem(ROWS * sp + 120, 128), 8), pl.ds(24, 8)),
        )

    def row_copy(d, n, send):
        sp = lax.rem(s + d, SPACE) if send else lax.rem(s + SPACE - d, SPACE)
        src, dst = row_parts(sp if send else s)[n]
        return copy(vr.at[:, src, :], vout.at[:, dst, block(s if send else sp)], row_s.at[n, d], row_r.at[n, d], at(chip, sp))

    for d in range(1, SPACE):
        for n in range(3):
            row_copy(d, n, True).start()
    for src, dst in row_parts(s):
        vout[:, dst, block(s)] = vr[:, src, :]

    def fin_copy(d, send):
        cols = block(lax.rem(s + SPACE - d, SPACE), k if send else 1 - k)
        return copy(vout.at[:, :, cols], vout.at[:, :, cols], fin_s.at[d], fin_r.at[d], partner)

    fin_copy(0, True).start()
    for d in range(1, SPACE):
        for n in range(3):
            row_copy(d, n, False).wait_recv()
        fin_copy(d, True).start()
    pair[1].wait_recv()
    for d in range(SPACE):
        fin_copy(d, False).wait_recv()

    for c in pair:
        c.wait_send()
    for d in range(1, SPACE):
        for n in range(3):
            depth_copy(d, n, True).wait_send()
            row_copy(d, n, True).wait_send()
        one_copy(d, True).wait_send()
    for d in range(1, CHIPS):
        two_copy(d, True).wait_send()
    for i in range(len(halos)):
        halo_copy(i).wait_send()
    for d in range(SPACE):
        fin_copy(d, True).wait_send()

    @pl.loop(1, CHIPS)
    def _(j):
        @pl.when(chip != j)
        def _():
            ret_copy(j).wait_send()


def final_kernel(v, boosted, other, esum, partial, init, depth, depth_halo, out):
    slot = lax.axis_index("tm")
    even = lax.rem(slot, 2) == 0
    first = slot == 0
    n = CHUNK + 256

    def right(x):
        return pltpu.roll(x, x.shape[1] - 1, 1)

    def left(x):
        return pltpu.roll(x, 1, 1)

    def down(x):
        return pltpu.roll(x, 23, 0)

    def up(x):
        return pltpu.roll(x, 1, 0)

    low = lax.broadcasted_iota(jnp.int32, (8, n), 0) < 4

    @pl.loop(0, COLS // CHUNK)
    def _(i):
        base = pl.multiple_of(i * CHUNK, CHUNK)
        lo = pl.multiple_of(lax.rem(base + COLS - 128, COLS), 128)
        hi = pl.multiple_of(lax.rem(base + CHUNK, COLS), 128)
        parts = (pl.ds(lo, 128), pl.ds(base, CHUNK), pl.ds(hi, 128))
        cols = pl.ds(base, CHUNK)

        def ring(f):
            x = jnp.concatenate([v[f, :, c] for c in parts], axis=1)
            return jnp.concatenate([x[:16], jnp.where(low, x[16:24], x[24:32])], axis=0)

        d = jnp.concatenate([jnp.concatenate([depth[:, c], depth_halo[:, c]], axis=0) for c in parts], axis=1)

        def stepped(state):
            h, u, w = state
            r = rates(h, u, w, d * u, d * w, left, right, up, down, lambda x: x)
            return [x + step_size * y for x, y in zip(state, r)]

        state = [ring(f) for f in range(3)]
        a = stepped(state)
        b = stepped(a)
        for f in range(3):
            begin = state[f][:16, 128 : 128 + CHUNK]
            ours = jnp.where(even, boosted[f, :, cols], other[f, :, cols])
            y1 = ours + a[f][:16, 128 : 128 + CHUNK]
            y2 = esum[f, :, cols] + b[f][:16, 128 : 128 + CHUNK]
            start = jnp.where(even, jnp.where(first, init[f, :, cols], begin), y1)
            end = jnp.where(even, y1, y2)
            out[0, f, :, cols] = start
            out[1, f, :, cols] = partial[f, :, cols] + 0.5 * (start + end)
            out[2, f, :, cols] = end


VM = pl.BlockSpec(memory_space=pltpu.VMEM)


def per_device(fine_nodes, init_state, mean_depth):
    points = fine_nodes[0].reshape(9, ROWS, COLS)
    slot = lax.axis_index("tm")
    last = slot == 31
    is_first = slot == 0
    ring_next = [((i + 1) % SPACE, i) for i in range(SPACE)]
    ring_prev = [(i, (i + 1) % SPACE) for i in range(SPACE)]

    stacked = jnp.concatenate([points, mean_depth[None]], axis=0)
    after = lax.ppermute(stacked[:, :4], "space", ring_next)
    before = lax.ppermute(stacked[:, ROWS - 4 :], "space", ring_prev)
    halo = jnp.concatenate([after, before], axis=1)

    end = points[6:9]
    shifted = lax.ppermute(end, "tm", [(i, i + 1) for i in range(31)])
    start = jnp.where(is_first, init_state, shifted)
    flat = lambda t, sp: (t % 32) * SPACE + sp % SPACE
    edge = jnp.where(last, init_state, end)
    start_after = lax.ppermute(
        edge[:, :4], ("tm", "space"), [(flat(t, sp + 1), flat(t + 1, sp)) for t in range(32) for sp in range(SPACE)]
    )
    start_before = lax.ppermute(
        edge[:, ROWS - 4 :], ("tm", "space"), [(flat(t, sp), flat(t + 1, sp + 1)) for t in range(32) for sp in range(SPACE)]
    )
    start_halo = jnp.concatenate([start_after, start_before], axis=1)

    state = jax.ShapeDtypeStruct((3, ROWS, COLS), F32)
    ringed = pltpu.VMEM((3, 24, COLS), F32)
    item, boosted, partial = pl.pallas_call(
        fine_kernel,
        out_shape=[state] * 3,
        in_specs=[VM] * 6,
        out_specs=[VM] * 3,
        scratch_shapes=[ringed] * 5,
        name="fine",
    )(points, halo[:9], start, start_halo, mean_depth, halo[9])

    dma = pltpu.SemaphoreType.DMA
    esum, other, v = pl.pallas_call(
        coarse_kernel,
        out_shape=[state, state, jax.ShapeDtypeStruct((3, 32, COLS), F32)],
        in_specs=[VM] * 3,
        out_specs=[VM] * 3,
        scratch_shapes=[
            pltpu.VMEM((3, ROWS, COLS), F32),
            pltpu.VMEM((3, 128, PART), F32),
            pltpu.VMEM((3, PART, 128), F32),
            pltpu.VMEM((128, 512), F32),
            pltpu.VMEM((512, 128), F32),
            pltpu.VMEM((CHIPS, 3, WIDE, 128), F32),
            pltpu.VMEM((CHIPS, 3, OWN, 128), F32),
            pltpu.VMEM((3, PART, 128), F32),
            pltpu.VMEM((3, 128, PART), F32),
            dma((2,)), dma((2,)), dma((8,)), dma((8,)), dma((3, 8)), dma((3, 8)), dma((16,)), dma((16,)),
            dma((8,)), dma((8,)), dma((16,)), dma((16,)), dma((3, 8)), dma((3, 8)), dma((8,)), dma((8,)),
        ],
        compiler_params=pltpu.CompilerParams(collective_id=0, has_side_effects=True),
        name="coarse",
    )(item, boosted, mean_depth)

    out = pl.pallas_call(
        final_kernel,
        out_shape=jax.ShapeDtypeStruct((3, 3, ROWS, COLS), F32),
        in_specs=[VM] * 8,
        out_specs=VM,
        name="final",
    )(v, boosted, other, esum, partial, init_state, mean_depth, halo[9])
    return out[None]


def solution(mesh):
    placed = (P("tm", None, None, "space", None), P(None, "space", None), P("space", None))
    return jax.shard_map(
        per_device,
        mesh=mesh,
        in_specs=placed,
        out_specs=P("tm", None, None, "space", None),
        check_vma=False,
    )
```

time: 767 us -> 169 us (0.22)
  the two profiles are of different devices: /device:TPU:192 before, /device:TPU:231 now
where the time goes in v1:
time: 169 us; the launch traced here: 168 us
  Pallas kernels  107 us (63%)
  waiting for transfers between devices  46.2 us (27%)
  other arithmetic  10.3 us (6%)
  starting transfers between devices  3.32 us (2%)
    pallas_call x1, Pallas kernels, per_device(): pl.pallas_call(coarse_kernel, out_shape=[state, state, jax.ShapeDtypeStru...  86.9 us
    ppermute x1, waiting for transfers between devices, per_device(): before = lax.ppermute(stacked[:, ROWS - 4:], 'space', ring_prev)  20.2 us
    ppermute x1, waiting for transfers between devices, per_device(): after = lax.ppermute(stacked[:, :4], 'space', ring_next)  15.1 us
    pallas_call x1, Pallas kernels, per_device(): pl.pallas_call(fine_kernel, out_shape=[state] * 3, in_specs=[VM] * 6, out...  13.5 us
    pallas_call x1, Pallas kernels, per_device(): pl.pallas_call(final_kernel, out_shape=jax.ShapeDtypeStruct((3, 3, ROWS,...  6.82 us
    ppermute x1, waiting for transfers between devices, per_device(): lax.ppermute(edge[:, ROWS - 4:], ('tm', 'space'), [(flat(t, sp), flat(t +...  5.49 us
    ppermute x1, waiting for transfers between devices, per_device(): lax.ppermute(edge[:, :4], ('tm', 'space'), [(flat(t, sp + 1), flat(t + 1,...  5.36 us
  transfers between devices with their start and end apart: 5, of which 4 were waited for; matrix products, arithmetic and copies ran while one was open for 3% of the time, Pallas kernels for 0%

profile of v1, /device:TPU:231, one launch (start us, length us, event | category | flops | bytes accessed | tf_op | source)
XLA Modules:
  0.0 168.1 jit_solution(15645293464414659279)
XLA Ops:
  0.0 0.0 copy-start
  0.0 3.2 %pad_maximum_fusion = (f32[10,4,4096]{2,1,0:T(4,128)}, f32[10,4,4096]{2,1,0:T(4,128)}) fusion(f32[1,16,4096]{2,1,0:T(8,128)} %bitcast.11, f32[9,16,4096]{2,1,0:T(8,128)} %bitcast.9), kind=kLoop, calls=%fused_computation.4 | loop fusion | flops 327680 | bytes 3932160 | tf_op jit(solution)/shard_map/concatenate | solution.py:424
  3.2 1.7 %collective-permute-start.1 = (f32[10,4,4096]{2,1,0:T(4,128)}, f32[10,4,4096]{2,1,0:T(4,128)}, u32[]{:S(2)}, u32[]{:S(2)}) collective-permute-start(f32[10,4,4096]{2,1,0:T(4,128)} %get-tuple-element.17), channel_id=1, source_target_pairs={{0,1},{1,2},{2,3},{3,4},{4,5},{5,6},{6,7},{7,0},{8,9},{9,10},{10,1... | collective-permute-start | bytes 1966088 | tf_op jit(solution)/shard_map/ppermute | solution.py:426
  5.0 0.0 collective-permute-start
  5.0 0.0 copy-done
  5.0 0.9 slice_bitcast_fusion
  5.9 0.0 copy-start.1
  5.9 1.4 collective-permute-start.2
  7.3 20.2 %collective-permute-done.1 = f32[10,4,4096]{2,1,0:T(4,128)} collective-permute-done((f32[10,4,4096]{2,1,0:T(4,128)}, f32[10,4,4096]{2,1,0:T(4,128)}, u32[]{:S(2)}, u32[]{:S(2)}) %collective-permute-start.1) | collective-permute-done | bytes 655392 | tf_op jit(solution)/shard_map/ppermute | solution.py:426
  27.6 15.1 %collective-permute-done = f32[10,4,4096]{2,1,0:T(4,128)} collective-permute-done((f32[10,4,4096]{2,1,0:T(4,128)}, f32[10,4,4096]{2,1,0:T(4,128)}, u32[]{:S(2)}, u32[]{:S(2)}) %collective-permute-start) | collective-permute-done | bytes 655392 | tf_op jit(solution)/shard_map/ppermute | solution.py:425
  42.6 2.5 %fusion.fine_halo = f32[9,8,4096]{2,1,0:T(8,128)} fusion(f32[10,4,4096]{2,1,0:T(4,128)} %collective-permute-done, f32[10,4,4096]{2,1,0:T(4,128)} %collective-permute-done.1), kind=kLoop, calls=%fused_computation.2 | loop fusion | flops 294912 | bytes 2490368 | tf_op jit(solution)/shard_map/concatenate | solution.py:427
  45.1 0.0 collective-permute-done.2
  45.1 0.0 copy-done.1
  45.2 2.2 %broadcast_select_fusion = (f32[3,16,4096]{2,1,0:T(8,128)S(1)}, f32[3,16,4096]{2,1,0:T(8,128)}) fusion(f32[3,16,4096]{2,1,0:T(8,128)S(1)} %copy-done.1, pred[]{:T(512)S(6)} %eq.7, f32[1,3,3,16,4096]{4,3,2,1,0:T(8,128)S(1)} %copy-done, f32[3,16,4096]{2,1,0:T(8,128)} %collective-permute-done.2, pred[]{:T(512)S(6)} %eq.6), kind=kLoop, calls=%fused_computation.7 | loop fusion | flops 393216 | bytes 3932162 | tf_op jit(solution)/shard_map/jit(_where)/select_n | solution.py:433
  47.3 0.1 fusion.2
  47.4 0.1 collective-permute-start.3
  47.5 0.1 collective-permute-start.4
  47.6 1.6 fusion.1.depth_halo
  49.1 5.4 %collective-permute-done.3 = f32[3,4,4096]{2,1,0:T(4,128)S(1)} collective-permute-done((f32[3,4,4096]{2,1,0:T(4,128)S(1)}, f32[3,4,4096]{2,1,0:T(4,128)S(1)}, u32[]{:S(2)}, u32[]{:S(2)}) %collective-permute-start.3) | collective-permute-done | bytes 196640 | tf_op jit(solution)/shard_map/ppermute | solution.py:434
  54.5 5.5 %collective-permute-done.4 = f32[3,4,4096]{2,1,0:T(4,128)S(1)} collective-permute-done((f32[3,4,4096]{2,1,0:T(4,128)S(1)}, f32[3,4,4096]{2,1,0:T(4,128)S(1)}, u32[]{:S(2)}, u32[]{:S(2)}) %collective-permute-start.4) | collective-permute-done | bytes 196640 | tf_op jit(solution)/shard_map/ppermute | solution.py:437
  60.0 0.8 pad_maximum_fusion.2.start_halo
  60.8 13.5 %fine.1 = (f32[3,16,4096]{2,1,0:T(8,128)}, f32[3,16,4096]{2,1,0:T(8,128)}, f32[3,16,4096]{2,1,0:T(8,128)}) custom-call(f32[9,16,4096]{2,1,0:T(8,128)} %bitcast.10, f32[9,8,4096]{2,1,0:T(8,128)} %fusion.fine_halo, f32[3,16,4096]{2,1,0:T(8,128)} %get-tuple-element.22.start, f32[3,8,4096]{2,1,0:T(8,128)} %pad_maximum_fusion.2.start_halo, f32[16,4096]{1,0:T(8,128)} %depth.5, ...), custom_call_target="tpu_custom_call" | custom-call | tf_op jit(solution)/shard_map/fine/pallas_call | solution.py:444
  74.3 86.9 %coarse.1 = (f32[3,16,4096]{2,1,0:T(8,128)}, f32[3,16,4096]{2,1,0:T(8,128)}, f32[3,32,4096]{2,1,0:T(8,128)}) custom-call(f32[3,16,4096]{2,1,0:T(8,128)} %get-tuple-element.11.item, f32[3,16,4096]{2,1,0:T(8,128)} %get-tuple-element.12.boosted, f32[16,4096]{1,0:T(8,128)} %depth.5), custom_call_target="tpu_custom_call" | custom-call | tf_op jit(solution)/shard_map/coarse/pallas_call | solution.py:454
  161.3 6.8 %final.1 = f32[3,3,16,4096]{3,2,1,0:T(8,128)} custom-call(f32[3,32,4096]{2,1,0:T(8,128)} %get-tuple-element.13.v, f32[3,16,4096]{2,1,0:T(8,128)} %get-tuple-element.12.boosted, f32[3,16,4096]{2,1,0:T(8,128)} %get-tuple-element.14.other, f32[3,16,4096]{2,1,0:T(8,128)} %get-tuple-element.15.esum, f32[3,16,4096]{2,1,0:T(8,128)} %get-tuple-element.16.partial, ...), custom_call_target="tpu_custom_call" | custom-call | tf_op jit(solution)/shard_map/final/pallas_call | solution.py:476
Async XLA Ops:
  0.0 5.0 %copy-start = (f32[1,3,3,16,4096]{4,3,2,1,0:T(8,128)S(1)}, f32[1,3,3,16,4096]{4,3,2,1,0:T(8,128)}, u32[]{:S(2)}) copy-start(f32[1,3,3,16,4096]{4,3,2,1,0:T(8,128)} %param.3) | copy-start | bytes 7077892
  3.2 24.4 %collective-permute-start.1 = (f32[10,4,4096]{2,1,0:T(4,128)}, f32[10,4,4096]{2,1,0:T(4,128)}, u32[]{:S(2)}, u32[]{:S(2)}) collective-permute-start(f32[10,4,4096]{2,1,0:T(4,128)} %get-tuple-element.17), channel_id=1, source_target_pairs={{0,1},{1,2},{2,3},{3,4},{4,5},{5,6},{6,7},{7,0},{8,9},{9,10},{10,1... | collective-permute-start | bytes 1966088 | tf_op jit(solution)/shard_map/ppermute | solution.py:426
  5.0 37.7 %collective-permute-start = (f32[10,4,4096]{2,1,0:T(4,128)}, f32[10,4,4096]{2,1,0:T(4,128)}, u32[]{:S(2)}, u32[]{:S(2)}) collective-permute-start(f32[10,4,4096]{2,1,0:T(4,128)} %get-tuple-element.18), channel_id=1, source_target_pairs={{1,0},{2,1},{3,2},{4,3},{5,4},{6,5},{7,6},{0,7},{9,8},{10,9},{11,1... | collective-permute-start | bytes 1966088 | tf_op jit(solution)/shard_map/ppermute | solution.py:425
  5.9 39.2 %copy-start.1 = (f32[3,16,4096]{2,1,0:T(8,128)S(1)}, f32[3,16,4096]{2,1,0:T(8,128)}, u32[]{:S(2)}) copy-start(f32[3,16,4096]{2,1,0:T(8,128)} %init.1) | copy-start | bytes 2359300
  5.9 39.2 %collective-permute-start.2 = (f32[3,16,4096]{2,1,0:T(8,128)}, f32[3,16,4096]{2,1,0:T(8,128)}, u32[]{:S(2)}, u32[]{:S(2)}) collective-permute-start(f32[3,16,4096]{2,1,0:T(8,128)} %slice_bitcast_fusion), channel_id=1, source_target_pairs={{0,8},{8,16},{16,24},{24,32},{32,40},{40,48},{48,56},{56,64},{64,7... | collective-permute-start | bytes 2359304 | tf_op jit(solution)/shard_map/ppermute | solution.py:430
  47.4 7.1 %collective-permute-start.3 = (f32[3,4,4096]{2,1,0:T(4,128)S(1)}, f32[3,4,4096]{2,1,0:T(4,128)S(1)}, u32[]{:S(2)}, u32[]{:S(2)}) collective-permute-start(f32[3,4,4096]{2,1,0:T(4,128)S(1)} %get-tuple-element.19), channel_id=1, source_target_pairs={{1,8},{2,9},{3,10},{4,11},{5,12},{6,13},{7,14},{0,15},{9,16},{10,1... | collective-permute-start | bytes 589832 | tf_op jit(solution)/shard_map/ppermute | solution.py:434
  47.5 12.5 %collective-permute-start.4 = (f32[3,4,4096]{2,1,0:T(4,128)S(1)}, f32[3,4,4096]{2,1,0:T(4,128)S(1)}, u32[]{:S(2)}, u32[]{:S(2)}) collective-permute-start(f32[3,4,4096]{2,1,0:T(4,128)S(1)} %get-tuple-element.20), channel_id=1, source_target_pairs={{0,9},{1,10},{2,11},{3,12},{4,13},{5,14},{6,15},{7,8},{8,17},{9,18... | collective-permute-start | bytes 589832 | tf_op jit(solution)/shard_map/ppermute | solution.py:437

commit v2 on v0

v2 whole, which is shorter than its diff:
```python
import functools

import jax
import jax.numpy as jnp
from jax import lax
from jax.experimental import pallas as pl
from jax.experimental.pallas import tpu as pltpu
from jax.sharding import PartitionSpec as P

MESH = pl.DeviceIdType.MESH
F32 = jnp.float32

step_size = 0.3
viscosity = 1.0 / 3.0
coriolis = 0.5
quad_near = 5.0 / 24.0
quad_mid = 1.0 / 3.0
quad_far = -1.0 / 24.0
half_step = 0.5 * step_size
start_share = -(half_step + step_size / 3.0)
one_share = 2.0 * step_size / 3.0
two_share = half_step - step_size / 3.0

ROWS = 16
COLS = 4096
SPACE = 8
CHIPS = 16
PART = 256
OWN = 16
HALO = 32
WIDE = OWN + 2 * HALO


def rates(h, u, v, de, dn, left, right, up, down, centre):
    nh, nu, nv = viscosity * h, viscosity * u, viscosity * v
    he, hn, hh = 0.5 * de, 0.5 * dn, 0.5 * h
    nhc, nuc, nvc = centre(nh), centre(nu), centre(nv)
    hr = right(nh - he) + left(nh + he) + down(centre(nh - hn)) + up(centre(nh + hn)) - 4.0 * nhc
    ur = right(nu - hh) + left(nu + hh) + down(nuc) + up(nuc) - 4.0 * nuc + coriolis * centre(v)
    vr = right(nv) + left(nv) + down(centre(nv - hh)) + up(centre(nv + hh)) - 4.0 * nvc - coriolis * centre(u)
    return hr, ur, vr


CHUNK = 512
RING = 24


def edges(base):
    lo = pl.multiple_of(lax.rem(base + COLS - 128, COLS), 128)
    hi = pl.multiple_of(lax.rem(base + CHUNK, COLS), 128)
    return pl.ds(lo, 128), pl.ds(base, CHUNK), pl.ds(hi, 128)


def wide(get, base):
    return jnp.concatenate([get(c) for c in edges(base)], axis=1)


def right(x):
    return pltpu.roll(x, x.shape[1] - 1, 1)


def left(x):
    return pltpu.roll(x, 1, 1)


def down(x):
    return pltpu.roll(x, RING - 1, 0)


def up(x):
    return pltpu.roll(x, 1, 0)


def inner(x):
    return x[:, 128 : 128 + CHUNK]


def ring_rates(q, depth, base):
    h, u, v = (wide(lambda c, f=f: q[f, :, c], base) for f in range(3))
    d = wide(lambda c: depth[:, c], base)
    return rates(h, u, v, d * u, d * v, lambda x: inner(left(x)), lambda x: inner(right(x)), up, down, inner)


def chunks(body):
    @pl.loop(0, COLS // CHUNK)
    def _(i):
        body(pl.multiple_of(i * CHUNK, CHUNK))


def sub_roll(x, by):
    by %= 8
    return x if by == 0 else pltpu.roll(x, by, 0)


def pack(parts, at):
    row = lax.broadcasted_iota(jnp.int32, parts[0].shape, 0)
    tile = sub_roll(parts[0], -at)
    for i in range(1, len(parts)):
        tile = jnp.where(row >= 2 * i, sub_roll(parts[i], 2 * i - at), tile)
    return tile


def unpack(after, before, i):
    row = lax.broadcasted_iota(jnp.int32, after.shape, 0)
    return jnp.where(row < 4, sub_roll(after, -2 * i), sub_roll(before, 6 - 2 * i))


def snake(chip):
    z, x = chip // 4, lax.rem(chip, 4)
    return z * 4 + jnp.where(lax.rem(z, 2) == 0, x, 3 - x)


def owner(s, i):
    o = jnp.where(lax.rem(s, 2) == 0, i, 31 - i)
    return snake(o // 2) * 2 + lax.rem(o, 2)


def owned(s, tm):
    o = snake(tm // 2) * 2 + lax.rem(tm, 2)
    return jnp.where(lax.rem(s, 2) == 0, o, 31 - o)


def coarse_kernel(
    points, init, depth,
    boosted, other, esum, partial, vout, drow,
    s0, a1, a2, ps, pr, fs, fr, s0r, q1, s1, q2, q3, q3s, q3r, br, item, ritem,
    rt, et, dr, dt, ex, vx, vt, vr,
    st_s, st_r, pk_s, pk_r, q3_ss, q3_rs, it_s, it_r, oth_s, oth_r, one_s, one_r, dep_s, dep_r, two_s, two_r,
    halo_s, halo_r, ret_s, ret_r, row_s, row_r, fin_s, fin_r,
):
    tm = lax.axis_index("tm")
    s = lax.axis_index("space")
    chip, k = tm // 2, lax.rem(tm, 2)
    mine = owned(s, tm)
    half, spot = mine // 16, lax.rem(mine, 16)
    s_next, s_prev = lax.rem(s + 1, SPACE), lax.rem(s + SPACE - 1, SPACE)
    tm_next, tm_prev = lax.rem(tm + 1, 32), lax.rem(tm + 31, 32)
    first = jnp.where(tm == 0, 1.0, 0.0).astype(F32)
    even = jnp.where(k == 0, step_size, 0.0).astype(F32)

    def at(t, sp):
        return {"tm": t, "space": sp}

    def near(step):
        p = lax.rem(32 * s + mine + step + 256, 256)
        return at(owner(p // 32, lax.rem(p, 32)), p // 32)

    partner = at(chip * 2 + 1 - k, s)
    nears = [near(1), near(-1), near(2), near(-2)]

    vt[...] = jnp.zeros_like(vt)
    barrier = pltpu.get_barrier_semaphore()
    peers = [at(lax.rem(tm + d, 32), s) for d in range(1, 32)]
    peers += [at(tm, lax.rem(s + d, SPACE)) for d in range(1, SPACE)]
    peers += [at(t, sp) for t in (tm_next, tm_prev) for sp in (s_next, s_prev)]
    peers += nears
    for p in peers:
        pl.semaphore_signal(barrier, inc=1, device_id=p, device_id_type=MESH)
    pl.semaphore_wait(barrier, len(peers))

    def copy(src, dst, ss, rs, dev):
        return pltpu.make_async_remote_copy(src_ref=src, dst_ref=dst, send_sem=ss, recv_sem=rs, device_id=dev, device_id_type=MESH)

    def block(sp, kk):
        return pl.ds(pl.multiple_of(512 * sp + 256 * kk, PART), PART)

    def rows(start, n=ROWS):
        return pl.ds(pl.multiple_of(start, 8), n)

    start = copy(points.at[6:9], s0, st_s.at[0], st_r.at[0], at(tm_next, s))

    @pl.when(tm < 31)
    def _():
        start.start()

    def prepare(base):
        cols = pl.ds(base, CHUNK)
        top, bottom = [], []
        for f in range(3):
            p0, p1, p2 = (points[3 * m + f, :, cols] for m in range(3))
            x = (step_size * quad_near - half_step) * p0 + (step_size * quad_mid) * p1 + (step_size * quad_far) * p2
            y = (step_size * quad_far) * p0 + (step_size * quad_mid - half_step) * p1 + (step_size * quad_near) * p2
            a1[f, :, cols] = x
            a2[f, :, cols] = y
            top.append((x[:8], y[:8]))
            bottom.append((x[8:], y[8:]))
        for n, (parts, row) in enumerate(((bottom, 6), (top, 0))):
            ps[n, 0, :, cols] = pack([p[0] for p in parts] + [parts[0][1]], row)
            ps[n, 1, :, cols] = pack([parts[1][1], parts[2][1]], row)
            tile = pl.ds(8, 8) if n == 0 else pl.ds(0, 8)
            ends = [jnp.where(tm == 31, init[f, tile, cols], points[6 + f, tile, cols]) for f in range(3)]
            fs[n, :, cols] = pack(ends + [depth[tile, cols]], row)

    chunks(prepare)
    packs = [
        (ps.at[0], pr.at[0], at(tm, s_next)),
        (ps.at[1], pr.at[1], at(tm, s_prev)),
        (fs.at[0], fr.at[0], at(tm_next, s_next)),
        (fs.at[1], fr.at[1], at(tm_next, s_prev)),
    ]
    packs = [copy(src, dst, pk_s.at[n], pk_r.at[n], dev) for n, (src, dst, dev) in enumerate(packs)]
    for c in packs:
        c.start()

    def depth_pieces(base):
        return (
            (pl.ds(pl.multiple_of(base, 128), PART), pl.ds(128, PART)),
            (pl.ds(pl.multiple_of(lax.rem(base + COLS - 128, COLS), 128), 128), pl.ds(0, 128)),
            (pl.ds(pl.multiple_of(lax.rem(base + PART, COLS), 128), 128), pl.ds(384, 128)),
        )

    def depth_copy(d, n, send):
        sp = lax.rem(s + d, SPACE) if send else lax.rem(s + SPACE - d, SPACE)
        to = sp if send else s
        src, dst = depth_pieces(512 * to + 256 * (owned(to, tm) // 16))[n]
        return copy(depth.at[:, src], dr.at[rows(ROWS * (s if send else sp)), dst], dep_s.at[n, d], dep_r.at[n, d], at(tm, sp))

    for d in range(1, SPACE):
        for n in range(3):
            depth_copy(d, n, True).start()
    for src, dst in depth_pieces(512 * s + 256 * half):
        dr[rows(ROWS * s), dst] = depth[:, src]

    for n, dev in enumerate((at(tm, s_prev), at(tm, s_next), at(tm_prev, s_prev), at(tm_prev, s_next))):
        src, dst = ((ps.at[n], pr.at[n]), (fs.at[n - 2], fr.at[n - 2]))[n // 2]
        copy(src, dst, pk_s.at[n], pk_r.at[n], dev).wait_recv()

    @pl.when(tm > 0)
    def _():
        copy(points.at[6:9], s0, st_s.at[0], st_r.at[0], at(tm_prev, s)).wait_recv()

    def ringed(base):
        cols = pl.ds(base, CHUNK)
        drow[:, cols] = jnp.concatenate([depth[:, cols], unpack(fr[1, :, cols], fr[0, :, cols], 3)], axis=0)
        for f in range(3):
            main = jnp.where(tm == 0, init[f, :, cols], s0[f, :, cols])
            x = jnp.concatenate([main, unpack(fr[1, :, cols], fr[0, :, cols], f)], axis=0)
            y = jnp.concatenate([a1[f, :, cols], unpack(pr[1, 0, :, cols], pr[0, 0, :, cols], f)], axis=0)
            s0r[f, :, cols] = x
            q1[f, :, cols] = half_step * x + y

    chunks(ringed)

    def one(base):
        cols = pl.ds(base, CHUNK)
        r = ring_rates(q1, drow, base)
        for f in range(3):
            x = s0r[f, :, cols] + r[f]
            tile, i = (0, 3) if f == 0 else (1, f - 1)
            y = jnp.concatenate([a2[f, :, cols], unpack(pr[1, tile, :, cols], pr[0, tile, :, cols], i)], axis=0)
            s1[f, :, cols] = x
            q2[f, :, cols] = half_step * x + y

    chunks(one)

    def two(base):
        cols = pl.ds(base, CHUNK)
        r = ring_rates(q2, drow, base)
        top, bottom = [], []
        for f in range(3):
            x, y = s0r[f, :ROWS, cols], s1[f, :ROWS, cols]
            z = y + r[f][:ROWS]
            partial[f, :, cols] = y - 0.5 * (x + z)
            q = (step_size * first + start_share) * x + one_share * y + two_share * z
            q3[f, :ROWS, cols] = q
            top.append(q[:8])
            bottom.append(q[8:])
        q3s[0, :, cols] = pack(bottom, 6)
        q3s[1, :, cols] = pack(top, 0)

    chunks(two)
    for n, sp in enumerate((s_next, s_prev)):
        copy(q3s.at[n], q3r.at[n], q3_ss.at[n], q3_rs.at[n], at(tm, sp)).start()

    for d in range(1, SPACE):
        for n in range(3):
            depth_copy(d, n, False).wait_recv()
    for t in range(4):
        dt[128 * t : 128 * t + 128, :] = dr[:, 128 * t : 128 * t + 128].T

    for n, sp in enumerate((s_prev, s_next)):
        copy(q3s.at[n], q3r.at[n], q3_ss.at[n], q3_rs.at[n], at(tm, sp)).wait_recv()

    def edge_rows(base):
        cols = pl.ds(base, CHUNK)
        for f in range(3):
            q3[f, ROWS:, cols] = unpack(q3r[1, :, cols], q3r[0, :, cols], f)

    chunks(edge_rows)

    def three(base):
        cols = pl.ds(base, CHUNK)
        r = ring_rates(q3, drow, base)
        for f in range(3):
            x = r[f] + first * s0r[f, :, cols]
            br[f, :, cols] = x
            boosted[f, :, cols] = x[:ROWS]

    chunks(three)
    give = copy(boosted, other, oth_s.at[0], oth_r.at[0], partner)
    give.start()

    def item_copy(i):
        cols = pl.ds(pl.multiple_of(i * CHUNK, CHUNK), CHUNK)
        return copy(item.at[:, :, cols], ritem.at[:, :, cols], it_s.at[i], it_r.at[i], partner)

    @pl.loop(0, COLS // CHUNK)
    def _(i):
        base = pl.multiple_of(i * CHUNK, CHUNK)
        cols = pl.ds(base, CHUNK)
        r = ring_rates(br, drow, base)
        for f in range(3):
            item[f, :, cols] = br[f, :ROWS, cols] + even * r[f][:ROWS]
        item_copy(i).start()

    def one_copy(sp, send):
        to, by = (sp, s) if send else (s, sp)
        n = to if send else by
        return copy(esum.at[:, :, block(to, k)], rt.at[:, rows(ROWS * by), :], one_s.at[n], one_r.at[by], at(tm, sp))

    @pl.loop(0, SPACE)
    def _(d):
        sp = lax.rem(s + d + 1, SPACE)
        cols = pl.ds(pl.multiple_of(sp * CHUNK, CHUNK), CHUNK)
        item_copy(sp).wait_recv()
        for f in range(3):
            esum[f, :, cols] = item[f, :, cols] + ritem[f, :, cols]

        @pl.when(sp != s)
        def _():
            one_copy(sp, True).start()

    rt[:, rows(ROWS * s), :] = esum[:, :, block(s, k)]
    for d in range(1, SPACE):
        one_copy(lax.rem(s + SPACE - d, SPACE), False).wait_recv()
    for f in range(3):
        for t in range(2):
            et[f, 128 * t : 128 * t + 128, :] = rt[f, :, 128 * t : 128 * t + 128].T

    def two_copy(n):
        return copy(et.at[:, rows(OWN * n, OWN), :], ex.at[chip, :, pl.ds(HALO, OWN), :], two_s.at[n], two_r.at[chip], at(owner(s, 16 * k + n), s))

    @pl.loop(0, 16)
    def _(m):
        n = lax.rem(m + spot, 16)
        to = owner(s, 16 * k + n)

        @pl.when(to != tm)
        def _():
            two_copy(n).start()

    @pl.when(half == k)
    def _():
        ex[chip, :, HALO : HALO + OWN, :] = et[:, rows(OWN * spot, OWN), :]

    def halo_copy(n, j, width):
        hop, sign = n // 2 + 1, 1 - 2 * (n % 2)
        far = OWN * (hop - 1)
        if sign > 0:
            src, dst = HALO + OWN - width, HALO - far - width
        else:
            src, dst = HALO, HALO + OWN + far
        return copy(ex.at[j, :, pl.ds(src, width), :], ex.at[j, :, pl.ds(dst, width), :], halo_s.at[n, j], halo_r.at[n, j], nears[n])

    def each_halo(j, act):
        for lo, hi, ns, width in ((0, 10, (0, 1), 16), (10, 14, (0, 1), 8), (0, 2, (2, 3), 16), (2, 6, (2, 3), 8)):
            @pl.when((j >= lo) & (j < hi))
            def _():
                for n in ns:
                    act(halo_copy(n, j, width))

    @pl.loop(0, CHIPS)
    def _(d):
        c = lax.rem(chip + d, CHIPS)

        @pl.when((c != chip) | (half != k))
        def _():
            src = et.at[:, rows(OWN * spot, OWN), :]
            copy(src, ex.at[c, :, pl.ds(HALO, OWN), :], two_s.at[0], two_r.at[c], at(c * 2 + half, s)).wait_recv()

        each_halo(c, lambda x: x.start())

    d_own = dt[rows(96 + OWN * spot, WIDE), :]

    def stepped(state):
        h, u, v = state
        r = rates(
            h, u, v, d_own * u, d_own * v,
            lambda x: pltpu.roll(x, 1, 0), lambda x: pltpu.roll(x, WIDE - 1, 0),
            lambda x: pltpu.roll(x, 1, 1), lambda x: pltpu.roll(x, 127, 1), lambda x: x,
        )
        return tuple(x + step_size * y for x, y in zip(state, r))

    def ret_copy(j):
        return copy(vx.at[j], vt.at[:, rows(OWN * spot, OWN), :], ret_s.at[j], ret_r.at[spot], at(j * 2 + half, s))

    def body(j, state):
        state = stepped(stepped(state))
        each_halo(j, lambda x: x.wait_recv())
        state = tuple(x + ex[j, f] for f, x in enumerate(state))
        for f in range(3):
            vx[j + 1, f] = state[f][HALO : HALO + OWN]

        @pl.when((chip != j + 1) | (half != k))
        def _():
            ret_copy(j + 1).start()

        return state

    empty = jnp.zeros((WIDE, 128), F32)
    lax.fori_loop(0, CHIPS - 1, body, (empty, empty, empty))

    @pl.when(chip > 0)
    def _():
        @pl.when(half == k)
        def _():
            vt[:, rows(OWN * spot, OWN), :] = vx[chip]

        @pl.loop(0, 16)
        def _(n):
            t = owner(s, 16 * k + n)

            @pl.when(t != tm)
            def _():
                copy(vx.at[0], vt.at[:, rows(OWN * n, OWN), :], ret_s.at[0], ret_r.at[n], at(t, s)).wait_recv()

    low = lax.broadcasted_iota(jnp.int32, (8, 128), 0) < 4
    for f in range(3):
        for t in range(2):
            cols = slice(128 * t, 128 * t + 128)
            x = vt[f, cols, :].T
            for sp in range(SPACE):
                vr[sp, f, :ROWS, cols] = x[16 * sp : 16 * sp + 16]
                a, b = (16 * sp + 16) % 128, (16 * sp + 120) % 128
                vr[sp, f, ROWS:, cols] = jnp.where(low, x[a : a + 8], x[b : b + 8])

    def row_copy(sp, send):
        to, by = (sp, s) if send else (s, sp)
        return copy(vr.at[to], vout.at[:, :, block(by, k)], row_s.at[sp], row_r.at[by], at(tm, sp))

    def fin_copy(sp, send):
        cols = block(sp, k if send else 1 - k)
        return copy(vout.at[:, :, cols], vout.at[:, :, cols], fin_s.at[sp], fin_r.at[sp], partner)

    for d in range(1, SPACE):
        row_copy(lax.rem(s + d, SPACE), True).start()
    vout[:, :, block(s, k)] = vr[s]
    fin_copy(s, True).start()
    for d in range(1, SPACE):
        sp = lax.rem(s + SPACE - d, SPACE)
        row_copy(sp, False).wait_recv()
        fin_copy(sp, True).start()
    give.wait_recv()
    for sp in range(SPACE):
        fin_copy(sp, False).wait_recv()

    @pl.when(tm < 31)
    def _():
        start.wait_send()

    for c in packs:
        c.wait_send()
    for n, sp in enumerate((s_next, s_prev)):
        copy(q3s.at[n], q3r.at[n], q3_ss.at[n], q3_rs.at[n], at(tm, sp)).wait_send()
    give.wait_send()
    for i in range(COLS // CHUNK):
        item_copy(i).wait_send()
    for d in range(1, SPACE):
        for n in range(3):
            depth_copy(d, n, True).wait_send()
        one_copy(lax.rem(s + d, SPACE), True).wait_send()
        row_copy(lax.rem(s + d, SPACE), True).wait_send()
    for sp in range(SPACE):
        fin_copy(sp, True).wait_send()

    @pl.loop(0, 16)
    def _(n):
        @pl.when(owner(s, 16 * k + n) != tm)
        def _():
            two_copy(n).wait_send()

        each_halo(n, lambda x: x.wait_send())

        @pl.when((n > 0) & ((chip != n) | (half != k)))
        def _():
            ret_copy(n).wait_send()


def final_kernel(v, boosted, other, esum, partial, init, depth, out):
    slot = lax.axis_index("tm")
    even = lax.rem(slot, 2) == 0
    first = slot == 0

    def body(base):
        cols = pl.ds(base, CHUNK)
        d = wide(lambda c: depth[:, c], base)

        def stepped(state):
            h, u, w = state
            r = rates(h, u, w, d * u, d * w, left, right, up, down, lambda x: x)
            return [x + step_size * y for x, y in zip(state, r)]

        state = [wide(lambda c, f=f: v[f, :, c], base) for f in range(3)]
        a = stepped(state)
        b = stepped(a)
        for f in range(3):
            begin = inner(state[f])[:ROWS]
            ours = jnp.where(even, boosted[f, :, cols], other[f, :, cols])
            y1 = ours + inner(a[f])[:ROWS]
            y2 = esum[f, :, cols] + inner(b[f])[:ROWS]
            start = jnp.where(even, jnp.where(first, init[f, :, cols], begin), y1)
            end = jnp.where(even, y1, y2)
            out[0, f, :, cols] = start
            out[1, f, :, cols] = partial[f, :, cols] + 0.5 * (start + end)
            out[2, f, :, cols] = end

    chunks(body)


VM = pl.BlockSpec(memory_space=pltpu.VMEM)


def per_device(fine_nodes, init_state, mean_depth):
    points = fine_nodes[0].reshape(9, ROWS, COLS)
    state = jax.ShapeDtypeStruct((3, ROWS, COLS), F32)
    ring = jax.ShapeDtypeStruct((3, RING, COLS), F32)

    def vm(*shape):
        return pltpu.VMEM(shape, F32)

    def sems(*shape):
        return [pltpu.SemaphoreType.DMA(shape)] * 2

    flat, ringed = vm(3, ROWS, COLS), vm(3, RING, COLS)
    boosted, other, esum, partial, v, depth = pl.pallas_call(
        coarse_kernel,
        out_shape=[state, state, state, state, ring, jax.ShapeDtypeStruct((RING, COLS), F32)],
        in_specs=[VM] * 3,
        out_specs=[VM] * 6,
        scratch_shapes=[
            flat, flat, flat, vm(2, 2, 8, COLS), vm(2, 2, 8, COLS), vm(2, 8, COLS), vm(2, 8, COLS),
            ringed, ringed, ringed, ringed, ringed, vm(2, 8, COLS), vm(2, 8, COLS), ringed, flat, flat,
            vm(3, 128, PART), vm(3, PART, 128), vm(128, 512), vm(512, 128),
            vm(CHIPS, 3, WIDE, 128), vm(CHIPS, 3, OWN, 128), vm(3, PART, 128), vm(SPACE, 3, RING, PART),
            *sems(1), *sems(4), *sems(2), *sems(8), *sems(1), *sems(8), *sems(3, 8), *sems(16),
            *sems(4, 16), *sems(16), *sems(8), *sems(8),
        ],
        compiler_params=pltpu.CompilerParams(collective_id=0, has_side_effects=True),
        name="sweep",
    )(points, init_state, mean_depth)

    out = pl.pallas_call(
        final_kernel,
        out_shape=jax.ShapeDtypeStruct((3, 3, ROWS, COLS), F32),
        in_specs=[VM] * 7,
        out_specs=VM,
        name="final",
    )(v, boosted, other, esum, partial, init_state, depth)
    return out[None]


def solution(mesh):
    placed = (P("tm", None, None, "space", None), P(None, "space", None), P("space", None))
    return jax.shard_map(
        per_device,
        mesh=mesh,
        in_specs=placed,
        out_specs=P("tm", None, None, "space", None),
        check_vma=False,
    )
```

time: 767 us -> 134 us (0.17)
  the two profiles are of different devices: /device:TPU:192 before, /device:TPU:1 now
where the time goes in v2:
time: 134 us
  Pallas kernels  134 us (100%)
    pallas_call x1, Pallas kernels, per_device(): pl.pallas_call(coarse_kernel, out_shape=[state, state, state, state, ring...  127 us
    pallas_call x1, Pallas kernels, per_device(): pl.pallas_call(final_kernel, out_shape=jax.ShapeDtypeStruct((3, 3, ROWS,...  6.72 us

profile of v2, /device:TPU:1, one launch (start us, length us, event | category | flops | bytes accessed | tf_op | source)
XLA Modules:
  0.0 133.7 jit_solution(3806759284424884418)
XLA Ops:
  0.0 127.0 %sweep.1 = (f32[3,16,4096]{2,1,0:T(8,128)}, f32[3,16,4096]{2,1,0:T(8,128)}, f32[3,16,4096]{2,1,0:T(8,128)}, f32[3,16,4096]{2,1,0:T(8,128)}, f32[3,24,4096]{2,1,0:T(8,128)}, /*index=5*/f32[24,4096]{1,0:T(8,128)}) custom-call(f32[9,16,4096]{2,1,0:T(8,128)} %bitcast.2, f32[3,16,4096]{2,1,0:T(8,128)} %init.3, f32[16,4096]{1,0:T(8,128)} %depth.1), custom_call_target="tpu_custom_call" | custom-call | tf_op jit(solution)/shard_map/sweep/pallas_call | solution.py:535
  127.0 6.7 %final.1 = f32[3,3,16,4096]{3,2,1,0:T(8,128)} custom-call(f32[3,24,4096]{2,1,0:T(8,128)} %get-tuple-element.11.v, f32[3,16,4096]{2,1,0:T(8,128)} %get-tuple-element.12.boosted, f32[3,16,4096]{2,1,0:T(8,128)} %get-tuple-element.13.other, f32[3,16,4096]{2,1,0:T(8,128)} %get-tuple-element.14.esum, f32[3,16,4096]{2,1,0:T(8,128)} %get-tuple-element.15.partial, ...), custom_call_target="tpu_custom_call" | custom-call | tf_op jit(solution)/shard_map/final/pallas_call | solution.py:552

commit v3 on v2

--- a/solution.py
+++ b/solution.py
@@ -87,6 +87,17 @@
         body(pl.multiple_of(i * CHUNK, CHUNK))
 
 
+PAIRS = COLS // CHUNK // 2
+FOLD = COLS // 2
+
+
+def pairs(body):
+    @pl.loop(0, PAIRS)
+    def _(j):
+        base = pl.multiple_of(j * CHUNK, CHUNK)
+        body(j, pl.ds(base, CHUNK), [base, pl.multiple_of(base + FOLD, CHUNK)])
+
+
 def sub_roll(x, by):
     by %= 8
     return x if by == 0 else pltpu.roll(x, by, 0)
@@ -100,6 +111,24 @@
     return tile
 
 
+def place(parts, at):
+    row = lax.broadcasted_iota(jnp.int32, parts[0].shape, 0)
+    tile = sub_roll(parts[0], -at[0])
+    for i in range(1, len(parts)):
+        tile = jnp.where(row >= i, sub_roll(parts[i], i - at[i]), tile)
+    return tile
+
+
+def fold(first, second):
+    row = lax.broadcasted_iota(jnp.int32, first.shape, 0)
+    return jnp.where(row < 4, first, sub_roll(second, 4))
+
+
+def unfold(after, before, i):
+    row = lax.broadcasted_iota(jnp.int32, after.shape, 0)
+    return jnp.where(row < 4, sub_roll(after, -i), sub_roll(before, 7 - i))
+
+
 def unpack(after, before, i):
     row = lax.broadcasted_iota(jnp.int32, after.shape, 0)
     return jnp.where(row < 4, sub_roll(after, -2 * i), sub_roll(before, 6 - 2 * i))
@@ -123,9 +152,9 @@
 def coarse_kernel(
     points, init, depth,
     boosted, other, esum, partial, vout, drow,
-    s0, a1, a2, ps, pr, fs, fr, s0r, q1, s1, q2, q3, q3s, q3r, br, item, ritem,
+    s0, a1, a2, ps, pr, fs, fr, s0r, q1, s1, q2, q2s, q2r, q3, q3s, q3r, br, item, ritem, relay,
     rt, et, dr, dt, ex, vx, vt, vr,
-    st_s, st_r, pk_s, pk_r, q3_ss, q3_rs, it_s, it_r, oth_s, oth_r, one_s, one_r, dep_s, dep_r, two_s, two_r,
+    st_s, st_r, rl_s, rl_r, pk_s, pk_r, q2_ss, q2_rs, q3_ss, q3_rs, it_s, it_r, oth_s, oth_r, one_s, one_r, dep_s, dep_r, two_s, two_r,
     halo_s, halo_r, ret_s, ret_r, row_s, row_r, fin_s, fin_r,
 ):
     tm = lax.axis_index("tm")
@@ -167,40 +196,69 @@
     def rows(start, n=ROWS):
         return pl.ds(pl.multiple_of(start, 8), n)
 
-    start = copy(points.at[6:9], s0, st_s.at[0], st_r.at[0], at(tm_next, s))
+    z_place = lax.rem(tm, 8)
+    far_end = (z_place == 7) & (tm < 31)
+    relays = (z_place == 1) & (tm < 24)
+    QUARTER = COLS // 4
+
+    def start_copy(n, to, via=False):
+        cols = pl.ds(QUARTER * n, QUARTER)
+        if via:
+            return copy(points.at[6:9, :, cols], relay.at[n - 2], st_s.at[n], rl_r.at[n - 2], at(to, s))
+        return copy(points.at[6:9, :, cols], s0.at[:, :, cols], st_s.at[n], st_r.at[n], at(to, s))
+
+    def pass_copy(n):
+        return copy(relay.at[n], s0.at[:, :, pl.ds(QUARTER * (n + 2), QUARTER)], rl_s.at[n], st_r.at[n + 2], at(lax.rem(tm + 7, 32), s))
 
     @pl.when(tm < 31)
     def _():
-        start.start()
-
-    def prepare(base):
-        cols = pl.ds(base, CHUNK)
-        top, bottom = [], []
-        for f in range(3):
-            p0, p1, p2 = (points[3 * m + f, :, cols] for m in range(3))
-            x = (step_size * quad_near - half_step) * p0 + (step_size * quad_mid) * p1 + (step_size * quad_far) * p2
-            y = (step_size * quad_far) * p0 + (step_size * quad_mid - half_step) * p1 + (step_size * quad_near) * p2
-            a1[f, :, cols] = x
-            a2[f, :, cols] = y
-            top.append((x[:8], y[:8]))
-            bottom.append((x[8:], y[8:]))
-        for n, (parts, row) in enumerate(((bottom, 6), (top, 0))):
-            ps[n, 0, :, cols] = pack([p[0] for p in parts] + [parts[0][1]], row)
-            ps[n, 1, :, cols] = pack([parts[1][1], parts[2][1]], row)
-            tile = pl.ds(8, 8) if n == 0 else pl.ds(0, 8)
-            ends = [jnp.where(tm == 31, init[f, tile, cols], points[6 + f, tile, cols]) for f in range(3)]
-            fs[n, :, cols] = pack(ends + [depth[tile, cols]], row)
-
-    chunks(prepare)
-    packs = [
-        (ps.at[0], pr.at[0], at(tm, s_next)),
-        (ps.at[1], pr.at[1], at(tm, s_prev)),
-        (fs.at[0], fr.at[0], at(tm_next, s_next)),
-        (fs.at[1], fr.at[1], at(tm_next, s_prev)),
-    ]
-    packs = [copy(src, dst, pk_s.at[n], pk_r.at[n], dev) for n, (src, dst, dev) in enumerate(packs)]
-    for c in packs:
-        c.start()
+        for n in range(2):
+            start_copy(n, tm_next).start()
+
+    @pl.when((tm < 31) & (z_place != 7))
+    def _():
+        for n in range(2, 4):
+            start_copy(n, tm_next).start()
+
+    @pl.when(far_end)
+    def _():
+        for n in range(2, 4):
+            start_copy(n, lax.rem(tm + 26, 32), True).start()
+
+    def pack_copy(n, j, send):
+        up_down = lax.rem(s + (1 if (n % 2 == 0) == send else SPACE - 1), SPACE)
+        slot = tm if n < 2 else (tm_next if send else tm_prev)
+        cols = pl.ds(pl.multiple_of(j * CHUNK, CHUNK), CHUNK)
+        src, dst = (ps, pr) if n < 2 else (fs, fr)
+        return copy(src.at[n % 2, :, cols], dst.at[n % 2, :, cols], pk_s.at[n, j], pk_r.at[n, j], at(slot, up_down))
+
+    def prepare(j, folded, bases):
+        tiles = [[], []], [[], []]
+        for base in bases:
+            cols = pl.ds(base, CHUNK)
+            top, bottom = [], []
+            for f in range(3):
+                p0, p1, p2 = (points[3 * m + f, :, cols] for m in range(3))
+                x = (step_size * quad_near - half_step) * p0 + (step_size * quad_mid) * p1 + (step_size * quad_far) * p2
+                y = (step_size * quad_far) * p0 + (step_size * quad_mid - half_step) * p1 + (step_size * quad_near) * p2
+                a1[f, :, cols] = x
+                a2[f, :, cols] = y
+                top.append(x[:8])
+                bottom.append(x[8:])
+            for n, (parts, tile, row, inside) in enumerate(((bottom, 8, 7, 6), (top, 0, 0, 1))):
+                d = depth[tile : tile + 8, cols]
+                ends = [
+                    jnp.where(tm == 31, init[f, tile : tile + 8, cols], points[6 + f, tile : tile + 8, cols]) for f in range(3)
+                ]
+                tiles[0][n].append(place(parts + [d], [row] * 4))
+                tiles[1][n].append(place(ends + [d], [row] * 3 + [inside]))
+        for n in range(2):
+            ps[n, :, folded] = fold(*tiles[0][n])
+            fs[n, :, folded] = fold(*tiles[1][n])
+        for n in range(4):
+            pack_copy(n, j, True).start()
+
+    pairs(prepare)
 
     def depth_pieces(base):
         return (
@@ -221,44 +279,86 @@
     for src, dst in depth_pieces(512 * s + 256 * half):
         dr[rows(ROWS * s), dst] = depth[:, src]
 
-    for n, dev in enumerate((at(tm, s_prev), at(tm, s_next), at(tm_prev, s_prev), at(tm_prev, s_next))):
-        src, dst = ((ps.at[n], pr.at[n]), (fs.at[n - 2], fr.at[n - 2]))[n // 2]
-        copy(src, dst, pk_s.at[n], pk_r.at[n], dev).wait_recv()
+    @pl.when(relays)
+    def _():
+        for n in range(2):
+            start_copy(n + 2, lax.rem(tm + 6, 32), True).wait_recv()
+            pass_copy(n).start()
+
+    for n in range(4):
+        for j in range(PAIRS):
+            pack_copy(n, j, False).wait_recv()
 
     @pl.when(tm > 0)
     def _():
-        copy(points.at[6:9], s0, st_s.at[0], st_r.at[0], at(tm_prev, s)).wait_recv()
-
-    def ringed(base):
-        cols = pl.ds(base, CHUNK)
-        drow[:, cols] = jnp.concatenate([depth[:, cols], unpack(fr[1, :, cols], fr[0, :, cols], 3)], axis=0)
-        for f in range(3):
-            main = jnp.where(tm == 0, init[f, :, cols], s0[f, :, cols])
-            x = jnp.concatenate([main, unpack(fr[1, :, cols], fr[0, :, cols], f)], axis=0)
-            y = jnp.concatenate([a1[f, :, cols], unpack(pr[1, 0, :, cols], pr[0, 0, :, cols], f)], axis=0)
-            s0r[f, :, cols] = x
-            q1[f, :, cols] = half_step * x + y
-
-    chunks(ringed)
-
-    def one(base):
-        cols = pl.ds(base, CHUNK)
-        r = ring_rates(q1, drow, base)
-        for f in range(3):
-            x = s0r[f, :, cols] + r[f]
-            tile, i = (0, 3) if f == 0 else (1, f - 1)
-            y = jnp.concatenate([a2[f, :, cols], unpack(pr[1, tile, :, cols], pr[0, tile, :, cols], i)], axis=0)
-            s1[f, :, cols] = x
-            q2[f, :, cols] = half_step * x + y
-
-    chunks(one)
-
-    def two(base):
+        for n in range(4):
+            start_copy(n, tm_prev).wait_recv()
+
+    def ringed(j, folded, bases):
+        row = lax.broadcasted_iota(jnp.int32, (8, CHUNK), 0)
+        for h, base in enumerate(bases):
+            cols = pl.ds(base, CHUNK)
+            pa, pb, fa, fb = pr[1, :, folded], pr[0, :, folded], fr[1, :, folded], fr[0, :, folded]
+            i = 4 * h + 3
+            d = jnp.where(row < 4, sub_roll(fa, 1 - i), sub_roll(fb, 6 - i))
+            d = jnp.where((row == 0) | (row == 7), unfold(pa, pb, i), d)
+            drow[:, cols] = jnp.concatenate([depth[:, cols], d], axis=0)
+            for f in range(3):
+                main = jnp.where(tm == 0, init[f, :, cols], s0[f, :, cols])
+                x = jnp.concatenate([main, unfold(fa, fb, 4 * h + f)], axis=0)
+                y = jnp.concatenate([a1[f, :, cols], unfold(pa, pb, 4 * h + f)], axis=0)
+                s0r[f, :, cols] = x
+                q1[f, :, cols] = half_step * x + y
+
+    pairs(ringed)
+
+    def q2_copy(n, j, send):
+        up_down = lax.rem(s + (1 if (n == 0) == send else SPACE - 1), SPACE)
+        cols = pl.ds(pl.multiple_of(j * CHUNK, CHUNK), CHUNK)
+        return copy(q2s.at[n, :, cols], q2r.at[n, :, cols], q2_ss.at[n, j], q2_rs.at[n, j], at(tm, up_down))
+
+    def one(j, folded, bases):
+        tiles = [[], []]
+        for base in bases:
+            cols = pl.ds(base, CHUNK)
+            r = ring_rates(q1, drow, base)
+            q = []
+            for f in range(3):
+                x = s0r[f, :ROWS, cols] + r[f][:ROWS]
+                s1[f, :, cols] = x
+                q.append(half_step * x + a2[f, :, cols])
+                q2[f, :ROWS, cols] = q[f]
+            tiles[0].append(place([x[8:] for x in q], [7] * 3))
+            tiles[1].append(place([x[:8] for x in q], [0] * 3))
+        for n in range(2):
+            q2s[n, :, folded] = fold(*tiles[n])
+            q2_copy(n, j, True).start()
+
+    pairs(one)
+    for n in range(2):
+        for j in range(PAIRS):
+            q2_copy(n, j, False).wait_recv()
+
+    def q2_rows(j, folded, bases):
+        for h, base in enumerate(bases):
+            for f in range(3):
+                q2[f, ROWS:, pl.ds(base, CHUNK)] = unfold(q2r[1, :, folded], q2r[0, :, folded], 4 * h + f)
+
+    pairs(q2_rows)
+
+    def q3_copy(n, i, send):
+        up_down = lax.rem(s + (1 if (n == 0) == send else SPACE - 1), SPACE)
+        cols = pl.ds(pl.multiple_of(i * CHUNK, CHUNK), CHUNK)
+        return copy(q3s.at[n, :, cols], q3r.at[n, :, cols], q3_ss.at[n, i], q3_rs.at[n, i], at(tm, up_down))
+
+    @pl.loop(0, COLS // CHUNK)
+    def _(i):
+        base = pl.multiple_of(i * CHUNK, CHUNK)
         cols = pl.ds(base, CHUNK)
         r = ring_rates(q2, drow, base)
         top, bottom = [], []
         for f in range(3):
-            x, y = s0r[f, :ROWS, cols], s1[f, :ROWS, cols]
+            x, y = s0r[f, :ROWS, cols], s1[f, :, cols]
             z = y + r[f][:ROWS]
             partial[f, :, cols] = y - 0.5 * (x + z)
             q = (step_size * first + start_share) * x + one_share * y + two_share * z
@@ -267,10 +367,8 @@
             bottom.append(q[8:])
         q3s[0, :, cols] = pack(bottom, 6)
         q3s[1, :, cols] = pack(top, 0)
-
-    chunks(two)
-    for n, sp in enumerate((s_next, s_prev)):
-        copy(q3s.at[n], q3r.at[n], q3_ss.at[n], q3_rs.at[n], at(tm, sp)).start()
+        for n in range(2):
+            q3_copy(n, i, True).start()
 
     for d in range(1, SPACE):
         for n in range(3):
@@ -278,8 +376,9 @@
     for t in range(4):
         dt[128 * t : 128 * t + 128, :] = dr[:, 128 * t : 128 * t + 128].T
 
-    for n, sp in enumerate((s_prev, s_next)):
-        copy(q3s.at[n], q3r.at[n], q3_ss.at[n], q3_rs.at[n], at(tm, sp)).wait_recv()
+    for i in range(COLS // CHUNK):
+        for n in range(2):
+            q3_copy(n, i, False).wait_recv()
 
     def edge_rows(base):
         cols = pl.ds(base, CHUNK)
@@ -313,41 +412,42 @@
             item[f, :, cols] = br[f, :ROWS, cols] + even * r[f][:ROWS]
         item_copy(i).start()
 
-    def one_copy(sp, send):
+    def one_copy(f, sp, send):
         to, by = (sp, s) if send else (s, sp)
         n = to if send else by
-        return copy(esum.at[:, :, block(to, k)], rt.at[:, rows(ROWS * by), :], one_s.at[n], one_r.at[by], at(tm, sp))
-
-    @pl.loop(0, SPACE)
-    def _(d):
-        sp = lax.rem(s + d + 1, SPACE)
-        cols = pl.ds(pl.multiple_of(sp * CHUNK, CHUNK), CHUNK)
-        item_copy(sp).wait_recv()
+        return copy(esum.at[f, :, block(to, k)], rt.at[f, rows(ROWS * by), :], one_s.at[f, n], one_r.at[f, by], at(tm, sp))
+
+    for i in range(COLS // CHUNK):
+        item_copy(i).wait_recv()
+
+    def summed(base):
+        cols = pl.ds(base, CHUNK)
         for f in range(3):
             esum[f, :, cols] = item[f, :, cols] + ritem[f, :, cols]
 
-        @pl.when(sp != s)
-        def _():
-            one_copy(sp, True).start()
-
+    chunks(summed)
+    for f in range(3):
+        for d in range(1, SPACE):
+            one_copy(f, lax.rem(s + d, SPACE), True).start()
     rt[:, rows(ROWS * s), :] = esum[:, :, block(s, k)]
-    for d in range(1, SPACE):
-        one_copy(lax.rem(s + SPACE - d, SPACE), False).wait_recv()
+
+    def two_copy(f, n):
+        src, dst = et.at[f, rows(OWN * n, OWN), :], ex.at[chip, f, pl.ds(HALO, OWN), :]
+        return copy(src, dst, two_s.at[f, n], two_r.at[f, chip], at(owner(s, 16 * k + n), s))
+
     for f in range(3):
+        for d in range(1, SPACE):
+            one_copy(f, lax.rem(s + SPACE - d, SPACE), False).wait_recv()
         for t in range(2):
             et[f, 128 * t : 128 * t + 128, :] = rt[f, :, 128 * t : 128 * t + 128].T
 
-    def two_copy(n):
-        return copy(et.at[:, rows(OWN * n, OWN), :], ex.at[chip, :, pl.ds(HALO, OWN), :], two_s.at[n], two_r.at[chip], at(owner(s, 16 * k + n), s))
-
-    @pl.loop(0, 16)
-    def _(m):
-        n = lax.rem(m + spot, 16)
-        to = owner(s, 16 * k + n)
-
-        @pl.when(to != tm)
-        def _():
-            two_copy(n).start()
+        @pl.loop(0, 16)
+        def _(m, f=f):
+            n = lax.rem(m + spot, 16)
+
+            @pl.when(owner(s, 16 * k + n) != tm)
+            def _():
+                two_copy(f, n).start()
 
     @pl.when(half == k)
     def _():
@@ -375,40 +475,46 @@
 
         @pl.when((c != chip) | (half != k))
         def _():
-            src = et.at[:, rows(OWN * spot, OWN), :]
-            copy(src, ex.at[c, :, pl.ds(HALO, OWN), :], two_s.at[0], two_r.at[c], at(c * 2 + half, s)).wait_recv()
+            for f in range(3):
+                src, dst = et.at[f, rows(OWN * spot, OWN), :], ex.at[c, f, pl.ds(HALO, OWN), :]
+                copy(src, dst, two_s.at[f, 0], two_r.at[f, c], at(c * 2 + half, s)).wait_recv()
 
         each_halo(c, lambda x: x.start())
 
-    d_own = dt[rows(96 + OWN * spot, WIDE), :]
-
-    def stepped(state):
-        h, u, v = state
-        r = rates(
-            h, u, v, d_own * u, d_own * v,
-            lambda x: pltpu.roll(x, 1, 0), lambda x: pltpu.roll(x, WIDE - 1, 0),
-            lambda x: pltpu.roll(x, 1, 1), lambda x: pltpu.roll(x, 127, 1), lambda x: x,
-        )
-        return tuple(x + step_size * y for x, y in zip(state, r))
+    def scanned(lo, hi, halo, state):
+        count = OWN + 2 * halo
+        d_own = dt[rows(128 - halo + OWN * spot, count), :]
+
+        def stepped(state):
+            h, u, v = state
+            r = rates(
+                h, u, v, d_own * u, d_own * v,
+                lambda x: pltpu.roll(x, 1, 0), lambda x: pltpu.roll(x, count - 1, 0),
+                lambda x: pltpu.roll(x, 1, 1), lambda x: pltpu.roll(x, 127, 1), lambda x: x,
+            )
+            return tuple(x + step_size * y for x, y in zip(state, r))
+
+        def body(j, state):
+            state = stepped(stepped(state))
+            each_halo(j, lambda x: x.wait_recv())
+            state = tuple(x + ex[j, f, HALO - halo : HALO + OWN + halo] for f, x in enumerate(state))
+            for f in range(3):
+                vx[j + 1, f] = state[f][halo : halo + OWN]
+
+            @pl.when((chip != j + 1) | (half != k))
+            def _():
+                ret_copy(j + 1).start()
+
+            return state
+
+        return lax.fori_loop(lo, hi, body, state)
 
     def ret_copy(j):
         return copy(vx.at[j], vt.at[:, rows(OWN * spot, OWN), :], ret_s.at[j], ret_r.at[spot], at(j * 2 + half, s))
 
-    def body(j, state):
-        state = stepped(stepped(state))
-        each_halo(j, lambda x: x.wait_recv())
-        state = tuple(x + ex[j, f] for f, x in enumerate(state))
-        for f in range(3):
-            vx[j + 1, f] = state[f][HALO : HALO + OWN]
-
-        @pl.when((chip != j + 1) | (half != k))
-        def _():
-            ret_copy(j + 1).start()
-
-        return state
-
-    empty = jnp.zeros((WIDE, 128), F32)
-    lax.fori_loop(0, CHIPS - 1, body, (empty, empty, empty))
+    state = scanned(0, 7, 32, (jnp.zeros((WIDE, 128), F32),) * 3)
+    state = scanned(7, 11, 16, tuple(x[16:64] for x in state))
+    scanned(11, CHIPS - 1, 8, tuple(x[8:40] for x in state))
 
     @pl.when(chip > 0)
     def _():
@@ -456,19 +562,30 @@
 
     @pl.when(tm < 31)
     def _():
-        start.wait_send()
-
-    for c in packs:
-        c.wait_send()
-    for n, sp in enumerate((s_next, s_prev)):
-        copy(q3s.at[n], q3r.at[n], q3_ss.at[n], q3_rs.at[n], at(tm, sp)).wait_send()
+        for n in range(4):
+            start_copy(n, tm_next).wait_send()
+
+    @pl.when(relays)
+    def _():
+        for n in range(2):
+            pass_copy(n).wait_send()
+
+    for n in range(4):
+        for j in range(PAIRS):
+            pack_copy(n, j, True).wait_send()
+    for n in range(2):
+        for j in range(PAIRS):
+            q2_copy(n, j, True).wait_send()
+        for i in range(COLS // CHUNK):
+            q3_copy(n, i, True).wait_send()
     give.wait_send()
     for i in range(COLS // CHUNK):
         item_copy(i).wait_send()
     for d in range(1, SPACE):
         for n in range(3):
             depth_copy(d, n, True).wait_send()
-        one_copy(lax.rem(s + d, SPACE), True).wait_send()
+        for f in range(3):
+            one_copy(f, lax.rem(s + d, SPACE), True).wait_send()
         row_copy(lax.rem(s + d, SPACE), True).wait_send()
     for sp in range(SPACE):
         fin_copy(sp, True).wait_send()
@@ -477,7 +594,8 @@
     def _(n):
         @pl.when(owner(s, 16 * k + n) != tm)
         def _():
-            two_copy(n).wait_send()
+            for f in range(3):
+                two_copy(f, n).wait_send()
 
         each_halo(n, lambda x: x.wait_send())
 
@@ -538,14 +656,15 @@
         in_specs=[VM] * 3,
         out_specs=[VM] * 6,
         scratch_shapes=[
-            flat, flat, flat, vm(2, 2, 8, COLS), vm(2, 2, 8, COLS), vm(2, 8, COLS), vm(2, 8, COLS),
-            ringed, ringed, ringed, ringed, ringed, vm(2, 8, COLS), vm(2, 8, COLS), ringed, flat, flat,
+            flat, flat, flat, vm(2, 8, FOLD), vm(2, 8, FOLD), vm(2, 8, FOLD), vm(2, 8, FOLD),
+            ringed, ringed, flat, ringed, vm(2, 8, FOLD), vm(2, 8, FOLD), ringed, vm(2, 8, COLS), vm(2, 8, COLS),
+            ringed, flat, flat, vm(2, 3, ROWS, COLS // 4),
             vm(3, 128, PART), vm(3, PART, 128), vm(128, 512), vm(512, 128),
             vm(CHIPS, 3, WIDE, 128), vm(CHIPS, 3, OWN, 128), vm(3, PART, 128), vm(SPACE, 3, RING, PART),
-            *sems(1), *sems(4), *sems(2), *sems(8), *sems(1), *sems(8), *sems(3, 8), *sems(16),
+            *sems(4), *sems(2), *sems(4, 4), *sems(2, 4), *sems(2, 8), *sems(8), *sems(1), *sems(3, 8), *sems(3, 8), *sems(3, 16),
             *sems(4, 16), *sems(16), *sems(8), *sems(8),
         ],
-        compiler_params=pltpu.CompilerParams(collective_id=0, has_side_effects=True),
+        compiler_params=pltpu.CompilerParams(collective_id=0, has_side_effects=True, vmem_limit_bytes=36 << 20),
         name="sweep",
     )(points, init_state, mean_depth)
 
@@ -554,6 +673,7 @@
         out_shape=jax.ShapeDtypeStruct((3, 3, ROWS, COLS), F32),
         in_specs=[VM] * 7,
         out_specs=VM,
+        compiler_params=pltpu.CompilerParams(vmem_limit_bytes=24 << 20),
         name="final",
     )(v, boosted, other, esum, partial, init_state, depth)
     return out[None]

time: 134 us -> 109 us (0.81)
  the two profiles are of different devices: /device:TPU:1 before, /device:TPU:231 now
where the time goes in v3:
time: 109 us; the launch traced here: 108 us
  Pallas kernels  104 us (95%)
  local copies, waits for them, and re-layouts  3.75 us (3%)
    pallas_call x1, Pallas kernels, per_device(): pl.pallas_call(coarse_kernel, out_shape=[state, state, state, state, ring...  100 us
    pallas_call x1, Pallas kernels, per_device(): pl.pallas_call(final_kernel, out_shape=jax.ShapeDtypeStruct((3, 3, ROWS,...  4.21 us
    unnamed x6, local copies, waits for them, and re-layouts  3.75 us

profile of v3, /device:TPU:231, one launch (start us, length us, event | category | flops | bytes accessed | tf_op | source)
XLA Modules:
  0.0 108.2 jit_solution(14575951064909549953)
XLA Ops:
  0.0 0.0 copy-start
  0.0 1.1 %copy-done = f32[3,16,4096]{2,1,0:T(8,128)S(1)} copy-done((f32[3,16,4096]{2,1,0:T(8,128)S(1)}, f32[3,16,4096]{2,1,0:T(8,128)}, u32[]{:S(2)}) %copy-start) | copy-done | bytes 786456
  1.1 0.0 copy-start.1
  1.1 1.7 %copy-done.1 = f32[1,3,3,16,4096]{4,3,2,1,0:T(8,128)S(1)} copy-done((f32[1,3,3,16,4096]{4,3,2,1,0:T(8,128)S(1)}, f32[1,3,3,16,4096]{4,3,2,1,0:T(8,128)}, u32[]{:S(2)}) %copy-start.1) | copy-done | bytes 2359320
  2.8 0.0 copy-start.2
  2.8 0.9 copy-done.2
  3.8 100.3 %sweep.1 = (f32[3,16,4096]{2,1,0:T(8,128)S(1)}, f32[3,16,4096]{2,1,0:T(8,128)S(1)}, f32[3,16,4096]{2,1,0:T(8,128)S(1)}, f32[3,16,4096]{2,1,0:T(8,128)S(1)}, f32[...) custom-call(f32[9,16,4096]{2,1,0:T(8,128)S(1)} %bitcast.2, f32[3,16,4096]{2,1,0:T(8,128)S(1)} %copy-done, ...), custom_call_target="tpu_custom_call" | custom-call | tf_op jit(solution)/shard_map/sweep/pallas_call | solution.py:653
  104.0 4.2 %final.1 = f32[3,3,16,4096]{3,2,1,0:T(8,128)} custom-call(f32[3,24,4096]{2,1,0:T(8,128)S(1)} %get-tuple-element.11.v, f32[3,16,4096]{2,1,0:T(8,128)S(1)} %get-tuple-element.12.boosted, f32[3,16,4096]{2,1,0:T(8,128)S(1)} %get-tuple-element.13.other, f32[3,16,4096]{2,1,0:T(8,128)S(1)} %get-tuple-element.14.esum, f32[3,16,4096]{2,1,0:T(8,128)S(1)} %get-tuple-element.15.partial, ...), custom_call_target="tpu_custom_call" | custom-call | tf_op jit(solution)/shard_map/final/pallas_call | solution.py:671
Async XLA Ops:
  0.0 1.1 %copy-start = (f32[3,16,4096]{2,1,0:T(8,128)S(1)}, f32[3,16,4096]{2,1,0:T(8,128)}, u32[]{:S(2)}) copy-start(f32[3,16,4096]{2,1,0:T(8,128)} %init.3) | copy-start | bytes 2359300
  1.1 1.7 %copy-start.1 = (f32[1,3,3,16,4096]{4,3,2,1,0:T(8,128)S(1)}, f32[1,3,3,16,4096]{4,3,2,1,0:T(8,128)}, u32[]{:S(2)}) copy-start(f32[1,3,3,16,4096]{4,3,2,1,0:T(8,128)} %param.3) | copy-start | bytes 7077892
  2.8 0.9 copy-start.2

commit v4 on v3

--- a/solution.py
+++ b/solution.py
@@ -134,27 +134,31 @@
     return jnp.where(row < 4, sub_roll(after, -2 * i), sub_roll(before, 6 - 2 * i))
 
 
-def snake(chip):
-    z, x = chip // 4, lax.rem(chip, 4)
+def snake(n):
+    z, x = n // 4, lax.rem(n, 4)
     return z * 4 + jnp.where(lax.rem(z, 2) == 0, x, 3 - x)
+
+
+def turned(s, chip):
+    return chip // 4 * 4 + lax.rem(chip + 2 * lax.rem(s, 2), 4)
 
 
 def owner(s, i):
     o = jnp.where(lax.rem(s, 2) == 0, i, 31 - i)
-    return snake(o // 2) * 2 + lax.rem(o, 2)
+    return turned(s, snake(o // 2)) * 2 + lax.rem(o, 2)
 
 
 def owned(s, tm):
-    o = snake(tm // 2) * 2 + lax.rem(tm, 2)
+    o = snake(turned(s, tm // 2)) * 2 + lax.rem(tm, 2)
     return jnp.where(lax.rem(s, 2) == 0, o, 31 - o)
 
 
 def coarse_kernel(
-    points, init, depth,
+    points_hbm, init_hbm, depth_hbm,
     boosted, other, esum, partial, vout, drow,
-    s0, a1, a2, ps, pr, fs, fr, s0r, q1, s1, q2, q2s, q2r, q3, q3s, q3r, br, item, ritem, relay,
+    points, init, depth, s0, a1, a2, ps, pr, fs, fr, s0r, q1, s1, q2, q2s, q2r, q3, q3s, q3r, br, item, ritem, relay_a, relay_b,
     rt, et, dr, dt, ex, vx, vt, vr,
-    st_s, st_r, rl_s, rl_r, pk_s, pk_r, q2_ss, q2_rs, q3_ss, q3_rs, it_s, it_r, oth_s, oth_r, one_s, one_r, dep_s, dep_r, two_s, two_r,
+    in_sem, st_s, st_r, rl_s, rl_r, pk_s, pk_r, q2_ss, q2_rs, q3_ss, q3_rs, it_s, it_r, oth_s, oth_r, one_s, one_r, dep_s, dep_r, two_s, two_r,
     halo_s, halo_r, ret_s, ret_r, row_s, row_r, fin_s, fin_r,
 ):
     tm = lax.axis_index("tm")
@@ -177,6 +181,10 @@
     partner = at(chip * 2 + 1 - k, s)
     nears = [near(1), near(-1), near(2), near(-2)]
 
+    loads = [pltpu.make_async_copy(points_hbm.at[3 * m : 3 * m + 3], points.at[3 * m : 3 * m + 3], in_sem.at[m]) for m in range(3)]
+    loads += [pltpu.make_async_copy(init_hbm, init, in_sem.at[3]), pltpu.make_async_copy(depth_hbm, depth, in_sem.at[4])]
+    for n in (2, 0, 1, 4, 3):
+        loads[n].start()
     vt[...] = jnp.zeros_like(vt)
     barrier = pltpu.get_barrier_semaphore()
     peers = [at(lax.rem(tm + d, 32), s) for d in range(1, 32)]
@@ -196,34 +204,39 @@
     def rows(start, n=ROWS):
         return pl.ds(pl.multiple_of(start, 8), n)
 
+    loads[2].wait()
+
     z_place = lax.rem(tm, 8)
     far_end = (z_place == 7) & (tm < 31)
-    relays = (z_place == 1) & (tm < 24)
-    QUARTER = COLS // 4
-
-    def start_copy(n, to, via=False):
-        cols = pl.ds(QUARTER * n, QUARTER)
-        if via:
-            return copy(points.at[6:9, :, cols], relay.at[n - 2], st_s.at[n], rl_r.at[n - 2], at(to, s))
-        return copy(points.at[6:9, :, cols], s0.at[:, :, cols], st_s.at[n], st_r.at[n], at(to, s))
-
-    def pass_copy(n):
-        return copy(relay.at[n], s0.at[:, :, pl.ds(QUARTER * (n + 2), QUARTER)], rl_s.at[n], st_r.at[n + 2], at(lax.rem(tm + 7, 32), s))
-
-    @pl.when(tm < 31)
-    def _():
-        for n in range(2):
-            start_copy(n, tm_next).start()
+    PIECE = COLS // 8
+    direct, by_a, by_b = range(0, 3), range(3, 6), range(6, 8)
+    routes = ((by_a, relay_a, 6, 1), (by_b, relay_b, 2, 5))
+
+    def piece(n):
+        return pl.ds(PIECE * n, PIECE)
+
+    def start_copy(n, to):
+        return copy(points.at[6:9, :, piece(n)], s0.at[:, :, piece(n)], st_s.at[n], st_r.at[n], at(to, s))
+
+    def via_copy(n, buffer, first_piece, to):
+        return copy(points.at[6:9, :, piece(n)], buffer.at[n - first_piece], st_s.at[n], rl_r.at[n], at(to, s))
+
+    def pass_copy(n, buffer, first_piece, ahead):
+        return copy(buffer.at[n - first_piece], s0.at[:, :, piece(n)], rl_s.at[n], st_r.at[n], at(lax.rem(tm + ahead, 32), s))
 
     @pl.when((tm < 31) & (z_place != 7))
     def _():
-        for n in range(2, 4):
+        for n in range(8):
             start_copy(n, tm_next).start()
 
     @pl.when(far_end)
     def _():
-        for n in range(2, 4):
-            start_copy(n, lax.rem(tm + 26, 32), True).start()
+        for ns, buffer, back, _ in routes:
+            for n in ns:
+                via_copy(n, buffer, ns[0], lax.rem(tm + 32 - back, 32)).start()
+
+    for n in (0, 1, 4, 3):
+        loads[n].wait()
 
     def pack_copy(n, j, send):
         up_down = lax.rem(s + (1 if (n % 2 == 0) == send else SPACE - 1), SPACE)
@@ -260,6 +273,11 @@
 
     pairs(prepare)
 
+    @pl.when(far_end)
+    def _():
+        for n in direct:
+            start_copy(n, tm_next).start()
+
     def depth_pieces(base):
         return (
             (pl.ds(pl.multiple_of(base, 128), PART), pl.ds(128, PART)),
@@ -279,11 +297,12 @@
     for src, dst in depth_pieces(512 * s + 256 * half):
         dr[rows(ROWS * s), dst] = depth[:, src]
 
-    @pl.when(relays)
-    def _():
-        for n in range(2):
-            start_copy(n + 2, lax.rem(tm + 6, 32), True).wait_recv()
-            pass_copy(n).start()
+    for ns, buffer, back, spot_of in routes:
+        @pl.when((z_place == spot_of) & (tm < 24))
+        def _(ns=ns, buffer=buffer, back=back):
+            for n in ns:
+                via_copy(n, buffer, ns[0], lax.rem(tm + back, 32)).wait_recv()
+                pass_copy(n, buffer, ns[0], back + 1).start()
 
     for n in range(4):
         for j in range(PAIRS):
@@ -291,7 +310,7 @@
 
     @pl.when(tm > 0)
     def _():
-        for n in range(4):
+        for n in range(8):
             start_copy(n, tm_prev).wait_recv()
 
     def ringed(j, folded, bases):
@@ -397,7 +416,6 @@
 
     chunks(three)
     give = copy(boosted, other, oth_s.at[0], oth_r.at[0], partner)
-    give.start()
 
     def item_copy(i):
         cols = pl.ds(pl.multiple_of(i * CHUNK, CHUNK), CHUNK)
@@ -412,6 +430,8 @@
             item[f, :, cols] = br[f, :ROWS, cols] + even * r[f][:ROWS]
         item_copy(i).start()
 
+    give.start()
+
     def one_copy(f, sp, send):
         to, by = (sp, s) if send else (s, sp)
         n = to if send else by
@@ -445,7 +465,7 @@
         def _(m, f=f):
             n = lax.rem(m + spot, 16)
 
-            @pl.when(owner(s, 16 * k + n) != tm)
+            @pl.when((owner(s, 16 * k + n) != tm) & (chip < CHIPS - 1))
             def _():
                 two_copy(f, n).start()
 
@@ -469,17 +489,17 @@
                 for n in ns:
                     act(halo_copy(n, j, width))
 
-    @pl.loop(0, CHIPS)
-    def _(d):
-        c = lax.rem(chip + d, CHIPS)
-
-        @pl.when((c != chip) | (half != k))
-        def _():
+    for c in (0, 1, 2, 5, 6, 9, 10, 13, 14, 3, 11, 7, 4, 8, 12):
+        @pl.when((chip != c) | (half != k))
+        def _(c=c):
             for f in range(3):
                 src, dst = et.at[f, rows(OWN * spot, OWN), :], ex.at[c, f, pl.ds(HALO, OWN), :]
                 copy(src, dst, two_s.at[f, 0], two_r.at[f, c], at(c * 2 + half, s)).wait_recv()
 
-        each_halo(c, lambda x: x.start())
+        for lo, hi, ns, width in ((0, 10, (0, 1), 16), (10, 14, (0, 1), 8), (0, 2, (2, 3), 16), (2, 6, (2, 3), 8)):
+            if lo <= c < hi:
+                for n in ns:
+                    halo_copy(n, c, width).start()
 
     def scanned(lo, hi, halo, state):
         count = OWN + 2 * halo
@@ -562,13 +582,14 @@
 
     @pl.when(tm < 31)
     def _():
-        for n in range(4):
+        for n in range(8):
             start_copy(n, tm_next).wait_send()
 
-    @pl.when(relays)
-    def _():
-        for n in range(2):
-            pass_copy(n).wait_send()
+    for ns, buffer, back, spot_of in routes:
+        @pl.when((z_place == spot_of) & (tm < 24))
+        def _(ns=ns, buffer=buffer, back=back):
+            for n in ns:
+                pass_copy(n, buffer, ns[0], back + 1).wait_send()
 
     for n in range(4):
         for j in range(PAIRS):
@@ -592,7 +613,7 @@
 
     @pl.loop(0, 16)
     def _(n):
-        @pl.when(owner(s, 16 * k + n) != tm)
+        @pl.when((owner(s, 16 * k + n) != tm) & (chip < CHIPS - 1))
         def _():
             for f in range(3):
                 two_copy(f, n).wait_send()
@@ -653,20 +674,21 @@
     boosted, other, esum, partial, v, depth = pl.pallas_call(
         coarse_kernel,
         out_shape=[state, state, state, state, ring, jax.ShapeDtypeStruct((RING, COLS), F32)],
-        in_specs=[VM] * 3,
+        in_specs=[pl.BlockSpec(memory_space=pltpu.HBM)] * 3,
         out_specs=[VM] * 6,
         scratch_shapes=[
+            vm(9, ROWS, COLS), flat, vm(ROWS, COLS),
             flat, flat, flat, vm(2, 8, FOLD), vm(2, 8, FOLD), vm(2, 8, FOLD), vm(2, 8, FOLD),
             ringed, ringed, flat, ringed, vm(2, 8, FOLD), vm(2, 8, FOLD), ringed, vm(2, 8, COLS), vm(2, 8, COLS),
-            ringed, flat, flat, vm(2, 3, ROWS, COLS // 4),
+            ringed, flat, flat, vm(3, 3, ROWS, COLS // 8), vm(2, 3, ROWS, COLS // 8),
             vm(3, 128, PART), vm(3, PART, 128), vm(128, 512), vm(512, 128),
             vm(CHIPS, 3, WIDE, 128), vm(CHIPS, 3, OWN, 128), vm(3, PART, 128), vm(SPACE, 3, RING, PART),
-            *sems(4), *sems(2), *sems(4, 4), *sems(2, 4), *sems(2, 8), *sems(8), *sems(1), *sems(3, 8), *sems(3, 8), *sems(3, 16),
+            pltpu.SemaphoreType.DMA((5,)), *sems(8), *sems(8), *sems(4, 4), *sems(2, 4), *sems(2, 8), *sems(8), *sems(1), *sems(3, 8), *sems(3, 8), *sems(3, 16),
             *sems(4, 16), *sems(16), *sems(8), *sems(8),
         ],
         compiler_params=pltpu.CompilerParams(collective_id=0, has_side_effects=True, vmem_limit_bytes=36 << 20),
         name="sweep",
-    )(points, init_state, mean_depth)
+    )(*(pltpu.with_memory_space_constraint(x, pltpu.HBM) for x in (points, init_state, mean_depth)))
 
     out = pl.pallas_call(
         final_kernel,

time: 109 us -> 96 us (0.88)
  Pallas kernels: 104 us -> 95.9 us
  local copies, waits for them, and re-layouts: 3.75 us -> 0.01 us
    pallas_call x1, Pallas kernels: 100 us -> 91.7 us  [per_device(): pl.pallas_call(coarse_kernel, out_shape=[state, state, state, state, ring...]
    unnamed x6 -> x2, local copies, waits for them, and re-layouts: 3.75 us -> 0.01 us
where the time goes in v4:
time: 96 us; the launch traced here: 95.9 us
  Pallas kernels  95.9 us (100%)
    pallas_call x1, Pallas kernels, per_device(): pl.pallas_call(coarse_kernel, out_shape=[state, state, state, state, ring...  91.7 us
    pallas_call x1, Pallas kernels, per_device(): pl.pallas_call(final_kernel, out_shape=jax.ShapeDtypeStruct((3, 3, ROWS,...  4.21 us

profile of v4, /device:TPU:231, one launch (start us, length us, event | category | flops | bytes accessed | tf_op | source)
XLA Modules:
  0.0 95.9 jit_solution(2882401293185227846)
XLA Ops:
  0.0 0.0 copy-start
  0.0 91.7 %sweep.1 = (f32[3,16,4096]{2,1,0:T(8,128)S(1)}, f32[3,16,4096]{2,1,0:T(8,128)S(1)}, f32[3,16,4096]{2,1,0:T(8,128)S(1)}, f32[3,16,4096]{2,1,0:T(8,128)S(1)}, f32[...) custom-call(f32[9,16,4096]{2,1,0:T(8,128)} %bitcast.2, f32[3,16,4096]{2,1,0:T(8,128)} %init.1, f32[16,4096]{1,0:T(8,128)} %depth_hbm.1), custom_call_target="tpu_custom_call" | custom-call | tf_op jit(solution)/shard_map/sweep/pallas_call | solution.py:674
  91.7 0.0 copy-done
  91.7 4.2 %final.1 = f32[3,3,16,4096]{3,2,1,0:T(8,128)} custom-call(f32[3,24,4096]{2,1,0:T(8,128)S(1)} %get-tuple-element.11.v, f32[3,16,4096]{2,1,0:T(8,128)S(1)} %get-tuple-element.12.boosted, f32[3,16,4096]{2,1,0:T(8,128)S(1)} %get-tuple-element.13.other, f32[3,16,4096]{2,1,0:T(8,128)S(1)} %get-tuple-element.14.esum, f32[3,16,4096]{2,1,0:T(8,128)S(1)} %get-tuple-element.15.partial, ...), custom_call_target="tpu_custom_call" | custom-call | tf_op jit(solution)/shard_map/final/pallas_call | solution.py:693
Async XLA Ops:
  0.0 91.7 %copy-start = (f32[3,16,4096]{2,1,0:T(8,128)S(1)}, f32[3,16,4096]{2,1,0:T(8,128)}, u32[]{:S(2)}) copy-start(f32[3,16,4096]{2,1,0:T(8,128)} %init.1) | copy-start | bytes 2359300

commit v5 on v4

--- a/solution.py
+++ b/solution.py
@@ -155,8 +155,8 @@
 
 def coarse_kernel(
     points_hbm, init_hbm, depth_hbm,
-    boosted, other, esum, partial, vout, drow,
-    points, init, depth, s0, a1, a2, ps, pr, fs, fr, s0r, q1, s1, q2, q2s, q2r, q3, q3s, q3r, br, item, ritem, relay_a, relay_b,
+    out,
+    boosted, other, esum, partial, vout, drow, points, init, depth, s0, a1, a2, ps, pr, fs, fr, s0r, q1, s1, q2, q2s, q2r, q3, q3s, q3r, br, item, ritem, relay_a, relay_b,
     rt, et, dr, dt, ex, vx, vt, vr,
     in_sem, st_s, st_r, rl_s, rl_r, pk_s, pk_r, q2_ss, q2_rs, q3_ss, q3_rs, it_s, it_r, oth_s, oth_r, one_s, one_r, dep_s, dep_r, two_s, two_r,
     halo_s, halo_r, ret_s, ret_r, row_s, row_r, fin_s, fin_r,
@@ -169,7 +169,6 @@
     s_next, s_prev = lax.rem(s + 1, SPACE), lax.rem(s + SPACE - 1, SPACE)
     tm_next, tm_prev = lax.rem(tm + 1, 32), lax.rem(tm + 31, 32)
     first = jnp.where(tm == 0, 1.0, 0.0).astype(F32)
-    even = jnp.where(k == 0, step_size, 0.0).astype(F32)
 
     def at(t, sp):
         return {"tm": t, "space": sp}
@@ -209,7 +208,7 @@
     z_place = lax.rem(tm, 8)
     far_end = (z_place == 7) & (tm < 31)
     PIECE = COLS // 8
-    direct, by_a, by_b = range(0, 3), range(3, 6), range(6, 8)
+    direct, by_a, by_b = range(0, 2), range(2, 5), range(5, 8)
     routes = ((by_a, relay_a, 6, 1), (by_b, relay_b, 2, 5))
 
     def piece(n):
@@ -278,25 +277,6 @@
         for n in direct:
             start_copy(n, tm_next).start()
 
-    def depth_pieces(base):
-        return (
-            (pl.ds(pl.multiple_of(base, 128), PART), pl.ds(128, PART)),
-            (pl.ds(pl.multiple_of(lax.rem(base + COLS - 128, COLS), 128), 128), pl.ds(0, 128)),
-            (pl.ds(pl.multiple_of(lax.rem(base + PART, COLS), 128), 128), pl.ds(384, 128)),
-        )
-
-    def depth_copy(d, n, send):
-        sp = lax.rem(s + d, SPACE) if send else lax.rem(s + SPACE - d, SPACE)
-        to = sp if send else s
-        src, dst = depth_pieces(512 * to + 256 * (owned(to, tm) // 16))[n]
-        return copy(depth.at[:, src], dr.at[rows(ROWS * (s if send else sp)), dst], dep_s.at[n, d], dep_r.at[n, d], at(tm, sp))
-
-    for d in range(1, SPACE):
-        for n in range(3):
-            depth_copy(d, n, True).start()
-    for src, dst in depth_pieces(512 * s + 256 * half):
-        dr[rows(ROWS * s), dst] = depth[:, src]
-
     for ns, buffer, back, spot_of in routes:
         @pl.when((z_place == spot_of) & (tm < 24))
         def _(ns=ns, buffer=buffer, back=back):
@@ -365,46 +345,58 @@
 
     pairs(q2_rows)
 
-    def q3_copy(n, i, send):
-        up_down = lax.rem(s + (1 if (n == 0) == send else SPACE - 1), SPACE)
-        cols = pl.ds(pl.multiple_of(i * CHUNK, CHUNK), CHUNK)
-        return copy(q3s.at[n, :, cols], q3r.at[n, :, cols], q3_ss.at[n, i], q3_rs.at[n, i], at(tm, up_down))
-
-    @pl.loop(0, COLS // CHUNK)
-    def _(i):
-        base = pl.multiple_of(i * CHUNK, CHUNK)
-        cols = pl.ds(base, CHUNK)
-        r = ring_rates(q2, drow, base)
-        top, bottom = [], []
-        for f in range(3):
-            x, y = s0r[f, :ROWS, cols], s1[f, :, cols]
-            z = y + r[f][:ROWS]
-            partial[f, :, cols] = y - 0.5 * (x + z)
-            q = (step_size * first + start_share) * x + one_share * y + two_share * z
-            q3[f, :ROWS, cols] = q
-            top.append(q[:8])
-            bottom.append(q[8:])
-        q3s[0, :, cols] = pack(bottom, 6)
-        q3s[1, :, cols] = pack(top, 0)
+    def q3_copy(n, j, send):
+        up_down = lax.rem(s + (1 if (n % 2 == 0) == send else SPACE - 1), SPACE)
+        cols = pl.ds(pl.multiple_of(j * CHUNK, CHUNK), CHUNK)
+        return copy(q3s.at[n, :, cols], q3r.at[n, :, cols], q3_ss.at[n, j], q3_rs.at[n, j], at(tm, up_down))
+
+    def two(j, folded, bases):
+        tiles = [[], [], [], []]
+        for base in bases:
+            cols = pl.ds(base, CHUNK)
+            r = ring_rates(q2, drow, base)
+            top, bottom = [], []
+            for f in range(3):
+                x, y = s0r[f, :ROWS, cols], s1[f, :, cols]
+                z = y + r[f][:ROWS]
+                partial[f, :, cols] = y - 0.5 * (x + z)
+                q = (step_size * first + start_share) * x + one_share * y + two_share * z
+                q3[f, :ROWS, cols] = q
+                top.append(q[:8])
+                bottom.append(q[8:])
+            for n, (parts, row) in enumerate(((bottom, 7), (top, 0), (bottom, 6), (top, 1))):
+                tiles[n].append(place(parts, [row] * 3))
+        for n in range(4):
+            q3s[n, :, folded] = fold(*tiles[n])
         for n in range(2):
-            q3_copy(n, i, True).start()
-
-    for d in range(1, SPACE):
-        for n in range(3):
-            depth_copy(d, n, False).wait_recv()
-    for t in range(4):
-        dt[128 * t : 128 * t + 128, :] = dr[:, 128 * t : 128 * t + 128].T
-
-    for i in range(COLS // CHUNK):
-        for n in range(2):
-            q3_copy(n, i, False).wait_recv()
-
-    def edge_rows(base):
-        cols = pl.ds(base, CHUNK)
-        for f in range(3):
-            q3[f, ROWS:, cols] = unpack(q3r[1, :, cols], q3r[0, :, cols], f)
-
-    chunks(edge_rows)
+            q3_copy(n, j, True).start()
+
+        @pl.when(k == 0)
+        def _():
+            for n in range(2, 4):
+                q3_copy(n, j, True).start()
+
+    pairs(two)
+    for n in range(2):
+        for j in range(PAIRS):
+            q3_copy(n, j, False).wait_recv()
+
+    @pl.when(k == 0)
+    def _():
+        for n in range(2, 4):
+            for j in range(PAIRS):
+                q3_copy(n, j, False).wait_recv()
+
+    def q3_rows(j, folded, bases):
+        row = lax.broadcasted_iota(jnp.int32, (8, CHUNK), 0)
+        for h, base in enumerate(bases):
+            for f in range(3):
+                i = 4 * h + f
+                near_rows = unfold(q3r[1, :, folded], q3r[0, :, folded], i)
+                far_rows = jnp.where(row < 4, sub_roll(q3r[3, :, folded], 1 - i), sub_roll(q3r[2, :, folded], 6 - i))
+                q3[f, ROWS:, pl.ds(base, CHUNK)] = jnp.where((row == 0) | (row == 7), near_rows, far_rows)
+
+    pairs(q3_rows)
 
     def three(base):
         cols = pl.ds(base, CHUNK)
@@ -427,7 +419,7 @@
         cols = pl.ds(base, CHUNK)
         r = ring_rates(br, drow, base)
         for f in range(3):
-            item[f, :, cols] = br[f, :ROWS, cols] + even * r[f][:ROWS]
+            item[f, :, cols] = jnp.where(k == 0, boosted[f, :, cols] + step_size * r[f][:ROWS], boosted[f, :, cols])
         item_copy(i).start()
 
     give.start()
@@ -450,6 +442,26 @@
         for d in range(1, SPACE):
             one_copy(f, lax.rem(s + d, SPACE), True).start()
     rt[:, rows(ROWS * s), :] = esum[:, :, block(s, k)]
+
+    def depth_pieces(base):
+        return (
+            (pl.ds(pl.multiple_of(base, 128), PART), pl.ds(128, PART)),
+            (pl.ds(pl.multiple_of(lax.rem(base + COLS - 128, COLS), 128), 128), pl.ds(0, 128)),
+            (pl.ds(pl.multiple_of(lax.rem(base + PART, COLS), 128), 128), pl.ds(384, 128)),
+        )
+
+    def depth_copy(d, n, send):
+        sp = lax.rem(s + d, SPACE) if send else lax.rem(s + SPACE - d, SPACE)
+        to = sp if send else s
+        src, dst = depth_pieces(512 * to + 256 * (owned(to, tm) // 16))[n]
+        return copy(depth.at[:, src], dr.at[rows(ROWS * (s if send else sp)), dst], dep_s.at[n, d], dep_r.at[n, d], at(tm, sp))
+
+    for d in range(1, SPACE):
+        for n in range(3):
+            depth_copy(d, n, True).start()
+    for src, dst in depth_pieces(512 * s + 256 * half):
+        dr[rows(ROWS * s), dst] = depth[:, src]
+
 
     def two_copy(f, n):
         src, dst = et.at[f, rows(OWN * n, OWN), :], ex.at[chip, f, pl.ds(HALO, OWN), :]
@@ -501,6 +513,13 @@
                 for n in ns:
                     halo_copy(n, c, width).start()
 
+    for d in range(1, SPACE):
+        for n in range(3):
+            depth_copy(d, n, False).wait_recv()
+    for t in range(4):
+        dt[128 * t : 128 * t + 128, :] = dr[:, 128 * t : 128 * t + 128].T
+
+
     def scanned(lo, hi, halo, state):
         count = OWN + 2 * halo
         d_own = dt[rows(128 - halo + OWN * spot, count), :]
@@ -535,6 +554,49 @@
     state = scanned(0, 7, 32, (jnp.zeros((WIDE, 128), F32),) * 3)
     state = scanned(7, 11, 16, tuple(x[16:64] for x in state))
     scanned(11, CHIPS - 1, 8, tuple(x[8:40] for x in state))
+
+    @pl.when(tm < 31)
+    def _():
+        for n in range(8):
+            start_copy(n, tm_next).wait_send()
+
+    for ns, buffer, back, spot_of in routes:
+        @pl.when((z_place == spot_of) & (tm < 24))
+        def _(ns=ns, buffer=buffer, back=back):
+            for n in ns:
+                pass_copy(n, buffer, ns[0], back + 1).wait_send()
+
+    for n in range(4):
+        for j in range(PAIRS):
+            pack_copy(n, j, True).wait_send()
+    for n in range(2):
+        for j in range(PAIRS):
+            q2_copy(n, j, True).wait_send()
+            q3_copy(n, j, True).wait_send()
+
+    @pl.when(k == 0)
+    def _():
+        for n in range(2, 4):
+            for j in range(PAIRS):
+                q3_copy(n, j, True).wait_send()
+
+    give.wait_send()
+    for i in range(COLS // CHUNK):
+        item_copy(i).wait_send()
+    for d in range(1, SPACE):
+        for n in range(3):
+            depth_copy(d, n, True).wait_send()
+        for f in range(3):
+            one_copy(f, lax.rem(s + d, SPACE), True).wait_send()
+
+    @pl.loop(0, 16)
+    def _(n):
+        @pl.when((owner(s, 16 * k + n) != tm) & (chip < CHIPS - 1))
+        def _():
+            for f in range(3):
+                two_copy(f, n).wait_send()
+
+        each_halo(n, lambda x: x.wait_send())
 
     @pl.when(chip > 0)
     def _():
@@ -572,88 +634,59 @@
         row_copy(lax.rem(s + d, SPACE), True).start()
     vout[:, :, block(s, k)] = vr[s]
     fin_copy(s, True).start()
-    for d in range(1, SPACE):
-        sp = lax.rem(s + SPACE - d, SPACE)
-        row_copy(sp, False).wait_recv()
-        fin_copy(sp, True).start()
     give.wait_recv()
-    for sp in range(SPACE):
-        fin_copy(sp, False).wait_recv()
-
-    @pl.when(tm < 31)
-    def _():
-        for n in range(8):
-            start_copy(n, tm_next).wait_send()
-
-    for ns, buffer, back, spot_of in routes:
-        @pl.when((z_place == spot_of) & (tm < 24))
-        def _(ns=ns, buffer=buffer, back=back):
-            for n in ns:
-                pass_copy(n, buffer, ns[0], back + 1).wait_send()
-
-    for n in range(4):
-        for j in range(PAIRS):
-            pack_copy(n, j, True).wait_send()
-    for n in range(2):
-        for j in range(PAIRS):
-            q2_copy(n, j, True).wait_send()
-        for i in range(COLS // CHUNK):
-            q3_copy(n, i, True).wait_send()
-    give.wait_send()
-    for i in range(COLS // CHUNK):
-        item_copy(i).wait_send()
-    for d in range(1, SPACE):
-        for n in range(3):
-            depth_copy(d, n, True).wait_send()
-        for f in range(3):
-            one_copy(f, lax.rem(s + d, SPACE), True).wait_send()
-        row_copy(lax.rem(s + d, SPACE), True).wait_send()
-    for sp in range(SPACE):
-        fin_copy(sp, True).wait_send()
-
-    @pl.loop(0, 16)
-    def _(n):
-        @pl.when((owner(s, 16 * k + n) != tm) & (chip < CHIPS - 1))
-        def _():
-            for f in range(3):
-                two_copy(f, n).wait_send()
-
-        each_halo(n, lambda x: x.wait_send())
-
-        @pl.when((n > 0) & ((chip != n) | (half != k)))
-        def _():
-            ret_copy(n).wait_send()
-
-
-def final_kernel(v, boosted, other, esum, partial, init, depth, out):
-    slot = lax.axis_index("tm")
-    even = lax.rem(slot, 2) == 0
-    first = slot == 0
-
-    def body(base):
+
+    def finish(sp):
+        base = pl.multiple_of(sp * CHUNK, CHUNK)
         cols = pl.ds(base, CHUNK)
-        d = wide(lambda c: depth[:, c], base)
+        d = wide(lambda c: drow[:, c], base)
 
         def stepped(state):
             h, u, w = state
             r = rates(h, u, w, d * u, d * w, left, right, up, down, lambda x: x)
             return [x + step_size * y for x, y in zip(state, r)]
 
-        state = [wide(lambda c, f=f: v[f, :, c], base) for f in range(3)]
+        state = [wide(lambda c, f=f: vout[f, :, c], base) for f in range(3)]
         a = stepped(state)
         b = stepped(a)
         for f in range(3):
             begin = inner(state[f])[:ROWS]
-            ours = jnp.where(even, boosted[f, :, cols], other[f, :, cols])
+            ours = jnp.where(k == 0, boosted[f, :, cols], other[f, :, cols])
             y1 = ours + inner(a[f])[:ROWS]
             y2 = esum[f, :, cols] + inner(b[f])[:ROWS]
-            start = jnp.where(even, jnp.where(first, init[f, :, cols], begin), y1)
-            end = jnp.where(even, y1, y2)
+            start = jnp.where(k == 0, jnp.where(tm == 0, init[f, :, cols], begin), y1)
+            end = jnp.where(k == 0, y1, y2)
             out[0, f, :, cols] = start
             out[1, f, :, cols] = partial[f, :, cols] + 0.5 * (start + end)
             out[2, f, :, cols] = end
 
-    chunks(body)
+    @pl.loop(1, SPACE)
+    def _(d):
+        sp = lax.rem(s + SPACE - d, SPACE)
+        row_copy(sp, False).wait_recv()
+        fin_copy(sp, True).start()
+        fin_copy(lax.rem(sp + 1, SPACE), False).wait_recv()
+
+        @pl.when(d >= 3)
+        def _():
+            finish(lax.rem(sp + 2, SPACE))
+
+    fin_copy(lax.rem(s + 1, SPACE), False).wait_recv()
+
+    @pl.loop(0, 3)
+    def _(i):
+        finish(lax.rem(s + 2 * SPACE - 6 - i, SPACE))
+
+    for d in range(1, SPACE):
+        row_copy(lax.rem(s + d, SPACE), True).wait_send()
+    for sp in range(SPACE):
+        fin_copy(sp, True).wait_send()
+
+    @pl.loop(1, 16)
+    def _(n):
+        @pl.when((chip != n) | (half != k))
+        def _():
+            ret_copy(n).wait_send()
 
 
 VM = pl.BlockSpec(memory_space=pltpu.VMEM)
@@ -661,8 +694,6 @@
 
 def per_device(fine_nodes, init_state, mean_depth):
     points = fine_nodes[0].reshape(9, ROWS, COLS)
-    state = jax.ShapeDtypeStruct((3, ROWS, COLS), F32)
-    ring = jax.ShapeDtypeStruct((3, RING, COLS), F32)
 
     def vm(*shape):
         return pltpu.VMEM(shape, F32)
@@ -671,33 +702,24 @@
         return [pltpu.SemaphoreType.DMA(shape)] * 2
 
     flat, ringed = vm(3, ROWS, COLS), vm(3, RING, COLS)
-    boosted, other, esum, partial, v, depth = pl.pallas_call(
+    out = pl.pallas_call(
         coarse_kernel,
-        out_shape=[state, state, state, state, ring, jax.ShapeDtypeStruct((RING, COLS), F32)],
+        out_shape=jax.ShapeDtypeStruct((3, 3, ROWS, COLS), F32),
         in_specs=[pl.BlockSpec(memory_space=pltpu.HBM)] * 3,
-        out_specs=[VM] * 6,
+        out_specs=VM,
         scratch_shapes=[
-            vm(9, ROWS, COLS), flat, vm(ROWS, COLS),
+            flat, flat, flat, flat, ringed, vm(RING, COLS), vm(9, ROWS, COLS), flat, vm(ROWS, COLS),
             flat, flat, flat, vm(2, 8, FOLD), vm(2, 8, FOLD), vm(2, 8, FOLD), vm(2, 8, FOLD),
-            ringed, ringed, flat, ringed, vm(2, 8, FOLD), vm(2, 8, FOLD), ringed, vm(2, 8, COLS), vm(2, 8, COLS),
-            ringed, flat, flat, vm(3, 3, ROWS, COLS // 8), vm(2, 3, ROWS, COLS // 8),
+            ringed, ringed, flat, ringed, vm(2, 8, FOLD), vm(2, 8, FOLD), ringed, vm(4, 8, FOLD), vm(4, 8, FOLD),
+            ringed, flat, flat, vm(3, 3, ROWS, COLS // 8), vm(3, 3, ROWS, COLS // 8),
             vm(3, 128, PART), vm(3, PART, 128), vm(128, 512), vm(512, 128),
             vm(CHIPS, 3, WIDE, 128), vm(CHIPS, 3, OWN, 128), vm(3, PART, 128), vm(SPACE, 3, RING, PART),
-            pltpu.SemaphoreType.DMA((5,)), *sems(8), *sems(8), *sems(4, 4), *sems(2, 4), *sems(2, 8), *sems(8), *sems(1), *sems(3, 8), *sems(3, 8), *sems(3, 16),
+            pltpu.SemaphoreType.DMA((5,)), *sems(8), *sems(8), *sems(4, 4), *sems(2, 4), *sems(4, 4), *sems(8), *sems(1), *sems(3, 8), *sems(3, 8), *sems(3, 16),
             *sems(4, 16), *sems(16), *sems(8), *sems(8),
         ],
-        compiler_params=pltpu.CompilerParams(collective_id=0, has_side_effects=True, vmem_limit_bytes=36 << 20),
+        compiler_params=pltpu.CompilerParams(collective_id=0, has_side_effects=True, vmem_limit_bytes=40 << 20),
         name="sweep",
     )(*(pltpu.with_memory_space_constraint(x, pltpu.HBM) for x in (points, init_state, mean_depth)))
-
-    out = pl.pallas_call(
-        final_kernel,
-        out_shape=jax.ShapeDtypeStruct((3, 3, ROWS, COLS), F32),
-        in_specs=[VM] * 7,
-        out_specs=VM,
-        compiler_params=pltpu.CompilerParams(vmem_limit_bytes=24 << 20),
-        name="final",
-    )(v, boosted, other, esum, partial, init_state, depth)
     return out[None]
 
 

time: 96 us -> 95.5 us (level)
  Pallas kernels: 95.9 us -> 94.1 us
  local copies, waits for them, and re-layouts: 0.01 us -> 1.41 us
    pallas_call x2 -> x1, Pallas kernels: 95.9 us -> 94.1 us  [per_device(): pl.pallas_call(coarse_kernel, out_shape=jax.ShapeDtypeStruct((3, 3, ROWS,...]
    unnamed x2 -> x1, local copies, waits for them, and re-layouts: 0.01 us -> 1.41 us
where the time goes in v5:
time: 95.5 us
  Pallas kernels  94.1 us (99%)
  local copies, waits for them, and re-layouts  1.41 us (1%)
    pallas_call x1, Pallas kernels, per_device(): pl.pallas_call(coarse_kernel, out_shape=jax.ShapeDtypeStruct((3, 3, ROWS,...  94.1 us

profile of v5, /device:TPU:231, one launch (start us, length us, event | category | flops | bytes accessed | tf_op | source)
XLA Modules:
  0.0 95.5 jit_solution(6555975447513520722)
XLA Ops:
  0.0 94.1 %sweep.1 = f32[3,3,16,4096]{3,2,1,0:T(8,128)S(1)} custom-call(f32[9,16,4096]{2,1,0:T(8,128)} %bitcast.3, f32[3,16,4096]{2,1,0:T(8,128)} %init_hbm.1, f32[16,4096]{1,0:T(8,128)} %depth_hbm.1), custom_call_target="tpu_custom_call" | custom-call | tf_op jit(solution)/shard_map/sweep/pallas_call | solution.py:705
  94.1 1.4 %copy.5 = f32[1,3,3,16,4096]{4,3,2,1,0:T(8,128)} copy(f32[1,3,3,16,4096]{4,3,2,1,0:T(8,128)S(1)} %bitcast.2) | data formatting | bytes 4718592

commit v6 on v5

--- a/solution.py
+++ b/solution.py
@@ -156,7 +156,7 @@
 def coarse_kernel(
     points_hbm, init_hbm, depth_hbm,
     out,
-    boosted, other, esum, partial, vout, drow, points, init, depth, s0, a1, a2, ps, pr, fs, fr, s0r, q1, s1, q2, q2s, q2r, q3, q3s, q3r, br, item, ritem, relay_a, relay_b,
+    boosted, other, esum, partial, vout, drow, points, init, depth, s0, a1, a2, ps, pr, fs, fr, s0r, q1, s1, q2, q2s, q2r, q3, q3s, q3r, br, item, ritem, relay_a, relay_b, relay_c,
     rt, et, dr, dt, ex, vx, vt, vr,
     in_sem, st_s, st_r, rl_s, rl_r, pk_s, pk_r, q2_ss, q2_rs, q3_ss, q3_rs, it_s, it_r, oth_s, oth_r, one_s, one_r, dep_s, dep_r, two_s, two_r,
     halo_s, halo_r, ret_s, ret_r, row_s, row_r, fin_s, fin_r,
@@ -208,8 +208,8 @@
     z_place = lax.rem(tm, 8)
     far_end = (z_place == 7) & (tm < 31)
     PIECE = COLS // 8
-    direct, by_a, by_b = range(0, 2), range(2, 5), range(5, 8)
-    routes = ((by_a, relay_a, 6, 1), (by_b, relay_b, 2, 5))
+    direct = range(0, 2)
+    routes = ((range(2, 4), relay_a, 6, 1), (range(4, 6), relay_b, 2, 5), (range(6, 8), relay_c, 4, 3))
 
     def piece(n):
         return pl.ds(PIECE * n, PIECE)
@@ -267,7 +267,7 @@
         for n in range(2):
             ps[n, :, folded] = fold(*tiles[0][n])
             fs[n, :, folded] = fold(*tiles[1][n])
-        for n in range(4):
+        for n in range(2, 4):
             pack_copy(n, j, True).start()
 
     pairs(prepare)
@@ -276,6 +276,10 @@
     def _():
         for n in direct:
             start_copy(n, tm_next).start()
+
+    for n in range(2):
+        for j in range(PAIRS):
+            pack_copy(n, j, True).start()
 
     for ns, buffer, back, spot_of in routes:
         @pl.when((z_place == spot_of) & (tm < 24))
@@ -501,7 +505,7 @@
                 for n in ns:
                     act(halo_copy(n, j, width))
 
-    for c in (0, 1, 2, 5, 6, 9, 10, 13, 14, 3, 11, 7, 4, 8, 12):
+    for c in (0, 1, 2, 3, 5, 6, 4, 7, 9, 10, 11, 8, 13, 14, 12):
         @pl.when((chip != c) | (half != k))
         def _(c=c):
             for f in range(3):
@@ -554,49 +558,6 @@
     state = scanned(0, 7, 32, (jnp.zeros((WIDE, 128), F32),) * 3)
     state = scanned(7, 11, 16, tuple(x[16:64] for x in state))
     scanned(11, CHIPS - 1, 8, tuple(x[8:40] for x in state))
-
-    @pl.when(tm < 31)
-    def _():
-        for n in range(8):
-            start_copy(n, tm_next).wait_send()
-
-    for ns, buffer, back, spot_of in routes:
-        @pl.when((z_place == spot_of) & (tm < 24))
-        def _(ns=ns, buffer=buffer, back=back):
-            for n in ns:
-                pass_copy(n, buffer, ns[0], back + 1).wait_send()
-
-    for n in range(4):
-        for j in range(PAIRS):
-            pack_copy(n, j, True).wait_send()
-    for n in range(2):
-        for j in range(PAIRS):
-            q2_copy(n, j, True).wait_send()
-            q3_copy(n, j, True).wait_send()
-
-    @pl.when(k == 0)
-    def _():
-        for n in range(2, 4):
-            for j in range(PAIRS):
-                q3_copy(n, j, True).wait_send()
-
-    give.wait_send()
-    for i in range(COLS // CHUNK):
-        item_copy(i).wait_send()
-    for d in range(1, SPACE):
-        for n in range(3):
-            depth_copy(d, n, True).wait_send()
-        for f in range(3):
-            one_copy(f, lax.rem(s + d, SPACE), True).wait_send()
-
-    @pl.loop(0, 16)
-    def _(n):
-        @pl.when((owner(s, 16 * k + n) != tm) & (chip < CHIPS - 1))
-        def _():
-            for f in range(3):
-                two_copy(f, n).wait_send()
-
-        each_halo(n, lambda x: x.wait_send())
 
     @pl.when(chip > 0)
     def _():
@@ -635,6 +596,50 @@
     vout[:, :, block(s, k)] = vr[s]
     fin_copy(s, True).start()
     give.wait_recv()
+
+    @pl.when(tm < 31)
+    def _():
+        for n in range(8):
+            start_copy(n, tm_next).wait_send()
+
+    for ns, buffer, back, spot_of in routes:
+        @pl.when((z_place == spot_of) & (tm < 24))
+        def _(ns=ns, buffer=buffer, back=back):
+            for n in ns:
+                pass_copy(n, buffer, ns[0], back + 1).wait_send()
+
+    for n in range(4):
+        for j in range(PAIRS):
+            pack_copy(n, j, True).wait_send()
+    for n in range(2):
+        for j in range(PAIRS):
+            q2_copy(n, j, True).wait_send()
+            q3_copy(n, j, True).wait_send()
+
+    @pl.when(k == 0)
+    def _():
+        for n in range(2, 4):
+            for j in range(PAIRS):
+                q3_copy(n, j, True).wait_send()
+
+    give.wait_send()
+    for i in range(COLS // CHUNK):
+        item_copy(i).wait_send()
+    for d in range(1, SPACE):
+        for n in range(3):
+            depth_copy(d, n, True).wait_send()
+        for f in range(3):
+            one_copy(f, lax.rem(s + d, SPACE), True).wait_send()
+
+    @pl.loop(0, 16)
+    def _(n):
+        @pl.when((owner(s, 16 * k + n) != tm) & (chip < CHIPS - 1))
+        def _():
+            for f in range(3):
+                two_copy(f, n).wait_send()
+
+        each_halo(n, lambda x: x.wait_send())
+
 
     def finish(sp):
         base = pl.multiple_of(sp * CHUNK, CHUNK)
@@ -711,7 +716,7 @@
             flat, flat, flat, flat, ringed, vm(RING, COLS), vm(9, ROWS, COLS), flat, vm(ROWS, COLS),
             flat, flat, flat, vm(2, 8, FOLD), vm(2, 8, FOLD), vm(2, 8, FOLD), vm(2, 8, FOLD),
             ringed, ringed, flat, ringed, vm(2, 8, FOLD), vm(2, 8, FOLD), ringed, vm(4, 8, FOLD), vm(4, 8, FOLD),
-            ringed, flat, flat, vm(3, 3, ROWS, COLS // 8), vm(3, 3, ROWS, COLS // 8),
+            ringed, flat, flat, vm(2, 3, ROWS, COLS // 8), vm(2, 3, ROWS, COLS // 8), vm(2, 3, ROWS, COLS // 8),
             vm(3, 128, PART), vm(3, PART, 128), vm(128, 512), vm(512, 128),
             vm(CHIPS, 3, WIDE, 128), vm(CHIPS, 3, OWN, 128), vm(3, PART, 128), vm(SPACE, 3, RING, PART),
             pltpu.SemaphoreType.DMA((5,)), *sems(8), *sems(8), *sems(4, 4), *sems(2, 4), *sems(4, 4), *sems(8), *sems(1), *sems(3, 8), *sems(3, 8), *sems(3, 16),

time: 95.5 us -> 92.1 us (0.964)
  Pallas kernels: 94.1 us -> 90.4 us
    pallas_call x1, Pallas kernels: 94.1 us -> 90.4 us  [per_device(): pl.pallas_call(coarse_kernel, out_shape=jax.ShapeDtypeStruct((3, 3, ROWS,...]
where the time goes in v6:
time: 92.1 us; the launch traced here: 91.8 us
  Pallas kernels  90.4 us (98%)
  local copies, waits for them, and re-layouts  1.41 us (2%)
    pallas_call x1, Pallas kernels, per_device(): pl.pallas_call(coarse_kernel, out_shape=jax.ShapeDtypeStruct((3, 3, ROWS,...  90.4 us

profile of v6, /device:TPU:231, one launch (start us, length us, event | category | flops | bytes accessed | tf_op | source)
XLA Modules:
  0.0 91.8 jit_solution(8813585652349999479)
XLA Ops:
  0.0 90.4 %sweep.1 = f32[3,3,16,4096]{3,2,1,0:T(8,128)S(1)} custom-call(f32[9,16,4096]{2,1,0:T(8,128)} %bitcast.3, f32[3,16,4096]{2,1,0:T(8,128)} %init_hbm.1, f32[16,4096]{1,0:T(8,128)} %depth_hbm.1), custom_call_target="tpu_custom_call" | custom-call | tf_op jit(solution)/shard_map/sweep/pallas_call | solution.py:710
  90.4 1.4 %copy.5 = f32[1,3,3,16,4096]{4,3,2,1,0:T(8,128)} copy(f32[1,3,3,16,4096]{4,3,2,1,0:T(8,128)S(1)} %bitcast.2) | data formatting | bytes 4718592

commit v7 on v6

--- a/solution.py
+++ b/solution.py
@@ -27,7 +27,8 @@
 CHIPS = 16
 PART = 256
 OWN = 16
-HALO = 32
+HALO = 16
+MIDDLE = 7
 WIDE = OWN + 2 * HALO
 
 
@@ -157,7 +158,7 @@
     points_hbm, init_hbm, depth_hbm,
     out,
     boosted, other, esum, partial, vout, drow, points, init, depth, s0, a1, a2, ps, pr, fs, fr, s0r, q1, s1, q2, q2s, q2r, q3, q3s, q3r, br, item, ritem, relay_a, relay_b, relay_c,
-    rt, et, dr, dt, ex, vx, vt, vr,
+    rt, et, dr, dt, ex, vx, middle, vt, vr,
     in_sem, st_s, st_r, rl_s, rl_r, pk_s, pk_r, q2_ss, q2_rs, q3_ss, q3_rs, it_s, it_r, oth_s, oth_r, one_s, one_r, dep_s, dep_r, two_s, two_r,
     halo_s, halo_r, ret_s, ret_r, row_s, row_r, fin_s, fin_r,
 ):
@@ -178,7 +179,7 @@
         return at(owner(p // 32, lax.rem(p, 32)), p // 32)
 
     partner = at(chip * 2 + 1 - k, s)
-    nears = [near(1), near(-1), near(2), near(-2)]
+    nears = [near(1), near(-1)]
 
     loads = [pltpu.make_async_copy(points_hbm.at[3 * m : 3 * m + 3], points.at[3 * m : 3 * m + 3], in_sem.at[m]) for m in range(3)]
     loads += [pltpu.make_async_copy(init_hbm, init, in_sem.at[3]), pltpu.make_async_copy(depth_hbm, depth, in_sem.at[4])]
@@ -186,7 +187,11 @@
         loads[n].start()
     vt[...] = jnp.zeros_like(vt)
     barrier = pltpu.get_barrier_semaphore()
-    peers = [at(lax.rem(tm + d, 32), s) for d in range(1, 32)]
+    z, x = tm // 8, lax.rem(tm // 2, 4)
+    peers = [
+        at(lax.rem(z + dz, 4) * 8 + lax.rem(x + dx, 4) * 2 + c, s)
+        for dz in (2, 1, 3, 0) for dx in (2, 1, 3, 0) for c in range(2) if dz or dx
+    ] + [partner]
     peers += [at(tm, lax.rem(s + d, SPACE)) for d in range(1, SPACE)]
     peers += [at(t, sp) for t in (tm_next, tm_prev) for sp in (s_next, s_prev)]
     peers += nears
@@ -489,20 +494,20 @@
     def _():
         ex[chip, :, HALO : HALO + OWN, :] = et[:, rows(OWN * spot, OWN), :]
 
+    spans = ((0, 2, 16), (2, 6, 8), (7, 10, 16), (10, 14, 8))
+
     def halo_copy(n, j, width):
-        hop, sign = n // 2 + 1, 1 - 2 * (n % 2)
-        far = OWN * (hop - 1)
-        if sign > 0:
-            src, dst = HALO + OWN - width, HALO - far - width
-        else:
-            src, dst = HALO, HALO + OWN + far
+        src, dst = (HALO + OWN - width, HALO - width) if n == 0 else (HALO, HALO + OWN)
         return copy(ex.at[j, :, pl.ds(src, width), :], ex.at[j, :, pl.ds(dst, width), :], halo_s.at[n, j], halo_r.at[n, j], nears[n])
 
+    def middle_copy(n):
+        return copy(vx.at[MIDDLE], middle.at[n], halo_s.at[n, 15], halo_r.at[n, 15], nears[n])
+
     def each_halo(j, act):
-        for lo, hi, ns, width in ((0, 10, (0, 1), 16), (10, 14, (0, 1), 8), (0, 2, (2, 3), 16), (2, 6, (2, 3), 8)):
+        for lo, hi, width in spans:
             @pl.when((j >= lo) & (j < hi))
             def _():
-                for n in ns:
+                for n in range(2):
                     act(halo_copy(n, j, width))
 
     for c in (0, 1, 2, 3, 5, 6, 4, 7, 9, 10, 11, 8, 13, 14, 12):
@@ -512,9 +517,9 @@
                 src, dst = et.at[f, rows(OWN * spot, OWN), :], ex.at[c, f, pl.ds(HALO, OWN), :]
                 copy(src, dst, two_s.at[f, 0], two_r.at[f, c], at(c * 2 + half, s)).wait_recv()
 
-        for lo, hi, ns, width in ((0, 10, (0, 1), 16), (10, 14, (0, 1), 8), (0, 2, (2, 3), 16), (2, 6, (2, 3), 8)):
+        for lo, hi, width in spans:
             if lo <= c < hi:
-                for n in ns:
+                for n in range(2):
                     halo_copy(n, c, width).start()
 
     for d in range(1, SPACE):
@@ -555,8 +560,13 @@
     def ret_copy(j):
         return copy(vx.at[j], vt.at[:, rows(OWN * spot, OWN), :], ret_s.at[j], ret_r.at[spot], at(j * 2 + half, s))
 
-    state = scanned(0, 7, 32, (jnp.zeros((WIDE, 128), F32),) * 3)
-    state = scanned(7, 11, 16, tuple(x[16:64] for x in state))
+    state = scanned(0, MIDDLE, HALO, (jnp.zeros((WIDE, 128), F32),) * 3)
+    for n in range(2):
+        middle_copy(n).start()
+    for n in range(2):
+        middle_copy(n).wait_recv()
+    state = tuple(jnp.concatenate([middle[0, f], x[HALO : HALO + OWN], middle[1, f]], axis=0) for f, x in enumerate(state))
+    state = scanned(MIDDLE, 11, HALO, state)
     scanned(11, CHIPS - 1, 8, tuple(x[8:40] for x in state))
 
     @pl.when(chip > 0)
@@ -639,6 +649,9 @@
                 two_copy(f, n).wait_send()
 
         each_halo(n, lambda x: x.wait_send())
+
+    for n in range(2):
+        middle_copy(n).wait_send()
 
 
     def finish(sp):
@@ -718,9 +731,9 @@
             ringed, ringed, flat, ringed, vm(2, 8, FOLD), vm(2, 8, FOLD), ringed, vm(4, 8, FOLD), vm(4, 8, FOLD),
             ringed, flat, flat, vm(2, 3, ROWS, COLS // 8), vm(2, 3, ROWS, COLS // 8), vm(2, 3, ROWS, COLS // 8),
             vm(3, 128, PART), vm(3, PART, 128), vm(128, 512), vm(512, 128),
-            vm(CHIPS, 3, WIDE, 128), vm(CHIPS, 3, OWN, 128), vm(3, PART, 128), vm(SPACE, 3, RING, PART),
+            vm(CHIPS, 3, WIDE, 128), vm(CHIPS, 3, OWN, 128), vm(2, 3, OWN, 128), vm(3, PART, 128), vm(SPACE, 3, RING, PART),
             pltpu.SemaphoreType.DMA((5,)), *sems(8), *sems(8), *sems(4, 4), *sems(2, 4), *sems(4, 4), *sems(8), *sems(1), *sems(3, 8), *sems(3, 8), *sems(3, 16),
-            *sems(4, 16), *sems(16), *sems(8), *sems(8),
+            *sems(2, 16), *sems(16), *sems(8), *sems(8),
         ],
         compiler_params=pltpu.CompilerParams(collective_id=0, has_side_effects=True, vmem_limit_bytes=40 << 20),
         name="sweep",

time: 92.1 us -> 92 us (level)
  no operation moved by 1% of the time
where the time goes in v7:
time: 92 us; the launch traced here: 91.4 us
  Pallas kernels  90 us (98%)
  local copies, waits for them, and re-layouts  1.41 us (2%)
    pallas_call x1, Pallas kernels, per_device(): pl.pallas_call(coarse_kernel, out_shape=jax.ShapeDtypeStruct((3, 3, ROWS,...  90 us

profile of v7, /device:TPU:231, one launch (start us, length us, event | category | flops | bytes accessed | tf_op | source)
XLA Modules:
  0.0 91.4 jit_solution(3786662503350120622)
XLA Ops:
  0.0 90.0 %sweep.1 = f32[3,3,16,4096]{3,2,1,0:T(8,128)S(1)} custom-call(f32[9,16,4096]{2,1,0:T(8,128)} %bitcast.3, f32[3,16,4096]{2,1,0:T(8,128)} %init_hbm.1, f32[16,4096]{1,0:T(8,128)} %depth_hbm.1), custom_call_target="tpu_custom_call" | custom-call | tf_op jit(solution)/shard_map/sweep/pallas_call | solution.py:723
  90.0 1.4 %copy.5 = f32[1,3,3,16,4096]{4,3,2,1,0:T(8,128)} copy(f32[1,3,3,16,4096]{4,3,2,1,0:T(8,128)S(1)} %bitcast.2) | data formatting | bytes 4718592

commit v8 on v7

--- a/solution.py
+++ b/solution.py
@@ -529,7 +529,7 @@
         dt[128 * t : 128 * t + 128, :] = dr[:, 128 * t : 128 * t + 128].T
 
 
-    def scanned(lo, hi, halo, state):
+    def scanned(lo, hi, halo, state, send):
         count = OWN + 2 * halo
         d_own = dt[rows(128 - halo + OWN * spot, count), :]
 
@@ -549,25 +549,33 @@
             for f in range(3):
                 vx[j + 1, f] = state[f][halo : halo + OWN]
 
-            @pl.when((chip != j + 1) | (half != k))
-            def _():
-                ret_copy(j + 1).start()
-
+            if send:
+                give_back(j + 1)
             return state
 
         return lax.fori_loop(lo, hi, body, state)
+
+    def give_back(j):
+        @pl.when((chip != j) | (half != k))
+        def _():
+            ret_copy(j).start()
 
     def ret_copy(j):
         return copy(vx.at[j], vt.at[:, rows(OWN * spot, OWN), :], ret_s.at[j], ret_r.at[spot], at(j * 2 + half, s))
 
-    state = scanned(0, MIDDLE, HALO, (jnp.zeros((WIDE, 128), F32),) * 3)
+    state = scanned(0, MIDDLE, HALO, (jnp.zeros((WIDE, 128), F32),) * 3, False)
     for n in range(2):
         middle_copy(n).start()
+
+    @pl.loop(0, MIDDLE)
+    def _(i):
+        give_back(1 + lax.rem(chip + i, MIDDLE))
+
     for n in range(2):
         middle_copy(n).wait_recv()
     state = tuple(jnp.concatenate([middle[0, f], x[HALO : HALO + OWN], middle[1, f]], axis=0) for f, x in enumerate(state))
-    state = scanned(MIDDLE, 11, HALO, state)
-    scanned(11, CHIPS - 1, 8, tuple(x[8:40] for x in state))
+    state = scanned(MIDDLE, 11, HALO, state, True)
+    scanned(11, CHIPS - 1, 8, tuple(x[8:40] for x in state), True)
 
     @pl.when(chip > 0)
     def _():

time: 92 us -> 90.3 us (0.982)
  Pallas kernels: 90 us -> 88.3 us
    pallas_call x1, Pallas kernels: 90 us -> 88.3 us  [per_device(): pl.pallas_call(coarse_kernel, out_shape=jax.ShapeDtypeStruct((3, 3, ROWS,...]
where the time goes in v8:
time: 90.3 us; the launch traced here: 89.7 us
  Pallas kernels  88.3 us (98%)
  local copies, waits for them, and re-layouts  1.41 us (2%)
    pallas_call x1, Pallas kernels, per_device(): pl.pallas_call(coarse_kernel, out_shape=jax.ShapeDtypeStruct((3, 3, ROWS,...  88.3 us

profile of v8, /device:TPU:231, one launch (start us, length us, event | category | flops | bytes accessed | tf_op | source)
XLA Modules:
  0.0 89.7 jit_solution(14987040868556356214)
XLA Ops:
  0.0 88.3 %sweep.1 = f32[3,3,16,4096]{3,2,1,0:T(8,128)S(1)} custom-call(f32[9,16,4096]{2,1,0:T(8,128)} %bitcast.3, f32[3,16,4096]{2,1,0:T(8,128)} %init_hbm.1, f32[16,4096]{1,0:T(8,128)} %depth_hbm.1), custom_call_target="tpu_custom_call" | custom-call | tf_op jit(solution)/shard_map/sweep/pallas_call | solution.py:731
  88.3 1.4 %copy.5 = f32[1,3,3,16,4096]{4,3,2,1,0:T(8,128)} copy(f32[1,3,3,16,4096]{4,3,2,1,0:T(8,128)S(1)} %bitcast.2) | data formatting | bytes 4718592

commit v9 on v8

--- a/solution.py
+++ b/solution.py
@@ -47,8 +47,11 @@
 
 
 def edges(base):
-    lo = pl.multiple_of(lax.rem(base + COLS - 128, COLS), 128)
-    hi = pl.multiple_of(lax.rem(base + CHUNK, COLS), 128)
+    if isinstance(base, int):
+        lo, hi = (base - 128) % COLS, (base + CHUNK) % COLS
+    else:
+        lo = pl.multiple_of(lax.rem(base + COLS - 128, COLS), 128)
+        hi = pl.multiple_of(lax.rem(base + CHUNK, COLS), 128)
     return pl.ds(lo, 128), pl.ds(base, CHUNK), pl.ds(hi, 128)
 
 
@@ -97,6 +100,11 @@
     def _(j):
         base = pl.multiple_of(j * CHUNK, CHUNK)
         body(j, pl.ds(base, CHUNK), [base, pl.multiple_of(base + FOLD, CHUNK)])
+
+
+def pair(body, j):
+    base = j * CHUNK
+    body(j, pl.ds(base, CHUNK), [base, base + FOLD])
 
 
 def sub_roll(x, by):
@@ -230,7 +238,7 @@
 
     @pl.when((tm < 31) & (z_place != 7))
     def _():
-        for n in range(8):
+        for n in (0, 4, 1, 5, 2, 6, 3, 7):
             start_copy(n, tm_next).start()
 
     @pl.when(far_end)
@@ -245,7 +253,7 @@
     def pack_copy(n, j, send):
         up_down = lax.rem(s + (1 if (n % 2 == 0) == send else SPACE - 1), SPACE)
         slot = tm if n < 2 else (tm_next if send else tm_prev)
-        cols = pl.ds(pl.multiple_of(j * CHUNK, CHUNK), CHUNK)
+        cols = pl.ds(j * CHUNK, CHUNK) if isinstance(j, int) else pl.ds(pl.multiple_of(j * CHUNK, CHUNK), CHUNK)
         src, dst = (ps, pr) if n < 2 else (fs, fr)
         return copy(src.at[n % 2, :, cols], dst.at[n % 2, :, cols], pk_s.at[n, j], pk_r.at[n, j], at(slot, up_down))
 
@@ -297,11 +305,6 @@
         for j in range(PAIRS):
             pack_copy(n, j, False).wait_recv()
 
-    @pl.when(tm > 0)
-    def _():
-        for n in range(8):
-            start_copy(n, tm_prev).wait_recv()
-
     def ringed(j, folded, bases):
         row = lax.broadcasted_iota(jnp.int32, (8, CHUNK), 0)
         for h, base in enumerate(bases):
@@ -318,11 +321,9 @@
                 s0r[f, :, cols] = x
                 q1[f, :, cols] = half_step * x + y
 
-    pairs(ringed)
-
     def q2_copy(n, j, send):
         up_down = lax.rem(s + (1 if (n == 0) == send else SPACE - 1), SPACE)
-        cols = pl.ds(pl.multiple_of(j * CHUNK, CHUNK), CHUNK)
+        cols = pl.ds(j * CHUNK, CHUNK) if isinstance(j, int) else pl.ds(pl.multiple_of(j * CHUNK, CHUNK), CHUNK)
         return copy(q2s.at[n, :, cols], q2r.at[n, :, cols], q2_ss.at[n, j], q2_rs.at[n, j], at(tm, up_down))
 
     def one(j, folded, bases):
@@ -342,27 +343,31 @@
             q2s[n, :, folded] = fold(*tiles[n])
             q2_copy(n, j, True).start()
 
-    pairs(one)
-    for n in range(2):
-        for j in range(PAIRS):
-            q2_copy(n, j, False).wait_recv()
-
-    def q2_rows(j, folded, bases):
-        for h, base in enumerate(bases):
-            for f in range(3):
-                q2[f, ROWS:, pl.ds(base, CHUNK)] = unfold(q2r[1, :, folded], q2r[0, :, folded], 4 * h + f)
-
-    pairs(q2_rows)
+    for j in range(PAIRS):
+        @pl.when(tm > 0)
+        def _(j=j):
+            start_copy(j, tm_prev).wait_recv()
+            start_copy(j + PAIRS, tm_prev).wait_recv()
+
+        pair(ringed, j)
+        if j >= 2:
+            pair(one, j - 1)
+    pair(one, 3)
+    pair(one, 0)
 
     def q3_copy(n, j, send):
         up_down = lax.rem(s + (1 if (n % 2 == 0) == send else SPACE - 1), SPACE)
-        cols = pl.ds(pl.multiple_of(j * CHUNK, CHUNK), CHUNK)
+        cols = pl.ds(j * CHUNK, CHUNK) if isinstance(j, int) else pl.ds(pl.multiple_of(j * CHUNK, CHUNK), CHUNK)
         return copy(q3s.at[n, :, cols], q3r.at[n, :, cols], q3_ss.at[n, j], q3_rs.at[n, j], at(tm, up_down))
 
     def two(j, folded, bases):
+        for n in range(2):
+            q2_copy(n, j, False).wait_recv()
         tiles = [[], [], [], []]
-        for base in bases:
+        for h, base in enumerate(bases):
             cols = pl.ds(base, CHUNK)
+            for f in range(3):
+                q2[f, ROWS:, cols] = unfold(q2r[1, :, folded], q2r[0, :, folded], 4 * h + f)
             r = ring_rates(q2, drow, base)
             top, bottom = [], []
             for f in range(3):
@@ -385,18 +390,18 @@
             for n in range(2, 4):
                 q3_copy(n, j, True).start()
 
-    pairs(two)
-    for n in range(2):
-        for j in range(PAIRS):
+    for j in (1, 2, 3, 0):
+        pair(two, j)
+
+    def q3_rows(j, folded, bases):
+        for n in range(2):
             q3_copy(n, j, False).wait_recv()
 
-    @pl.when(k == 0)
-    def _():
-        for n in range(2, 4):
-            for j in range(PAIRS):
+        @pl.when(k == 0)
+        def _():
+            for n in range(2, 4):
                 q3_copy(n, j, False).wait_recv()
 
-    def q3_rows(j, folded, bases):
         row = lax.broadcasted_iota(jnp.int32, (8, CHUNK), 0)
         for h, base in enumerate(bases):
             for f in range(3):
@@ -405,17 +410,22 @@
                 far_rows = jnp.where(row < 4, sub_roll(q3r[3, :, folded], 1 - i), sub_roll(q3r[2, :, folded], 6 - i))
                 q3[f, ROWS:, pl.ds(base, CHUNK)] = jnp.where((row == 0) | (row == 7), near_rows, far_rows)
 
-    pairs(q3_rows)
-
-    def three(base):
-        cols = pl.ds(base, CHUNK)
-        r = ring_rates(q3, drow, base)
-        for f in range(3):
-            x = r[f] + first * s0r[f, :, cols]
-            br[f, :, cols] = x
-            boosted[f, :, cols] = x[:ROWS]
-
-    chunks(three)
+    def three(j, folded, bases):
+        for base in bases:
+            cols = pl.ds(base, CHUNK)
+            r = ring_rates(q3, drow, base)
+            for f in range(3):
+                x = r[f] + first * s0r[f, :, cols]
+                br[f, :, cols] = x
+                boosted[f, :, cols] = x[:ROWS]
+
+    pair(q3_rows, 1)
+    pair(q3_rows, 2)
+    pair(q3_rows, 3)
+    pair(three, 2)
+    pair(q3_rows, 0)
+    for j in (3, 0, 1):
+        pair(three, j)
     give = copy(boosted, other, oth_s.at[0], oth_r.at[0], partner)
 
     def item_copy(i):

time: 90.3 us -> 87.5 us (0.969)
  the two profiles are of different devices: /device:TPU:231 before, /device:TPU:7 now
where the time goes in v9:
time: 87.5 us
  Pallas kernels  86.1 us (98%)
  local copies, waits for them, and re-layouts  1.41 us (2%)
    pallas_call x1, Pallas kernels, per_device(): pl.pallas_call(coarse_kernel, out_shape=jax.ShapeDtypeStruct((3, 3, ROWS,...  86.1 us

profile of v9, /device:TPU:7, one launch (start us, length us, event | category | flops | bytes accessed | tf_op | source)
XLA Modules:
  0.0 87.5 jit_solution(10760356965007901423)
XLA Ops:
  0.0 86.1 %sweep.1 = f32[3,3,16,4096]{3,2,1,0:T(8,128)S(1)} custom-call(f32[9,16,4096]{2,1,0:T(8,128)} %bitcast.3, f32[3,16,4096]{2,1,0:T(8,128)} %init_hbm.1, f32[16,4096]{1,0:T(8,128)} %depth_hbm.1), custom_call_target="tpu_custom_call" | custom-call | tf_op jit(solution)/shard_map/sweep/pallas_call | solution.py:741
  86.1 1.4 %copy.5 = f32[1,3,3,16,4096]{4,3,2,1,0:T(8,128)} copy(f32[1,3,3,16,4096]{4,3,2,1,0:T(8,128)S(1)} %bitcast.2) | data formatting | bytes 4718592

commit v10 on v9

--- a/solution.py
+++ b/solution.py
@@ -165,8 +165,8 @@
 def coarse_kernel(
     points_hbm, init_hbm, depth_hbm,
     out,
-    boosted, other, esum, partial, vout, drow, points, init, depth, s0, a1, a2, ps, pr, fs, fr, s0r, q1, s1, q2, q2s, q2r, q3, q3s, q3r, br, item, ritem, relay_a, relay_b, relay_c,
-    rt, et, dr, dt, ex, vx, middle, vt, vr,
+    boosted, other, esum, partial, vout, vob, vh, drow, points, init, depth, s0, a1, a2, ps, pr, fs, fr, s0r, q1, s1, q2, q2s, q2r, q3, q3s, q3r, br, item, ritem, relay_a, relay_b, relay_c,
+    rt, et, dr, dt, ex, vx, middle, vt, vr, vb,
     in_sem, st_s, st_r, rl_s, rl_r, pk_s, pk_r, q2_ss, q2_rs, q3_ss, q3_rs, it_s, it_r, oth_s, oth_r, one_s, one_r, dep_s, dep_r, two_s, two_r,
     halo_s, halo_r, ret_s, ret_r, row_s, row_r, fin_s, fin_r,
 ):
@@ -601,28 +601,49 @@
             def _():
                 copy(vx.at[0], vt.at[:, rows(OWN * n, OWN), :], ret_s.at[0], ret_r.at[n], at(t, s)).wait_recv()
 
-    low = lax.broadcasted_iota(jnp.int32, (8, 128), 0) < 4
-    for f in range(3):
+    tile_row = lax.broadcasted_iota(jnp.int32, (8, 128), 0)
+    turned_back = [[vt[f, 128 * t : 128 * t + 128, :].T for t in range(2)] for f in range(3)]
+
+    def around(x, sp):
+        a, b = (16 * sp + 16) % 128, (16 * sp + 120) % 128
+        return jnp.where(tile_row < 2, x[a : a + 8], pltpu.roll(x[b : b + 8], 4, 0))
+
+    def stack(x, y):
+        return jnp.where(tile_row < 4, x, pltpu.roll(y, 4, 0))
+
+    for sp in range(SPACE):
         for t in range(2):
             cols = slice(128 * t, 128 * t + 128)
-            x = vt[f, cols, :].T
-            for sp in range(SPACE):
-                vr[sp, f, :ROWS, cols] = x[16 * sp : 16 * sp + 16]
-                a, b = (16 * sp + 16) % 128, (16 * sp + 120) % 128
-                vr[sp, f, ROWS:, cols] = jnp.where(low, x[a : a + 8], x[b : b + 8])
-
-    def row_copy(sp, send):
+            for f in range(3):
+                vr[sp, 16 * f : 16 * f + 16, cols] = turned_back[f][t][16 * sp : 16 * sp + 16]
+            vr[sp, 48:, cols] = stack(around(turned_back[0][t], sp), around(turned_back[1][t], sp))
+        vb[sp] = stack(around(turned_back[2][0], sp), around(turned_back[2][1], sp))
+
+    def side(sp, kk):
+        return pl.ds(pl.multiple_of(256 * sp + 128 * kk, 128), 128)
+
+    def row_copies(sp, send):
         to, by = (sp, s) if send else (s, sp)
-        return copy(vr.at[to], vout.at[:, :, block(by, k)], row_s.at[sp], row_r.at[by], at(tm, sp))
-
-    def fin_copy(sp, send):
-        cols = block(sp, k if send else 1 - k)
-        return copy(vout.at[:, :, cols], vout.at[:, :, cols], fin_s.at[sp], fin_r.at[sp], partner)
+        return (
+            copy(vr.at[to], vout.at[:, block(by, k)], row_s.at[0, sp], row_r.at[0, by], at(tm, sp)),
+            copy(vb.at[to], vob.at[:, side(by, k)], row_s.at[1, sp], row_r.at[1, by], at(tm, sp)),
+        )
+
+    def fin_copies(sp, send):
+        kk = k if send else 1 - k
+        cols, beside = block(sp, kk), side(sp, kk)
+        return (
+            copy(vout.at[:, cols], vout.at[:, cols], fin_s.at[0, sp], fin_r.at[0, sp], partner),
+            copy(vob.at[:, beside], vob.at[:, beside], fin_s.at[1, sp], fin_r.at[1, sp], partner),
+        )
 
     for d in range(1, SPACE):
-        row_copy(lax.rem(s + d, SPACE), True).start()
-    vout[:, :, block(s, k)] = vr[s]
-    fin_copy(s, True).start()
+        for c in row_copies(lax.rem(s + d, SPACE), True):
+            c.start()
+    vout[:, block(s, k)] = vr[s]
+    vob[:, side(s, k)] = vb[s]
+    for c in fin_copies(s, True):
+        c.start()
     give.wait_recv()
 
     @pl.when(tm < 31)
@@ -672,6 +693,19 @@
         middle_copy(n).wait_send()
 
 
+    def spread(sp):
+        cols = pl.ds(pl.multiple_of(sp * CHUNK, CHUNK), CHUNK)
+        row = lax.broadcasted_iota(jnp.int32, (8, CHUNK), 0)
+        x = vout[48:, cols]
+        y = pltpu.roll(x, 4, 0)
+        vh[0, :, cols] = jnp.where(row < 4, x, y)
+        vh[1, :, cols] = jnp.where(row < 4, y, x)
+        for kk in range(2):
+            x = vob[:, side(sp, kk)]
+            y = pltpu.roll(x, 4, 0)
+            for t, z in enumerate((jnp.where(tile_row < 4, x, y), jnp.where(tile_row < 4, y, x))):
+                vh[2, :, pl.ds(pl.multiple_of(512 * sp + 256 * kk + 128 * t, 128), 128)] = z
+
     def finish(sp):
         base = pl.multiple_of(sp * CHUNK, CHUNK)
         cols = pl.ds(base, CHUNK)
@@ -682,7 +716,9 @@
             r = rates(h, u, w, d * u, d * w, left, right, up, down, lambda x: x)
             return [x + step_size * y for x, y in zip(state, r)]
 
-        state = [wide(lambda c, f=f: vout[f, :, c], base) for f in range(3)]
+        state = [
+            wide(lambda c, f=f: jnp.concatenate([vout[16 * f : 16 * f + 16, c], vh[f, :, c]], axis=0), base) for f in range(3)
+        ]
         a = stepped(state)
         b = stepped(a)
         for f in range(3):
@@ -699,24 +735,32 @@
     @pl.loop(1, SPACE)
     def _(d):
         sp = lax.rem(s + SPACE - d, SPACE)
-        row_copy(sp, False).wait_recv()
-        fin_copy(sp, True).start()
-        fin_copy(lax.rem(sp + 1, SPACE), False).wait_recv()
+        for c in row_copies(sp, False):
+            c.wait_recv()
+        for c in fin_copies(sp, True):
+            c.start()
+        for c in fin_copies(lax.rem(sp + 1, SPACE), False):
+            c.wait_recv()
+        spread(lax.rem(sp + 1, SPACE))
 
         @pl.when(d >= 3)
         def _():
             finish(lax.rem(sp + 2, SPACE))
 
-    fin_copy(lax.rem(s + 1, SPACE), False).wait_recv()
+    for c in fin_copies(lax.rem(s + 1, SPACE), False):
+        c.wait_recv()
+    spread(lax.rem(s + 1, SPACE))
 
     @pl.loop(0, 3)
     def _(i):
         finish(lax.rem(s + 2 * SPACE - 6 - i, SPACE))
 
     for d in range(1, SPACE):
-        row_copy(lax.rem(s + d, SPACE), True).wait_send()
+        for c in row_copies(lax.rem(s + d, SPACE), True):
+            c.wait_send()
     for sp in range(SPACE):
-        fin_copy(sp, True).wait_send()
+        for c in fin_copies(sp, True):
+            c.wait_send()
 
     @pl.loop(1, 16)
     def _(n):
@@ -744,14 +788,14 @@
         in_specs=[pl.BlockSpec(memory_space=pltpu.HBM)] * 3,
         out_specs=VM,
         scratch_shapes=[
-            flat, flat, flat, flat, ringed, vm(RING, COLS), vm(9, ROWS, COLS), flat, vm(ROWS, COLS),
+            flat, flat, flat, flat, vm(56, COLS), vm(8, FOLD), vm(3, 8, COLS), vm(RING, COLS), vm(9, ROWS, COLS), flat, vm(ROWS, COLS),
             flat, flat, flat, vm(2, 8, FOLD), vm(2, 8, FOLD), vm(2, 8, FOLD), vm(2, 8, FOLD),
             ringed, ringed, flat, ringed, vm(2, 8, FOLD), vm(2, 8, FOLD), ringed, vm(4, 8, FOLD), vm(4, 8, FOLD),
             ringed, flat, flat, vm(2, 3, ROWS, COLS // 8), vm(2, 3, ROWS, COLS // 8), vm(2, 3, ROWS, COLS // 8),
             vm(3, 128, PART), vm(3, PART, 128), vm(128, 512), vm(512, 128),
-            vm(CHIPS, 3, WIDE, 128), vm(CHIPS, 3, OWN, 128), vm(2, 3, OWN, 128), vm(3, PART, 128), vm(SPACE, 3, RING, PART),
+            vm(CHIPS, 3, WIDE, 128), vm(CHIPS, 3, OWN, 128), vm(2, 3, OWN, 128), vm(3, PART, 128), vm(SPACE, 56, PART), vm(SPACE, 8, 128),
             pltpu.SemaphoreType.DMA((5,)), *sems(8), *sems(8), *sems(4, 4), *sems(2, 4), *sems(4, 4), *sems(8), *sems(1), *sems(3, 8), *sems(3, 8), *sems(3, 16),
-            *sems(2, 16), *sems(16), *sems(8), *sems(8),
+            *sems(2, 16), *sems(16), *sems(2, 8), *sems(2, 8),
         ],
         compiler_params=pltpu.CompilerParams(collective_id=0, has_side_effects=True, vmem_limit_bytes=40 << 20),
         name="sweep",

time: 87.5 us -> 86.7 us (level)
  the two profiles are of different devices: /device:TPU:7 before, /device:TPU:231 now
where the time goes in v10:
time: 86.7 us; the launch traced here: 85.9 us
  Pallas kernels  84.5 us (97%)
  local copies, waits for them, and re-layouts  1.41 us (2%)
    pallas_call x1, Pallas kernels, per_device(): pl.pallas_call(coarse_kernel, out_shape=jax.ShapeDtypeStruct((3, 3, ROWS,...  84.5 us

profile of v10, /device:TPU:231, one launch (start us, length us, event | category | flops | bytes accessed | tf_op | source)
XLA Modules:
  0.0 85.9 jit_solution(430625173887158983)
XLA Ops:
  0.0 84.5 %sweep.1 = f32[3,3,16,4096]{3,2,1,0:T(8,128)S(1)} custom-call(f32[9,16,4096]{2,1,0:T(8,128)} %bitcast.3, f32[3,16,4096]{2,1,0:T(8,128)} %init_hbm.1, f32[16,4096]{1,0:T(8,128)} %depth_hbm.1), custom_call_target="tpu_custom_call" | custom-call | tf_op jit(solution)/shard_map/sweep/pallas_call | solution.py:785
  84.5 1.4 %copy.5 = f32[1,3,3,16,4096]{4,3,2,1,0:T(8,128)} copy(f32[1,3,3,16,4096]{4,3,2,1,0:T(8,128)S(1)} %bitcast.2) | data formatting | bytes 4718592

commit v11 on v10

--- a/solution.py
+++ b/solution.py
@@ -448,15 +448,13 @@
         n = to if send else by
         return copy(esum.at[f, :, block(to, k)], rt.at[f, rows(ROWS * by), :], one_s.at[f, n], one_r.at[f, by], at(tm, sp))
 
-    for i in range(COLS // CHUNK):
+    @pl.loop(0, COLS // CHUNK)
+    def _(i):
         item_copy(i).wait_recv()
-
-    def summed(base):
-        cols = pl.ds(base, CHUNK)
+        cols = pl.ds(pl.multiple_of(i * CHUNK, CHUNK), CHUNK)
         for f in range(3):
             esum[f, :, cols] = item[f, :, cols] + ritem[f, :, cols]
 
-    chunks(summed)
     for f in range(3):
         for d in range(1, SPACE):
             one_copy(f, lax.rem(s + d, SPACE), True).start()
@@ -587,23 +585,11 @@
     state = scanned(MIDDLE, 11, HALO, state, True)
     scanned(11, CHIPS - 1, 8, tuple(x[8:40] for x in state), True)
 
-    @pl.when(chip > 0)
+    @pl.when((chip > 0) & (half == k))
     def _():
-        @pl.when(half == k)
-        def _():
-            vt[:, rows(OWN * spot, OWN), :] = vx[chip]
-
-        @pl.loop(0, 16)
-        def _(n):
-            t = owner(s, 16 * k + n)
-
-            @pl.when(t != tm)
-            def _():
-                copy(vx.at[0], vt.at[:, rows(OWN * n, OWN), :], ret_s.at[0], ret_r.at[n], at(t, s)).wait_recv()
+        vt[:, rows(OWN * spot, OWN), :] = vx[chip]
 
     tile_row = lax.broadcasted_iota(jnp.int32, (8, 128), 0)
-    turned_back = [[vt[f, 128 * t : 128 * t + 128, :].T for t in range(2)] for f in range(3)]
-
     def around(x, sp):
         a, b = (16 * sp + 16) % 128, (16 * sp + 120) % 128
         return jnp.where(tile_row < 2, x[a : a + 8], pltpu.roll(x[b : b + 8], 4, 0))
@@ -611,13 +597,8 @@
     def stack(x, y):
         return jnp.where(tile_row < 4, x, pltpu.roll(y, 4, 0))
 
-    for sp in range(SPACE):
-        for t in range(2):
-            cols = slice(128 * t, 128 * t + 128)
-            for f in range(3):
-                vr[sp, 16 * f : 16 * f + 16, cols] = turned_back[f][t][16 * sp : 16 * sp + 16]
-            vr[sp, 48:, cols] = stack(around(turned_back[0][t], sp), around(turned_back[1][t], sp))
-        vb[sp] = stack(around(turned_back[2][0], sp), around(turned_back[2][1], sp))
+    def half_block(sp, t):
+        return pl.ds(pl.multiple_of(512 * sp + 256 * k + 128 * t, 128), 128)
 
     def side(sp, kk):
         return pl.ds(pl.multiple_of(256 * sp + 128 * kk, 128), 128)
@@ -625,8 +606,8 @@
     def row_copies(sp, send):
         to, by = (sp, s) if send else (s, sp)
         return (
-            copy(vr.at[to], vout.at[:, block(by, k)], row_s.at[0, sp], row_r.at[0, by], at(tm, sp)),
-            copy(vb.at[to], vob.at[:, side(by, k)], row_s.at[1, sp], row_r.at[1, by], at(tm, sp)),
+            *(copy(vr.at[t, to], vout.at[:, half_block(by, t)], row_s.at[t, sp], row_r.at[t, by], at(tm, sp)) for t in range(2)),
+            copy(vb.at[to], vob.at[:, side(by, k)], row_s.at[2, sp], row_r.at[2, by], at(tm, sp)),
         )
 
     def fin_copies(sp, send):
@@ -637,10 +618,30 @@
             copy(vob.at[:, beside], vob.at[:, beside], fin_s.at[1, sp], fin_r.at[1, sp], partner),
         )
 
-    for d in range(1, SPACE):
-        for c in row_copies(lax.rem(s + d, SPACE), True):
-            c.start()
-    vout[:, block(s, k)] = vr[s]
+    for t in range(2):
+        @pl.when(chip > 0)
+        def _(t=t):
+            @pl.loop(8 * t, 8 * t + 8)
+            def _(n):
+                frm = owner(s, 16 * k + n)
+
+                @pl.when(frm != tm)
+                def _():
+                    copy(vx.at[0], vt.at[:, rows(OWN * n, OWN), :], ret_s.at[0], ret_r.at[n], at(frm, s)).wait_recv()
+
+        xs = [vt[f, 128 * t : 128 * t + 128, :].T for f in range(3)]
+        for sp in range(SPACE):
+            for f in range(3):
+                vr[t, sp, 16 * f : 16 * f + 16, :] = xs[f][16 * sp : 16 * sp + 16]
+            vr[t, sp, 48:, :] = stack(around(xs[0], sp), around(xs[1], sp))
+        if t == 1:
+            other_half = vt[2, :128, :].T
+            for sp in range(SPACE):
+                vb[sp] = stack(around(other_half, sp), around(xs[2], sp))
+        for d in range(1, SPACE):
+            for c in row_copies(lax.rem(s + d, SPACE), True)[t : 1 if t == 0 else 3]:
+                c.start()
+        vout[:, half_block(s, t)] = vr[t, s]
     vob[:, side(s, k)] = vb[s]
     for c in fin_copies(s, True):
         c.start()
@@ -793,9 +794,9 @@
             ringed, ringed, flat, ringed, vm(2, 8, FOLD), vm(2, 8, FOLD), ringed, vm(4, 8, FOLD), vm(4, 8, FOLD),
             ringed, flat, flat, vm(2, 3, ROWS, COLS // 8), vm(2, 3, ROWS, COLS // 8), vm(2, 3, ROWS, COLS // 8),
             vm(3, 128, PART), vm(3, PART, 128), vm(128, 512), vm(512, 128),
-            vm(CHIPS, 3, WIDE, 128), vm(CHIPS, 3, OWN, 128), vm(2, 3, OWN, 128), vm(3, PART, 128), vm(SPACE, 56, PART), vm(SPACE, 8, 128),
+            vm(CHIPS, 3, WIDE, 128), vm(CHIPS, 3, OWN, 128), vm(2, 3, OWN, 128), vm(3, PART, 128), vm(2, SPACE, 56, 128), vm(SPACE, 8, 128),
             pltpu.SemaphoreType.DMA((5,)), *sems(8), *sems(8), *sems(4, 4), *sems(2, 4), *sems(4, 4), *sems(8), *sems(1), *sems(3, 8), *sems(3, 8), *sems(3, 16),
-            *sems(2, 16), *sems(16), *sems(2, 8), *sems(2, 8),
+            *sems(2, 16), *sems(16), *sems(3, 8), *sems(2, 8),
         ],
         compiler_params=pltpu.CompilerParams(collective_id=0, has_side_effects=True, vmem_limit_bytes=40 << 20),
         name="sweep",

time: 86.7 us -> 87.4 us (level)
  no operation moved by 1% of the time
where the time goes in v11:
time: 87.4 us; the launch traced here: 85.7 us
  Pallas kernels  84.3 us (96%)
  local copies, waits for them, and re-layouts  1.41 us (2%)
    pallas_call x1, Pallas kernels, per_device(): pl.pallas_call(coarse_kernel, out_shape=jax.ShapeDtypeStruct((3, 3, ROWS,...  84.3 us

profile of v11, /device:TPU:231, one launch (start us, length us, event | category | flops | bytes accessed | tf_op | source)
XLA Modules:
  0.0 85.7 jit_solution(3317112889754856972)
XLA Ops:
  0.0 84.3 %sweep.1 = f32[3,3,16,4096]{3,2,1,0:T(8,128)S(1)} custom-call(f32[9,16,4096]{2,1,0:T(8,128)} %bitcast.3, f32[3,16,4096]{2,1,0:T(8,128)} %init_hbm.1, f32[16,4096]{1,0:T(8,128)} %depth_hbm.1), custom_call_target="tpu_custom_call" | custom-call | tf_op jit(solution)/shard_map/sweep/pallas_call | solution.py:786
  84.3 1.4 %copy.5 = f32[1,3,3,16,4096]{4,3,2,1,0:T(8,128)} copy(f32[1,3,3,16,4096]{4,3,2,1,0:T(8,128)S(1)} %bitcast.2) | data formatting | bytes 4718592

commit v12 on v11

--- a/solution.py
+++ b/solution.py
@@ -460,23 +460,21 @@
             one_copy(f, lax.rem(s + d, SPACE), True).start()
     rt[:, rows(ROWS * s), :] = esum[:, :, block(s, k)]
 
-    def depth_pieces(base):
-        return (
-            (pl.ds(pl.multiple_of(base, 128), PART), pl.ds(128, PART)),
-            (pl.ds(pl.multiple_of(lax.rem(base + COLS - 128, COLS), 128), 128), pl.ds(0, 128)),
-            (pl.ds(pl.multiple_of(lax.rem(base + PART, COLS), 128), 128), pl.ds(384, 128)),
-        )
+    def depth_pieces(sp):
+        i = owned(sp, tm)
+        tile = 4 * sp + 2 * (i // 16) + lax.rem(i, 16) // 8 + jnp.where(lax.rem(i, 8) == 0, -1, 0)
+        return [(pl.ds(pl.multiple_of(lax.rem(tile + 32 + n, 32) * 128, 128), 128), pl.ds(128 * n, 128)) for n in range(2)]
 
     def depth_copy(d, n, send):
         sp = lax.rem(s + d, SPACE) if send else lax.rem(s + SPACE - d, SPACE)
         to = sp if send else s
-        src, dst = depth_pieces(512 * to + 256 * (owned(to, tm) // 16))[n]
+        src, dst = depth_pieces(to)[n]
         return copy(depth.at[:, src], dr.at[rows(ROWS * (s if send else sp)), dst], dep_s.at[n, d], dep_r.at[n, d], at(tm, sp))
 
     for d in range(1, SPACE):
-        for n in range(3):
+        for n in range(2):
             depth_copy(d, n, True).start()
-    for src, dst in depth_pieces(512 * s + 256 * half):
+    for src, dst in depth_pieces(s):
         dr[rows(ROWS * s), dst] = depth[:, src]
 
 
@@ -518,7 +516,7 @@
                 for n in range(2):
                     act(halo_copy(n, j, width))
 
-    for c in (0, 1, 2, 3, 5, 6, 4, 7, 9, 10, 11, 8, 13, 14, 12):
+    for c in (0, 1, 2, 3, 4, 5, 6, 7, 8, 9, 10, 11, 12, 13, 14):
         @pl.when((chip != c) | (half != k))
         def _(c=c):
             for f in range(3):
@@ -531,15 +529,15 @@
                     halo_copy(n, c, width).start()
 
     for d in range(1, SPACE):
-        for n in range(3):
+        for n in range(2):
             depth_copy(d, n, False).wait_recv()
-    for t in range(4):
+    for t in range(2):
         dt[128 * t : 128 * t + 128, :] = dr[:, 128 * t : 128 * t + 128].T
 
 
     def scanned(lo, hi, halo, state, send):
         count = OWN + 2 * halo
-        d_own = dt[rows(128 - halo + OWN * spot, count), :]
+        d_own = dt[rows(jnp.where(lax.rem(spot, 8) == 0, 128, OWN * lax.rem(spot, 8)) - halo, count), :]
 
         def stepped(state):
             h, u, v = state
@@ -676,7 +674,7 @@
     for i in range(COLS // CHUNK):
         item_copy(i).wait_send()
     for d in range(1, SPACE):
-        for n in range(3):
+        for n in range(2):
             depth_copy(d, n, True).wait_send()
         for f in range(3):
             one_copy(f, lax.rem(s + d, SPACE), True).wait_send()
@@ -793,7 +791,7 @@
             flat, flat, flat, vm(2, 8, FOLD), vm(2, 8, FOLD), vm(2, 8, FOLD), vm(2, 8, FOLD),
             ringed, ringed, flat, ringed, vm(2, 8, FOLD), vm(2, 8, FOLD), ringed, vm(4, 8, FOLD), vm(4, 8, FOLD),
             ringed, flat, flat, vm(2, 3, ROWS, COLS // 8), vm(2, 3, ROWS, COLS // 8), vm(2, 3, ROWS, COLS // 8),
-            vm(3, 128, PART), vm(3, PART, 128), vm(128, 512), vm(512, 128),
+            vm(3, 128, PART), vm(3, PART, 128), vm(128, 256), vm(256, 128),
             vm(CHIPS, 3, WIDE, 128), vm(CHIPS, 3, OWN, 128), vm(2, 3, OWN, 128), vm(3, PART, 128), vm(2, SPACE, 56, 128), vm(SPACE, 8, 128),
             pltpu.SemaphoreType.DMA((5,)), *sems(8), *sems(8), *sems(4, 4), *sems(2, 4), *sems(4, 4), *sems(8), *sems(1), *sems(3, 8), *sems(3, 8), *sems(3, 16),
             *sems(2, 16), *sems(16), *sems(3, 8), *sems(2, 8),

time: 87.4 us -> 86.4 us (0.989); the launches traced: 85.7 us -> 85.7 us
  no operation moved by 1% of the time
where the time goes in v12:
time: 86.4 us; the launch traced here: 85.7 us
  Pallas kernels  84.3 us (98%)
  local copies, waits for them, and re-layouts  1.41 us (2%)
    pallas_call x1, Pallas kernels, per_device(): pl.pallas_call(coarse_kernel, out_shape=jax.ShapeDtypeStruct((3, 3, ROWS,...  84.3 us

profile of v12, /device:TPU:231, one launch (start us, length us, event | category | flops | bytes accessed | tf_op | source)
XLA Modules:
  0.0 85.7 jit_solution(3778934358008457586)
XLA Ops:
  0.0 84.3 %sweep.1 = f32[3,3,16,4096]{3,2,1,0:T(8,128)S(1)} custom-call(f32[9,16,4096]{2,1,0:T(8,128)} %bitcast.3, f32[3,16,4096]{2,1,0:T(8,128)} %init_hbm.1, f32[16,4096]{1,0:T(8,128)} %depth_hbm.1), custom_call_target="tpu_custom_call" | custom-call | tf_op jit(solution)/shard_map/sweep/pallas_call | solution.py:784
  84.3 1.4 %copy.5 = f32[1,3,3,16,4096]{4,3,2,1,0:T(8,128)} copy(f32[1,3,3,16,4096]{4,3,2,1,0:T(8,128)S(1)} %bitcast.2) | data formatting | bytes 4718592
